TPU v7x, 8 devices: a whole 2x2x1 slice. The times are simulated.
8 devices in a mesh: col: 2 (over z, y), row: 4 (over x, core).
Axes of the slice: x: 2, y: 2, z: 1, core: 2. Of those that a mesh axis runs over, the one named last changes fastest.
Arguments:
- vel_u: float32 [41, 192, 1024], P(None, 'row', 'col')
- vel_v: float32 [41, 192, 1024], P(None, 'row', 'col')
- temperature: float32 [41, 192, 1024], P(None, 'row', 'col')
- salinity: float32 [41, 192, 1024], P(None, 'row', 'col')
- surf_eta: float32 [192, 1024], P('row', 'col')
- trans_u: float32 [192, 1024], P('row', 'col')
- trans_v: float32 [192, 1024], P('row', 'col')
- bottom_depth: float32 [192, 1024], P('row', 'col')
- level_count: int32 [192, 1024], P('row', 'col')
- avg_weights: float32 [30], replicated
Outputs:
- output 1: float32 [192, 1024], P('row', 'col')
- output 2: float32 [192, 1024], P('row', 'col')
- output 3: float32 [192, 1024], P('row', 'col')
- output 4: float32 [41, 192, 1024], P(None, 'row', 'col')
- output 5: float32 [41, 192, 1024], P(None, 'row', 'col')
- output 6: float32 [41, 192, 1024], P(None, 'row', 'col')
- output 7: float32 [41, 192, 1024], P(None, 'row', 'col')
All inputs are finite; a program needn't handle non-finite values.
Results may differ from a plain program's by a relative error of at most 0.001.
Values sent between devices are 32-bit elements.
A program may use at most 1 GiB of HBM per device.

v0:
```python
import jax
import jax.numpy as jnp
from jax import lax
from jax.sharding import PartitionSpec as P

TIME_STEP = 1.0
GRAVITY = 16.0
BC_GRAVITY = 4.0
EXPAND_T = 0.2
CONTRACT_S = 0.6
CORIO_F0 = 0.4
CORIO_BETA = 0.4
VISC_R = 2.0
DIFF_R = 0.5


def shifted(padded, step_y, step_x):
    n_rows = padded.shape[-2] - 2
    n_cols = padded.shape[-1] - 2
    return padded[..., 1 + step_y:1 + step_y + n_rows, 1 + step_x:1 + step_x + n_cols]


def tri_solve(right_side, active, strength):
    link = strength * active[1:]
    zero_row = jnp.zeros_like(right_side[:1])
    low_links = jnp.concatenate([zero_row, link], axis=0)
    up_links = jnp.concatenate([link, zero_row], axis=0)

    def down(carry, level):
        ratio_prev, value_prev = carry
        low_link, up_link, target = level
        denominator = 1.0 + low_link + up_link + low_link * ratio_prev
        ratio = -up_link / denominator
        value = (target + low_link * value_prev) / denominator
        return (ratio, value), (ratio, value)

    start = (jnp.zeros_like(right_side[0]), jnp.zeros_like(right_side[0]))
    _, (ratios, values) = lax.scan(down, start, (low_links, up_links, right_side))

    def back(below, level):
        ratio, value = level
        solved = value - ratio * below
        return solved, solved

    _, solved_all = lax.scan(back, jnp.zeros_like(right_side[0]), (ratios, values), reverse=True)
    return solved_all


def ocean_columns(u_pad, v_pad, array_b15, salinity_pad, count_pad, depth_pad, coriolis_u, coriolis_v):
    n_levels = u_pad.shape[0]
    count_mid = shifted(count_pad, 0, 0)
    levels_u = jnp.minimum(count_mid, shifted(count_pad, 0, 1))
    levels_uw = jnp.minimum(shifted(count_pad, 0, -1), count_mid)
    levels_v = jnp.minimum(count_mid, shifted(count_pad, 1, 0))
    levels_vs = jnp.minimum(shifted(count_pad, -1, 0), count_mid)
    level_index = jnp.arange(n_levels)[:, None, None]
    mask_mid = (level_index < count_mid).astype(jnp.float32)
    mask_u = (level_index < levels_u).astype(jnp.float32)
    mask_uw = (level_index < levels_uw).astype(jnp.float32)
    mask_v = (level_index < levels_v).astype(jnp.float32)
    mask_vs = (level_index < levels_vs).astype(jnp.float32)
    u_mid = shifted(u_pad, 0, 0)
    v_mid = shifted(v_pad, 0, 0)
    u_west = shifted(u_pad, 0, -1)
    v_south = shifted(v_pad, -1, 0)
    v_at_u = 0.25 * (v_mid + shifted(v_pad, 0, 1) + v_south + shifted(v_pad, -1, 1))
    u_at_v = 0.25 * (u_mid + u_west + shifted(u_pad, 1, 0) + shifted(u_pad, 1, -1))
    inertia_u = 0.5 * (u_mid * (shifted(u_pad, 0, 1) - u_west) + v_at_u * (shifted(u_pad, 1, 0) - shifted(u_pad, -1, 0)))
    inertia_v = 0.5 * (u_at_v * (shifted(v_pad, 0, 1) - shifted(v_pad, 0, -1)) + v_mid * (shifted(v_pad, 1, 0) - v_south))
    density = CONTRACT_S * salinity_pad - EXPAND_T * array_b15
    pressure = (BC_GRAVITY / n_levels) * (jnp.cumsum(density, axis=0) - 0.5 * density)
    pressure_mid = shifted(pressure, 0, 0)
    u_star = u_mid + TIME_STEP * (coriolis_u * v_at_u - inertia_u - shifted(pressure, 0, 1) + pressure_mid)
    v_star = v_mid + TIME_STEP * (-coriolis_v * u_at_v - inertia_v - shifted(pressure, 1, 0) + pressure_mid)
    u_visc = tri_solve(u_star, mask_u, VISC_R)
    v_visc = tri_solve(v_star, mask_v, VISC_R)
    count_u = jnp.maximum(jnp.sum(mask_u, axis=0), 1.0)
    count_v = jnp.maximum(jnp.sum(mask_v, axis=0), 1.0)
    depth_mid = shifted(depth_pad, 0, 0)
    depth_u = 0.5 * (depth_mid + shifted(depth_pad, 0, 1))
    depth_v = 0.5 * (depth_mid + shifted(depth_pad, 1, 0))
    force_u = depth_u * jnp.sum(mask_u * (u_visc - u_mid), axis=0) / count_u / TIME_STEP
    force_v = depth_v * jnp.sum(mask_v * (v_visc - v_mid), axis=0) / count_v / TIME_STEP
    shear_u = u_visc - jnp.sum(mask_u * u_visc, axis=0) / count_u
    shear_v = v_visc - jnp.sum(mask_v * v_visc, axis=0) / count_v
    wet_u = (levels_u > 0).astype(jnp.float32)
    wet_v = (levels_v > 0).astype(jnp.float32)

    def advect(tracer_pad):
        tracer_mid = shifted(tracer_pad, 0, 0)
        flux_east = mask_u * u_mid * (tracer_mid + shifted(tracer_pad, 0, 1))
        flux_west = mask_uw * u_west * (shifted(tracer_pad, 0, -1) + tracer_mid)
        flux_north = mask_v * v_mid * (tracer_mid + shifted(tracer_pad, 1, 0))
        flux_south = mask_vs * v_south * (shifted(tracer_pad, -1, 0) + tracer_mid)
        return tracer_mid - 0.5 * TIME_STEP * (flux_east - flux_west + flux_north - flux_south)

    value_a15 = tri_solve(advect(array_b15), mask_mid, DIFF_R)
    salinity_new = tri_solve(advect(salinity_pad), mask_mid, DIFF_R)
    return (shear_u, shear_v, mask_u, mask_v, depth_u, depth_v, wet_u, wet_v, force_u, force_v, value_a15, salinity_new)


def fast_update(stack_pad, force_u, force_v, depth_u, depth_v, wet_u, wet_v, coriolis_u, coriolis_v, dt_fast):
    eta_pad = stack_pad[0]
    trans_u_pad = stack_pad[1]
    trans_v_pad = stack_pad[2]
    eta_ext = eta_pad[1:, 1:] - dt_fast * (trans_u_pad[1:, 1:] - trans_u_pad[1:, :-1] + trans_v_pad[1:, 1:] - trans_v_pad[:-1, 1:])
    eta_new = eta_ext[:-1, :-1]
    trans_u_old = shifted(trans_u_pad, 0, 0)
    trans_v_old = shifted(trans_v_pad, 0, 0)
    v_at_u = 0.25 * (trans_v_old + shifted(trans_v_pad, 0, 1) + shifted(trans_v_pad, -1, 0) + shifted(trans_v_pad, -1, 1))
    u_at_v = 0.25 * (trans_u_old + shifted(trans_u_pad, 0, -1) + shifted(trans_u_pad, 1, 0) + shifted(trans_u_pad, 1, -1))
    trans_u_new = wet_u * (trans_u_old + dt_fast * (coriolis_u * v_at_u + force_u - GRAVITY * depth_u * (eta_ext[:-1, 1:] - eta_new)))
    trans_v_new = wet_v * (trans_v_old + dt_fast * (force_v - coriolis_v * u_at_v - GRAVITY * depth_v * (eta_ext[1:, :-1] - eta_new)))
    return eta_new, trans_u_new, trans_v_new


def solution(mesh):
    n_col = mesh.shape['col']
    n_row = mesh.shape['row']
    east_moves = [(index, (index + 1) % n_col) for index in range(n_col)]
    west_moves = [(index, (index - 1) % n_col) for index in range(n_col)]
    north_moves = [(index, index + 1) for index in range(n_row - 1)]
    south_moves = [(index + 1, index) for index in range(n_row - 1)]

    def exchange(field):
        from_west = lax.ppermute(field[..., -1:], 'col', east_moves)
        from_east = lax.ppermute(field[..., :1], 'col', west_moves)
        wide = jnp.concatenate([from_west, field, from_east], axis=-1)
        from_south = lax.ppermute(wide[..., -1:, :], 'row', north_moves)
        from_north = lax.ppermute(wide[..., :1, :], 'row', south_moves)
        return jnp.concatenate([from_south, wide, from_north], axis=-2)

    def step(vel_u, vel_v, value_a11, salinity, surf_eta, trans_u, trans_v, bottom_depth, level_count, avg_weights):
        n_rows = surf_eta.shape[0]
        total_rows = n_rows * n_row
        dt_fast = TIME_STEP / avg_weights.shape[0]
        row_pos = (lax.axis_index('row') * n_rows + jnp.arange(n_rows)).astype(jnp.float32)[:, None]
        coriolis_u = CORIO_F0 + CORIO_BETA * ((row_pos + 0.5) / total_rows - 0.5)
        coriolis_v = CORIO_F0 + CORIO_BETA * ((row_pos + 1.0) / total_rows - 0.5)
        columns = ocean_columns(exchange(vel_u), exchange(vel_v), exchange(value_a11), exchange(salinity), exchange(level_count), exchange(bottom_depth), coriolis_u, coriolis_v)
        shear_u, shear_v, mask_u, mask_v, depth_u, depth_v, wet_u, wet_v, force_u, force_v, value_a15, salinity_new = columns

        def subcycle(carry, weight):
            eta_old, trans_u_old, trans_v_old, acc_u, acc_v = carry
            stack_pad = exchange(jnp.stack([eta_old, trans_u_old, trans_v_old]))
            eta_new, trans_u_new, trans_v_new = fast_update(stack_pad, force_u, force_v, depth_u, depth_v, wet_u, wet_v, coriolis_u, coriolis_v, dt_fast)
            return (eta_new, trans_u_new, trans_v_new, acc_u + weight * trans_u_new, acc_v + weight * trans_v_new), None

        zero_field = jnp.zeros_like(surf_eta)
        final, _ = lax.scan(subcycle, (surf_eta, trans_u, trans_v, zero_field, zero_field), avg_weights)
        eta_fin, trans_u_fin, trans_v_fin, bar_u, bar_v = final
        vel_u_new = mask_u * (shear_u + bar_u / depth_u)
        vel_v_new = mask_v * (shear_v + bar_v / depth_v)
        return (eta_fin, trans_u_fin, trans_v_fin, vel_u_new, vel_v_new, value_a15, salinity_new)

    cube = P(None, 'row', 'col')
    flat = P('row', 'col')
    return jax.shard_map(step, mesh=mesh, in_specs=(cube, cube, cube, cube, flat, flat, flat, flat, flat, P()), out_specs=(flat, flat, flat, cube, cube, cube, cube), check_vma=False)
```

profile of v0, /device:TPU:0, one launch (start us, length us, event | category | flops | bytes accessed | tf_op | source)
XLA Modules:
  0.0 1294.0 jit_solution(14957807125057059685)
XLA Ops:
  1.5 3.4 collective-permute-start.23
  17.6 8.4 fusion.130
  36.6 3.0 collective-permute-start.26
  42.0 4.3 fusion.132
  47.4 4.4 fusion.131
  55.7 2.9 pad_maximum_fusion.36
  62.2 2.6 pad_maximum_fusion.43
  67.2 3.7 collective-permute-start.8
  73.0 2.8 pad_maximum_fusion.40
  75.8 3.3 collective-permute-start.15
  83.6 2.9 pad_maximum_fusion.46
  86.5 4.2 collective-permute-start.19
  90.7 3.8 maximum_maximum_fusion
  97.2 12.0 fusion.47
  114.1 71.8 %while.163 = (s32[]{:T(128)}, f32[48,512]{1,0:T(8,128)S(1)}, f32[48,512]{1,0:T(8,128)S(1)}, f32[41,48,512]{2,1,0:T(8,128)}, f32[41,48,512]{2,1,0:T(8,128)}, /*in...) while((s32[]{:T(128)}, f32[48,512]{1,0:T(8,128)S(1)}, ...), condition=%wide.region_22.23_spmd.clone, body=%wide.region_21.22_spmd.clone.sunk | while | flops 270339 | bytes 885359 | solution.py:38
  188.4 67.9 %while.164 = (s32[]{:T(128)}, f32[48,512]{1,0:T(8,128)S(1)}, f32[41,48,512]{2,1,0:T(8,128)}, f32[41,48,512]{2,1,0:T(8,128)}, f32[41,48,512]{2,1,0:T(8,128)}, /*index=5*/s32[]{:T(128)}, s32[]{:T(128)}, s32[]{:T(128)}) while((s32[]{:T(128)}, f32[48,512]{1,0:T(8,128)S(1)}, f32[41,48,512]{2,1,0:T(8,128)}, ...), condition=%wide.region_24.25_spmd.clone, body=%wide.region_23.24_spmd.clone.sunk | while | flops 73732 | bytes 491631 | solution.py:45
  256.3 4.3 collective-permute-start.12
  261.9 19.7 %fusion.60 = f32[41,48,512]{2,1,0:T(8,128)} fusion(f32[41,48,512]{2,1,0:T(8,128)} %param.30, f32[41,1,514]{2,1,0:T(1,128)} %collective-permute-done.19, f32[41,48,1]{2,1,0:T(8,128)} %copy.35, f32[41,48,1]{2,1,0:T(8,128)} %copy-done.11, f32[41,1,514]{2,1,0:T(1,128)} %collective-permute-done.20, f32[41,48,512]{2,1,0:T(8,128)} %param.28, ...), kind=kLoop, calls=%fused_computation.136 | loop fusion | flops 30228480 | bytes 20737744 | tf_op jit(solution)/shard_map/sub | solution.py:95
  286.5 71.8 %while.161 = (s32[]{:T(128)}, f32[48,512]{1,0:T(8,128)S(1)}, f32[48,512]{1,0:T(8,128)S(1)}, f32[41,48,512]{2,1,0:T(8,128)}, f32[41,48,512]{2,1,0:T(8,128)}, /*in...) while((s32[]{:T(128)}, f32[48,512]{1,0:T(8,128)S(1)}, ...), condition=%wide.region_18.19_spmd.clone, body=%wide.region_17.18_spmd.clone.sunk | while | flops 270339 | bytes 885359 | solution.py:38
  360.8 67.9 %while.162 = (s32[]{:T(128)}, f32[48,512]{1,0:T(8,128)S(1)}, f32[41,48,512]{2,1,0:T(8,128)}, f32[41,48,512]{2,1,0:T(8,128)}, f32[41,48,512]{2,1,0:T(8,128)}, /*index=5*/s32[]{:T(128)}, s32[]{:T(128)}, s32[]{:T(128)}) while((s32[]{:T(128)}, f32[48,512]{1,0:T(8,128)S(1)}, f32[41,48,512]{2,1,0:T(8,128)}, ...), condition=%wide.region_20.21_spmd.clone, body=%wide.region_19.20_spmd.clone.sunk | while | flops 73732 | bytes 491631 | solution.py:45
  428.6 72.7 %subtract_multiply_fusion = f32[41,50,514]{2,1,0:T(8,128)} fusion(f32[41,1,514]{2,1,0:T(1,128)} %collective-permute-done.20, f32[41,48,1]{2,1,0:T(8,128)} %copy.35, f32[41,48,512]{2,1,0:T(8,128)} %param.30, f32[41,48,1]{2,1,0:T(8,128)} %copy-done.11, f32[41,1,514]{2,1,0:T(1,128)} %collective-permute-done.19, f32[41,1,514]{2,1,0:T(1,128)} %collective-permute-done.16, ...), kind=kOutput, calls=%fused_computation.109 | output fusion | flops 68490496 | bytes 12644400 | tf_op jit(solution)/shard_map/jit(cumsum)/reduce_window_sum | solution.py:71
  501.4 6.8 pad_maximum_fusion.9
  508.2 16.6 %fusion.79 = f32[41,48,512]{2,1,0:T(8,128)} fusion(f32[41,48,512]{2,1,0:T(8,128)S(1)} %copy-done.1, f32[41,50,514]{2,1,0:T(8,128)} %subtract_multiply_fusion, f32[41,1,514]{2,1,0:T(1,128)} %collective-permute-done.12, f32[41,48,1]{2,1,0:T(8,128)S(1)} %copy-done.22, f32[41,48,1]{2,1,0:T(8,128)S(1)} %copy.25, f32[41,49,514]{2,1,0:T(8,128)} %copy-done.6, ...), kind=kLoop, calls=%fused_computation.169 | loop fusion | flops 21159936 | bytes 32351816 | tf_op jit(solution)/shard_map/add | solution.py:73
  529.7 71.8 %while.157 = (s32[]{:T(128)}, f32[48,512]{1,0:T(8,128)S(1)}, f32[48,512]{1,0:T(8,128)S(1)}, f32[41,48,512]{2,1,0:T(8,128)}, f32[41,48,512]{2,1,0:T(8,128)}, /*in...) while((s32[]{:T(128)}, f32[48,512]{1,0:T(8,128)S(1)}, ...), condition=%wide.region_2.3_spmd.clone, body=%wide.region_1.2_spmd.clone.sunk | while | flops 270339 | bytes 885359 | solution.py:38
  601.5 2.5 broadcast.274.clone.3
  604.0 67.9 %while.158 = (s32[]{:T(128)}, f32[48,512]{1,0:T(8,128)S(1)}, f32[41,48,512]{2,1,0:T(8,128)}, f32[41,48,512]{2,1,0:T(8,128)}, f32[41,48,512]{2,1,0:T(8,128)}, /*index=5*/s32[]{:T(128)}, s32[]{:T(128)}, s32[]{:T(128)}) while((s32[]{:T(128)}, f32[48,512]{1,0:T(8,128)S(1)}, f32[41,48,512]{2,1,0:T(8,128)}, f32[41,48,512]{2,1,0:T(8,128)}, ...), condition=%wide.region_4.5_spmd.clone, body=%wide.region_3.4_spmd.clone.sunk | while | flops 73732 | bytes 491631 | solution.py:45
  671.9 5.4 select_reduce_fusion.1
  677.7 15.7 %fusion.70 = f32[41,48,512]{2,1,0:T(8,128)} fusion(f32[41,48,512]{2,1,0:T(8,128)S(1)} %copy-done.5, f32[41,50,514]{2,1,0:T(8,128)} %subtract_multiply_fusion, f32[41,1,514]{2,1,0:T(1,128)} %collective-permute-done.25, f32[41,48,1]{2,1,0:T(8,128)S(1)} %copy-done.14, f32[41,48,1]{2,1,0:T(8,128)S(1)} %copy-done.21, f32[41,49,514]{2,1,0:T(8,128)} %pad_maximum_fusion.9, ...), kind=kLoop, calls=%fused_computation.154 | loop fusion | flops 21159936 | bytes 32351816 | tf_op jit(solution)/shard_map/add | solution.py:74
  695.9 2.5 broadcast.274.clone.2
  698.4 72.0 %while.159 = (s32[]{:T(128)}, f32[48,512]{1,0:T(8,128)S(1)}, f32[48,512]{1,0:T(8,128)S(1)}, f32[41,48,512]{2,1,0:T(8,128)}, f32[41,48,512]{2,1,0:T(8,128)}, /*in...) while((s32[]{:T(128)}, f32[48,512]{1,0:T(8,128)S(1)}, ...), condition=%wide.region_8.9_spmd.clone, body=%wide.region_7.8_spmd.clone.sunk | while | flops 270339 | bytes 885359 | solution.py:38
  772.9 67.9 %while.160 = (s32[]{:T(128)}, f32[48,512]{1,0:T(8,128)S(1)}, f32[41,48,512]{2,1,0:T(8,128)}, f32[41,48,512]{2,1,0:T(8,128)}, f32[41,48,512]{2,1,0:T(8,128)}, /*index=5*/s32[]{:T(128)}, s32[]{:T(128)}, s32[]{:T(128)}) while((s32[]{:T(128)}, f32[48,512]{1,0:T(8,128)S(1)}, f32[41,48,512]{2,1,0:T(8,128)}, f32[41,48,512]{2,1,0:T(8,128)}, ...), condition=%wide.region_10.11_spmd.clone, body=%wide.region_9.10_spmd.clone.sunk | while | flops 73732 | bytes 491631 | solution.py:45
  840.9 4.6 select_reduce_fusion
  845.8 439.0 %while.165 = (s32[]{:T(128)}, f32[48,512]{1,0:T(8,128)S(1)}, f32[48,512]{1,0:T(8,128)S(1)}, f32[48,512]{1,0:T(8,128)S(1)}, f32[48,512]{1,0:T(8,128)S(1)}, /*inde...) while((s32[]{:T(128)}, f32[48,512]{1,0:T(8,128)S(1)}, ...), condition=%wide.region_14.15_spmd.clone.clone.clone, body=%wide.region_13.14_spmd.clone.clone.clone.sunk | while | flops 1339152 | bytes 5150624 | solution.py:150
  853.6 3.0 collective-permute-start.3
  867.0 4.0 collective-permute-start.3
  881.0 4.8 collective-permute-start.3
  895.6 4.8 collective-permute-start.3
  910.3 4.8 collective-permute-start.3
  925.0 4.8 collective-permute-start.3
  939.7 4.8 collective-permute-start.3
  954.3 4.8 collective-permute-start.3
  969.0 4.8 collective-permute-start.3
  983.6 4.8 collective-permute-start.3
  998.4 4.8 collective-permute-start.3
  1013.0 4.8 collective-permute-start.3
  1027.7 4.8 collective-permute-start.3
  1042.3 4.8 collective-permute-start.3
  1057.1 4.8 collective-permute-start.3
  1071.7 4.8 collective-permute-start.3
  1086.4 4.8 collective-permute-start.3
  1101.0 4.8 collective-permute-start.3
  1115.7 4.8 collective-permute-start.3
  1130.4 4.8 collective-permute-start.3
  1145.1 4.8 collective-permute-start.3
  1159.7 4.8 collective-permute-start.3
  1174.4 4.8 collective-permute-start.3
  1189.0 4.8 collective-permute-start.3
  1203.8 4.8 collective-permute-start.3
  1218.4 4.8 collective-permute-start.3
  1233.1 4.8 collective-permute-start.3
  1247.7 4.8 collective-permute-start.3
  1262.4 4.8 collective-permute-start.3
  1277.1 4.8 collective-permute-start.3
  1285.0 8.6 add_select_fusion
  (1024 shorter events, 927.8 us)
Async XLA Ops:
  1.5 29.9 %collective-permute-start.23 = (s32[48,1]{1,0:T(8,128)S(1)}, s32[48,1]{1,0:T(8,128)S(1)}, u32[]{:S(2)}, u32[]{:S(2)}) collective-permute-start(s32[48,1]{1,0:T(8,128)S(1)} %get-tuple-element.1216), channel_id=1, source_target_pairs={{0,4},{4,0},{1,5},{5,1},{2,6},{6,2},{3,7},{7,3}} | collective-permute-start | bytes 584 | tf_op jit(solution)/shard_map/ppermute | solution.py:126
  4.9 26.5 %collective-permute-start.5 = (s32[48,1]{1,0:T(8,128)S(1)}, s32[48,1]{1,0:T(8,128)S(1)}, u32[]{:S(2)}, u32[]{:S(2)}) collective-permute-start(s32[48,1]{1,0:T(8,128)S(1)} %get-tuple-element.1217), channel_id=1, source_target_pairs={{0,4},{4,0},{1,5},{5,1},{2,6},{6,2},{3,7},{7,3}} | collective-permute-start | bytes 584 | tf_op jit(solution)/shard_map/ppermute | solution.py:127
  7.1 47.4 %collective-permute-start.6 = (f32[41,48,1]{1,2,0:T(1,128)S(1)}, f32[41,48,1]{1,2,0:T(1,128)S(1)}, u32[]{:S(2)}, u32[]{:S(2)}) collective-permute-start(f32[41,48,1]{1,2,0:T(1,128)S(1)} %copy.41), channel_id=1, source_target_pairs={{0,4},{4,0},{1,5},{5,1},{2,6},{6,2},{3,7},{7,3}} | collective-permute-start | bytes 23624 | tf_op jit(solution)/shard_map/ppermute | solution.py:127
  9.5 45.7 %collective-permute-start.7 = (f32[41,48,1]{1,2,0:T(1,128)S(1)}, f32[41,48,1]{1,2,0:T(1,128)S(1)}, u32[]{:S(2)}, u32[]{:S(2)}) collective-permute-start(f32[41,48,1]{1,2,0:T(1,128)S(1)} %copy.42), channel_id=1, source_target_pairs={{0,4},{4,0},{1,5},{5,1},{2,6},{6,2},{3,7},{7,3}} | collective-permute-start | bytes 23624 | tf_op jit(solution)/shard_map/ppermute | solution.py:126
  29.4 31.0 %collective-permute-start.13 = (f32[41,48,1]{1,2,0:T(1,128)S(1)}, f32[41,48,1]{1,2,0:T(1,128)S(1)}, u32[]{:S(2)}, u32[]{:S(2)}) collective-permute-start(f32[41,48,1]{1,2,0:T(1,128)S(1)} %copy.45), channel_id=1, source_target_pairs={{0,4},{4,0},{1,5},{5,1},{2,6},{6,2},{3,7},{7,3}} | collective-permute-start | bytes 23624 | tf_op jit(solution)/shard_map/ppermute | solution.py:126
  36.6 15.4 %collective-permute-start.26 = (s32[1,514]{1,0:T(1,128)S(1)}, s32[1,514]{1,0:T(1,128)S(1)}, u32[]{:S(2)}, u32[]{:S(2)}) collective-permute-start(s32[1,514]{1,0:T(1,128)S(1)} %get-tuple-element.1204), channel_id=1, source_target_pairs={{0,1},{1,2},{2,3},{4,5},{5,6},{6,7}} | collective-permute-start | bytes 6176 | tf_op jit(solution)/shard_map/ppermute | solution.py:129
  51.8 9.3 collective-permute-start.14
  52.8 26.3 %collective-permute-start.10 = (f32[41,48,1]{1,2,0:T(1,128)}, f32[41,48,1]{1,2,0:T(1,128)}, u32[]{:S(2)}, u32[]{:S(2)}) collective-permute-start(f32[41,48,1]{1,2,0:T(1,128)} %copy.44), channel_id=1, source_target_pairs={{0,4},{4,0},{1,5},{5,1},{2,6},{6,2},{3,7},{7,3}} | collective-permute-start | bytes 23624 | tf_op jit(solution)/shard_map/ppermute | solution.py:126
  55.0 11.1 collective-permute-start.17
  58.6 12.3 collective-permute-start.18
  60.8 20.7 %collective-permute-start.9 = (f32[41,48,1]{1,2,0:T(1,128)}, f32[41,48,1]{1,2,0:T(1,128)}, u32[]{:S(2)}, u32[]{:S(2)}) collective-permute-start(f32[41,48,1]{1,2,0:T(1,128)} %copy.43), channel_id=1, source_target_pairs={{0,4},{4,0},{1,5},{5,1},{2,6},{6,2},{3,7},{7,3}} | collective-permute-start | bytes 23624 | tf_op jit(solution)/shard_map/ppermute | solution.py:127
  64.8 780.8 %collective-permute-start.22 = (f32[1,514]{1,0:T(1,128)S(1)}, f32[1,514]{1,0:T(1,128)S(1)}, u32[]{:S(2)}, u32[]{:S(2)}) collective-permute-start(f32[1,514]{1,0:T(1,128)S(1)} %pad_maximum_fusion.52), channel_id=1, source_target_pairs={{1,0},{2,1},{3,2},{5,4},{6,5},{7,6}} | collective-permute-start | bytes 6176 | tf_op jit(solution)/shard_map/ppermute | solution.py:130
  67.2 23.5 %collective-permute-start.8 = (f32[41,1,514]{2,1,0:T(1,128)}, f32[41,1,514]{2,1,0:T(1,128)}, u32[]{:S(2)}, u32[]{:S(2)}) collective-permute-start(f32[41,1,514]{2,1,0:T(1,128)} %get-tuple-element.1183), channel_id=1, source_target_pairs={{0,1},{1,2},{2,3},{4,5},{5,6},{6,7}} | collective-permute-start | bytes 252896 | tf_op jit(solution)/shard_map/ppermute | solution.py:129
  75.8 20.1 %collective-permute-start.15 = (f32[41,1,514]{2,1,0:T(1,128)}, f32[41,1,514]{2,1,0:T(1,128)}, u32[]{:S(2)}, u32[]{:S(2)}) collective-permute-start(f32[41,1,514]{2,1,0:T(1,128)} %get-tuple-element.1188), channel_id=1, source_target_pairs={{0,1},{1,2},{2,3},{4,5},{5,6},{6,7}} | collective-permute-start | bytes 252896 | tf_op jit(solution)/shard_map/ppermute | solution.py:129
  80.2 16.9 %collective-permute-start.16 = (f32[41,1,514]{2,1,0:T(1,128)}, f32[41,1,514]{2,1,0:T(1,128)}, u32[]{:S(2)}, u32[]{:S(2)}) collective-permute-start(f32[41,1,514]{2,1,0:T(1,128)} %get-tuple-element.1189), channel_id=1, source_target_pairs={{1,0},{2,1},{3,2},{5,4},{6,5},{7,6}} | collective-permute-start | bytes 252896 | tf_op jit(solution)/shard_map/ppermute | solution.py:130
  86.5 174.1 %collective-permute-start.19 = (f32[41,1,514]{2,1,0:T(1,128)}, f32[41,1,514]{2,1,0:T(1,128)}, u32[]{:S(2)}, u32[]{:S(2)}) collective-permute-start(f32[41,1,514]{2,1,0:T(1,128)} %get-tuple-element.1186), channel_id=1, source_target_pairs={{0,1},{1,2},{2,3},{4,5},{5,6},{6,7}} | collective-permute-start | bytes 252896 | tf_op jit(solution)/shard_map/ppermute | solution.py:129
  94.6 167.3 %collective-permute-start.20 = (f32[41,1,514]{2,1,0:T(1,128)}, f32[41,1,514]{2,1,0:T(1,128)}, u32[]{:S(2)}, u32[]{:S(2)}) collective-permute-start(f32[41,1,514]{2,1,0:T(1,128)} %get-tuple-element.1187), channel_id=1, source_target_pairs={{1,0},{2,1},{3,2},{5,4},{6,5},{7,6}} | collective-permute-start | bytes 252896 | tf_op jit(solution)/shard_map/ppermute | solution.py:130
  95.9 405.5 %collective-permute-start.11 = (f32[41,1,514]{2,1,0:T(1,128)}, f32[41,1,514]{2,1,0:T(1,128)}, u32[]{:S(2)}, u32[]{:S(2)}) collective-permute-start(f32[41,1,514]{2,1,0:T(1,128)} %get-tuple-element.1184), channel_id=1, source_target_pairs={{1,0},{2,1},{3,2},{5,4},{6,5},{7,6}} | collective-permute-start | bytes 252896 | tf_op jit(solution)/shard_map/ppermute | solution.py:130
  256.3 251.9 %collective-permute-start.12 = (f32[41,1,514]{2,1,0:T(1,128)}, f32[41,1,514]{2,1,0:T(1,128)}, u32[]{:S(2)}, u32[]{:S(2)}) collective-permute-start(f32[41,1,514]{2,1,0:T(1,128)} %get-tuple-element.1185), channel_id=1, source_target_pairs={{0,1},{1,2},{2,3},{4,5},{5,6},{6,7}} | collective-permute-start | bytes 252896 | tf_op jit(solution)/shard_map/ppermute | solution.py:129
  260.6 416.7 %collective-permute-start.25 = (f32[41,1,514]{2,1,0:T(1,128)}, f32[41,1,514]{2,1,0:T(1,128)}, u32[]{:S(2)}, u32[]{:S(2)}) collective-permute-start(f32[41,1,514]{2,1,0:T(1,128)} %get-tuple-element.1182), channel_id=1, source_target_pairs={{1,0},{2,1},{3,2},{5,4},{6,5},{7,6}} | collective-permute-start | bytes 252896 | tf_op jit(solution)/shard_map/ppermute | solution.py:130
  865.7 6.0 collective-permute-start.2
  879.7 6.7 collective-permute-start.2
  881.0 5.6 collective-permute-start.3
  894.3 6.7 collective-permute-start.2
  895.6 5.6 collective-permute-start.3
  909.0 6.7 collective-permute-start.2
  910.3 5.6 collective-permute-start.3
  923.7 6.7 collective-permute-start.2
  925.0 5.6 collective-permute-start.3
  938.4 6.7 collective-permute-start.2
  939.7 5.6 collective-permute-start.3
  953.0 6.7 collective-permute-start.2
  954.3 5.6 collective-permute-start.3
  967.7 6.7 collective-permute-start.2
  969.0 5.6 collective-permute-start.3
  982.3 6.7 collective-permute-start.2
  983.6 5.6 collective-permute-start.3
  997.1 6.7 collective-permute-start.2
  998.4 5.6 collective-permute-start.3
  1011.7 6.7 collective-permute-start.2
  1013.0 5.6 collective-permute-start.3
  1026.4 6.7 collective-permute-start.2
  1027.7 5.6 collective-permute-start.3
  1041.0 6.7 collective-permute-start.2
  1055.8 6.7 collective-permute-start.2
  1070.4 6.7 collective-permute-start.2
  1085.1 6.7 collective-permute-start.2
  1099.7 6.7 collective-permute-start.2
  1114.4 6.7 collective-permute-start.2
  1129.1 6.7 collective-permute-start.2
  1130.4 5.6 collective-permute-start.3
  1143.8 6.7 collective-permute-start.2
  1158.4 6.7 collective-permute-start.2
  1159.7 5.6 collective-permute-start.3
  1173.1 6.7 collective-permute-start.2
  1187.7 6.7 collective-permute-start.2
  1189.0 5.6 collective-permute-start.3
  1202.5 6.7 collective-permute-start.2
  1217.1 6.7 collective-permute-start.2
  1218.4 5.6 collective-permute-start.3
  1231.8 6.7 collective-permute-start.2
  1246.4 6.7 collective-permute-start.2
  1261.1 6.7 collective-permute-start.2
  1275.8 6.7 collective-permute-start.2
  (137 other events, 2204.9 us)
where the time goes:
time: 1320 us; the launch traced here: 1290 us
  other arithmetic  812 us (62%)
  starting transfers between devices  281 us (21%)
  waiting for transfers between devices  109 us (8%)
  local copies, waits for them, and re-layouts  87.7 us (7%)
    dynamic_update_slice x328, other arithmetic, tri_solve(): lax.scan(down, start, (low_links, up_links, right_side))  559 us
    ppermute x35, starting transfers between devices, exchange(): from_south = lax.ppermute(wide[..., -1:, :], 'row', north_moves)  159 us
    another operation x1, other arithmetic, ocean_columns(): jnp.cumsum(density, axis=0) - 0.5 * density  72.7 us
    ppermute x36, waiting for transfers between devices, exchange(): from_east = lax.ppermute(field[..., :1], 'col', west_moves)  69.8 us
    ppermute x36, starting transfers between devices, exchange(): from_north = lax.ppermute(wide[..., :1, :], 'row', south_moves)  46.5 us
    ppermute x36, starting transfers between devices, exchange(): from_east = lax.ppermute(field[..., :1], 'col', west_moves)  37.9 us
    ppermute x36, starting transfers between devices, exchange(): from_west = lax.ppermute(field[..., -1:], 'col', east_moves)  37.1 us
    ppermute x36, waiting for transfers between devices, exchange(): from_west = lax.ppermute(field[..., -1:], 'col', east_moves)  33.5 us
  transfers between devices with their start and end apart: 143, of which 91 were waited for; matrix products, arithmetic and copies ran while one was open for 63% of the time, Pallas kernels for 0%

commit v1 on v0

v1 whole, which is shorter than its diff:
```python
import functools

import jax
import jax.numpy as jnp
from jax import lax
from jax.experimental import pallas as pl
from jax.experimental.pallas import tpu as pltpu
from jax.sharding import PartitionSpec as P

TIME_STEP = 1.0
GRAVITY = 16.0
BC_GRAVITY = 4.0
EXPAND_T = 0.2
CONTRACT_S = 0.6
CORIO_F0 = 0.4
CORIO_BETA = 0.4
VISC_R = 2.0
DIFF_R = 0.5

LEV = 41
ROWS = 48
SUB = 8
COLS = 512
LANES = 128
STRIPS = COLS // LANES
TILES = ROWS // SUB
PITCH = 56
REACH = 32
EXT = ROWS + 2 * REACH
EXT_TILES = EXT // SUB
PAGE = EXT + 16
MESH = pl.DeviceIdType.MESH
F32 = jnp.float32
VMEM_LIMIT = 62 * 1024 * 1024


def tables(strength):
    inner, last, ratio = [], [], 0.0
    for level in range(LEV):
        low = strength if level else 0.0
        pivot = 1.0 + low + strength - low * ratio
        inner.append(pivot)
        last.append(1.0 + low - low * ratio)
        ratio = strength / pivot
    return inner, last


def lane_index():
    return lax.broadcasted_iota(jnp.int32, (SUB, LANES), 1)


def west_of(strips, edge, at_last):
    mixed = [jnp.where(at_last, edge if c == 0 else strips[c - 1], strips[c]) for c in range(len(strips))]
    return [pltpu.roll(x, 1, 1) for x in mixed]


def east_of(strips, edge, at_first):
    n = len(strips)
    mixed = [jnp.where(at_first, edge if c == n - 1 else strips[c + 1], strips[c]) for c in range(n)]
    return [pltpu.roll(x, LANES - 1, 1) for x in mixed]


def places(n_row):
    row = lax.axis_index('row')
    col = lax.axis_index('col')
    other = 1 - col
    has_north = row < n_row - 1
    has_south = row > 0
    return dict(
        row=row, has_north=has_north, has_south=has_south,
        side={'col': other, 'row': row},
        north={'col': col, 'row': row + 1}, south={'col': col, 'row': row - 1},
        north_side={'col': other, 'row': row + 1}, south_side={'col': other, 'row': row - 1})


def meet(at):
    barrier = pltpu.get_barrier_semaphore()
    pl.semaphore_signal(barrier, inc=1, device_id=at['side'], device_id_type=MESH)

    @pl.when(at['has_north'])
    def _():
        pl.semaphore_signal(barrier, inc=1, device_id=at['north'], device_id_type=MESH)
        pl.semaphore_signal(barrier, inc=1, device_id=at['north_side'], device_id_type=MESH)

    @pl.when(at['has_south'])
    def _():
        pl.semaphore_signal(barrier, inc=1, device_id=at['south'], device_id_type=MESH)
        pl.semaphore_signal(barrier, inc=1, device_id=at['south_side'], device_id_type=MESH)

    return barrier


def await_meet(barrier, at):
    pl.semaphore_wait(barrier, 1 + 2 * at['has_north'].astype(jnp.int32) + 2 * at['has_south'].astype(jnp.int32))


def remote(src, dst, send, recv, where):
    return pltpu.make_async_remote_copy(src_ref=src, dst_ref=dst, send_sem=send, recv_sem=recv, device_id=where, device_id_type=MESH)


def halo_kernel(n_row, u, v, t, s, eta, tu, tv, depth, count,
                north_rows, south_rows, side_cols, own_cols, counts, wide_north, wide_south, wide_side,
                edge, fold, zero, load_sem, zero_sem, send_sem, recv_sem):
    at = places(n_row)
    fields = (u, v, t, s)
    loads = []
    for f in range(4):
        for e in range(2):
            copy = pltpu.make_async_copy(fields[f].at[:, :, pl.ds(e * (COLS - LANES), LANES)], edge.at[f, e], load_sem.at[f, e])
            copy.start()
            loads.append(copy)
    barrier = meet(at)
    lane = lane_index()
    fast = (eta, tu, tv, depth)
    low_half = lax.broadcasted_iota(jnp.int32, (ROWS, LANES), 1) < LANES // 2
    for f in range(4):
        fold[f] = jnp.where(low_half, fast[f][:, :LANES], fast[f][:, COLS - LANES:])
    for c in range(STRIPS):
        counts[c, SUB:SUB + ROWS, :] = count[:, c * LANES:(c + 1) * LANES].astype(F32)

    @pl.when(jnp.logical_not(at['has_north']))
    def _():
        zero[...] = jnp.zeros_like(zero)
        counts[:, SUB + ROWS:, :] = jnp.zeros((STRIPS, SUB, LANES), F32)
        side_cols[:, SUB + ROWS:, :] = jnp.zeros((4, SUB, LANES), F32)
        wide_north[...] = jnp.zeros_like(wide_north)
        wide_side[:, REACH + ROWS:, :] = jnp.zeros((4, REACH, LANES), F32)
        for f in range(4):
            pltpu.make_async_copy(zero, north_rows.at[f], zero_sem.at[f]).start()

    @pl.when(jnp.logical_not(at['has_south']))
    def _():
        zero[...] = jnp.zeros_like(zero)
        counts[:, :SUB, :] = jnp.zeros((STRIPS, SUB, LANES), F32)
        side_cols[:, :SUB, :] = jnp.zeros((4, SUB, LANES), F32)
        wide_south[...] = jnp.zeros_like(wide_south)
        wide_side[:, :REACH, :] = jnp.zeros((4, REACH, LANES), F32)
        for f in range(4):
            pltpu.make_async_copy(zero, south_rows.at[f], zero_sem.at[f]).start()

    await_meet(barrier, at)
    slot = iter(range(64))
    go_north, go_south, go_side = [], [], []

    def send(bucket, src, dst, where):
        i = next(slot)
        bucket.append(remote(src, dst, send_sem.at[i], recv_sem.at[i], at[where]))

    for f in range(4):
        send(go_north, fields[f].at[:, pl.ds(ROWS - 1, 1), :], south_rows.at[f], 'north')
        send(go_south, fields[f].at[:, pl.ds(0, 1), :], north_rows.at[f], 'south')
    send(go_north, counts.at[:, pl.ds(ROWS, SUB), :], counts.at[:, pl.ds(0, SUB), :], 'north')
    send(go_south, counts.at[:, pl.ds(SUB, SUB), :], counts.at[:, pl.ds(SUB + ROWS, SUB), :], 'south')
    for f in range(4):
        send(go_north, fast[f].at[pl.ds(ROWS - REACH, REACH), :], wide_south.at[f], 'north')
        send(go_south, fast[f].at[pl.ds(0, REACH), :], wide_north.at[f], 'south')
    send(go_side, fold, wide_side.at[:, pl.ds(REACH, ROWS), :], 'side')
    send(go_north, fold.at[:, pl.ds(ROWS - REACH, REACH), :], wide_side.at[:, pl.ds(0, REACH), :], 'north_side')
    send(go_south, fold.at[:, pl.ds(0, REACH), :], wide_side.at[:, pl.ds(REACH + ROWS, REACH), :], 'south_side')

    @pl.when(at['has_north'])
    def _():
        for copy in go_north:
            copy.start()

    @pl.when(at['has_south'])
    def _():
        for copy in go_south:
            copy.start()

    for copy in go_side:
        copy.start()

    half = lane >> 1
    at_first = lane == 0
    for f in range(4):
        loads[2 * f].wait()
        loads[2 * f + 1].wait()

        def pack(tile, _):
            rows = pl.ds(pl.multiple_of(SUB * tile, SUB), SUB)
            packed = jnp.zeros((SUB, LANES), F32)
            for k in range(LEV + 1 if f == 0 else LEV):
                if k < LEV:
                    first, last = edge[f, 0, k, rows, :], edge[f, 1, k, rows, :]
                else:
                    shifted = pl.ds(pl.multiple_of(SUB * tile + SUB, SUB), SUB)
                    first, last = counts[0, shifted, :], counts[STRIPS - 1, shifted, :]
                both = pltpu.roll(jnp.where(at_first, first, last), 2 * k + 1, 1)
                packed = jnp.where(half == k, both, packed)
            own_cols[f, rows, :] = packed
            return 0

        lax.fori_loop(0, TILES, pack, 0)
        send(go_side, own_cols.at[f], side_cols.at[f, pl.ds(SUB, ROWS), :], 'side')
        go_side[-1].start()
    late_south, late_north = [], []
    send(late_south, own_cols.at[0, pl.ds(0, SUB), :], side_cols.at[0, pl.ds(SUB + ROWS, SUB), :], 'south_side')
    send(late_north, own_cols.at[1, pl.ds(ROWS - SUB, SUB), :], side_cols.at[1, pl.ds(0, SUB), :], 'north_side')

    @pl.when(at['has_north'])
    def _():
        late_north[0].start()

    @pl.when(at['has_south'])
    def _():
        late_south[0].start()

    for copy in go_side:
        copy.wait()

    @pl.when(at['has_north'])
    def _():
        for copy in go_north + late_north:
            copy.wait_send()
        for copy in go_south + late_south:
            copy.wait_recv()

    @pl.when(at['has_south'])
    def _():
        for copy in go_south + late_south:
            copy.wait_send()
        for copy in go_north + late_north:
            copy.wait_recv()

    @pl.when(jnp.logical_not(at['has_north']))
    def _():
        for f in range(4):
            pltpu.make_async_copy(zero, north_rows.at[f], zero_sem.at[f]).wait()

    @pl.when(jnp.logical_not(at['has_south']))
    def _():
        for f in range(4):
            pltpu.make_async_copy(zero, south_rows.at[f], zero_sem.at[f]).wait()


def force_kernel(n_row, force, wide_north, wide_south, wide_side, fold, send_sem, recv_sem):
    at = places(n_row)
    barrier = meet(at)
    low_half = lax.broadcasted_iota(jnp.int32, (ROWS, LANES), 1) < LANES // 2
    for f in range(2):
        fold[f] = jnp.where(low_half, force[f, :, :LANES], force[f, :, COLS - LANES:])

    @pl.when(jnp.logical_not(at['has_north']))
    def _():
        wide_north[...] = jnp.zeros_like(wide_north)
        wide_side[:, REACH + ROWS:, :] = jnp.zeros((2, REACH, LANES), F32)

    @pl.when(jnp.logical_not(at['has_south']))
    def _():
        wide_south[...] = jnp.zeros_like(wide_south)
        wide_side[:, :REACH, :] = jnp.zeros((2, REACH, LANES), F32)

    await_meet(barrier, at)

    def copy_of(i, src, dst, where):
        return remote(src, dst, send_sem.at[i], recv_sem.at[i], at[where])

    go_north = [copy_of(0, force.at[:, pl.ds(ROWS - REACH, REACH), :], wide_south, 'north'),
                copy_of(1, fold.at[:, pl.ds(ROWS - REACH, REACH), :], wide_side.at[:, pl.ds(0, REACH), :], 'north_side')]
    go_south = [copy_of(2, force.at[:, pl.ds(0, REACH), :], wide_north, 'south'),
                copy_of(3, fold.at[:, pl.ds(0, REACH), :], wide_side.at[:, pl.ds(REACH + ROWS, REACH), :], 'south_side')]
    go_side = copy_of(4, fold, wide_side.at[:, pl.ds(REACH, ROWS), :], 'side')

    @pl.when(at['has_north'])
    def _():
        for copy in go_north:
            copy.start()

    @pl.when(at['has_south'])
    def _():
        for copy in go_south:
            copy.start()

    go_side.start()
    go_side.wait()

    @pl.when(at['has_north'])
    def _():
        for copy in go_north:
            copy.wait_send()
        for copy in go_south:
            copy.wait_recv()

    @pl.when(at['has_south'])
    def _():
        for copy in go_south:
            copy.wait_send()
        for copy in go_north:
            copy.wait_recv()


def strip_copies(tile, fields, strips, sem):
    rows = pl.ds(pl.multiple_of(SUB * tile, SUB), SUB)
    return [pltpu.make_async_copy(fields[f].at[:, rows, pl.ds(LANES * c, LANES)], strips[f].at[c, pl.ds(1, LEV), rows, :], sem.at[tile, f, c])
            for f in range(len(fields)) for c in range(STRIPS)]


def border_copies(north_rows, south_rows, strips, sem):
    copies = []
    for f in range(len(strips)):
        for c in range(STRIPS):
            lanes = pl.ds(LANES * c, LANES)
            copies.append(pltpu.make_async_copy(north_rows.at[f, :, :, lanes], strips[f].at[c, pl.ds(1, LEV), pl.ds(ROWS, 1), :], sem.at[0, f, c]))
            copies.append(pltpu.make_async_copy(south_rows.at[f, :, :, lanes], strips[f].at[c, pl.ds(0, LEV), pl.ds(PITCH - 1, 1), :], sem.at[1, f, c]))
    return copies


def level_rows(tile, c, k, offset=0):
    return pl.ds(SUB * tile + (c * (LEV + 1) * PITCH + PITCH * (k + 1) + offset), SUB)


def face_counts(counts_flat, side_cols, tile, at_first):
    rows = SUB * tile + SUB
    mid = [counts_flat[pl.ds(rows + c * 64, SUB), :] for c in range(STRIPS)]
    north = [counts_flat[pl.ds(rows + c * 64 + 1, SUB), :] for c in range(STRIPS)]
    edge = pltpu.roll(side_cols[0, pl.ds(rows, SUB), :], LANES - 1 - 2 * LEV, 1)
    east = east_of(mid, edge, at_first)
    return mid, [jnp.minimum(a, b) for a, b in zip(mid, east)], [jnp.minimum(a, b) for a, b in zip(mid, north)]


def momentum_kernel(n_row, u, v, t, s, north_rows, south_rows, side_cols, counts,
                    wu_out, wv_out, force, level_mean,
                    u_s, v_s, t_s, s_s, p_s, b_s, wu, wv, load_sem, border_sem, store_sem):
    row = lax.axis_index('row')
    fields, strips = (u, v, t, s), (u_s, v_s, t_s, s_s)
    borders = border_copies(north_rows, south_rows, strips, border_sem)
    for copy in strip_copies(TILES - 1, fields, strips, load_sem):
        copy.start()
    for copy in borders:
        copy.start()
    for tile in range(TILES - 2, -1, -1):
        for copy in strip_copies(tile, fields, strips, load_sem):
            copy.start()
    for copy in strip_copies(TILES - 1, fields, strips, load_sem):
        copy.wait()
    for copy in borders:
        copy.wait()
    lane = lane_index()
    at_first, at_last = lane == 0, lane == LANES - 1
    rows_total = (LEV + 1) * PITCH * STRIPS
    uf, vf, tf, sf, pf, bf = [ref.reshape(rows_total, LANES) for ref in (u_s, v_s, t_s, s_s, p_s, b_s)]
    counts_flat = counts.reshape(STRIPS * 64, LANES)
    half_scale = 0.5 * BC_GRAVITY / LEV
    pivot, _ = tables(VISC_R)
    four = range(STRIPS)

    def density(sal, tem):
        return (half_scale * CONTRACT_S) * sal - (half_scale * EXPAND_T) * tem

    acc = [jnp.zeros((SUB, LANES), F32)] * STRIPS
    side_u = side_cols[0, pl.ds(SUB + ROWS, SUB), :]
    for k in range(LEV):
        edge = pltpu.roll(side_u, LANES - 1 - 2 * k, 1)
        uu = [uf[level_rows(TILES, c, k), :] for c in four]
        uw = west_of(uu, edge, at_last)
        for c in four:
            at = level_rows(TILES, c, k)
            bf[at, :] = uu[c] + uw[c]
            rho = density(sf[at, :], tf[at, :])
            pf[at, :] = acc[c] + rho
            acc[c] = (acc[c] + rho) + rho

    def tile_step(step, _):
        tile = TILES - 1 - step

        @pl.when(tile > 0)
        def _():
            for copy in strip_copies(tile - 1, fields, strips, load_sem):
                copy.wait()

        mid_count, nu, nv = face_counts(counts_flat, side_cols, tile, at_first)
        row_pos = (row * ROWS + SUB * tile + lax.broadcasted_iota(jnp.int32, (SUB, LANES), 0)).astype(F32)
        fu = 0.25 * (CORIO_F0 + CORIO_BETA * ((row_pos + 0.5) / (ROWS * n_row) - 0.5))
        fv = 0.25 * (CORIO_F0 + CORIO_BETA * ((row_pos + 1.0) / (ROWS * n_row) - 0.5))
        mid_rows = pl.ds(SUB * tile + SUB, SUB)
        side_u = side_cols[0, mid_rows, :]
        side_v = side_cols[1, mid_rows, :]
        side_a = side_v + side_cols[1, pl.ds(SUB * tile + 7, SUB), :]
        side_r = density(side_cols[3, mid_rows, :], side_cols[2, mid_rows, :])
        zero = jnp.zeros((SUB, LANES), F32)
        acc = [zero] * STRIPS
        acc_e = zero
        xu, xv = [zero] * STRIPS, [zero] * STRIPS
        sum_du, sum_dv, sum_su, sum_sv = [zero] * STRIPS, [zero] * STRIPS, [zero] * STRIPS, [zero] * STRIPS
        for k in range(LEV):
            turn = LANES - 1 - 2 * k
            here = [level_rows(tile, c, k) for c in four]
            up = [level_rows(tile, c, k, 1) for c in four]
            below = [level_rows(tile, c, k, -1) for c in four]
            uu = [uf[here[c], :] for c in four]
            vv = [vf[here[c], :] for c in four]
            v_south = [vf[below[c], :] for c in four]
            edge_u = pltpu.roll(side_u, turn, 1)
            edge_v = pltpu.roll(side_v, turn, 1)
            u_west = west_of(uu, edge_u, at_last)
            u_east = east_of(uu, edge_u, at_first)
            v_west = west_of(vv, edge_v, at_last)
            v_east = east_of(vv, edge_v, at_first)
            pair_v = [vv[c] + v_south[c] for c in four]
            pair_ve = east_of(pair_v, pltpu.roll(side_a, turn, 1), at_first)
            rho_e = pltpu.roll(side_r, turn, 1)
            p_edge = acc_e + rho_e
            acc_e = p_edge + rho_e
            pp = []
            for c in four:
                rho = density(sf[here[c], :], tf[here[c], :])
                pp.append(acc[c] + rho)
                acc[c] = pp[c] + rho
                pf[here[c], :] = pp[c]
            p_east = east_of(pp, p_edge, at_first)
            for c in four:
                pair_u = uu[c] + u_west[c]
                bf[here[c], :] = pair_u
                v4 = pair_v[c] + pair_ve[c]
                u4 = pair_u + bf[up[c], :]
                du = v4 * (fu - 0.125 * (uf[up[c], :] - uf[below[c], :])) - 0.5 * uu[c] * (u_east[c] - u_west[c]) + (pp[c] - p_east[c])
                dv = (pp[c] - pf[up[c], :]) - u4 * (fv + 0.125 * (v_east[c] - v_west[c])) - 0.5 * vv[c] * (vf[up[c], :] - v_south[c])
                us, vs = uu[c] + du, vv[c] + dv
                on_u, on_v = nu[c] > k, nv[c] > k
                sum_du[c] += jnp.where(on_u, du, 0.0)
                sum_dv[c] += jnp.where(on_v, dv, 0.0)
                sum_su[c] += jnp.where(on_u, us, 0.0)
                sum_sv[c] += jnp.where(on_v, vs, 0.0)
                xu[c] = us * (1.0 / pivot[k]) + xu[c] * (VISC_R / pivot[k])
                xv[c] = vs * (1.0 / pivot[k]) + xv[c] * (VISC_R / pivot[k])
                wu[tile, k, c] = xu[c]
                wv[tile, k, c] = xv[c]
        out_rows = pl.ds(pl.multiple_of(SUB * tile, SUB), SUB)
        for c in four:
            lanes = pl.ds(LANES * c, LANES)
            inv_u = 1.0 / jnp.maximum(nu[c], 1.0)
            inv_v = 1.0 / jnp.maximum(nv[c], 1.0)
            force[0, out_rows, lanes] = sum_du[c] * inv_u
            force[1, out_rows, lanes] = sum_dv[c] * inv_v
            level_mean[0, out_rows, lanes] = sum_su[c] * inv_u
            level_mean[1, out_rows, lanes] = sum_sv[c] * inv_v
        pltpu.make_async_copy(wu.at[tile], wu_out.at[tile], store_sem.at[0, tile]).start()
        pltpu.make_async_copy(wv.at[tile], wv_out.at[tile], store_sem.at[1, tile]).start()
        return 0

    lax.fori_loop(0, TILES, tile_step, 0)
    for tile in range(TILES):
        pltpu.make_async_copy(wu.at[tile], wu_out.at[tile], store_sem.at[0, tile]).wait()
        pltpu.make_async_copy(wv.at[tile], wv_out.at[tile], store_sem.at[1, tile]).wait()


def tracer_kernel(u, v, t, s, north_rows, south_rows, side_cols, own_cols, counts,
                  t_out, s_out,
                  u_s, v_s, t_s, s_s, ft_s, fs_s, wt, ws, t_new, s_new, load_sem, border_sem, store_sem):
    fields, strips = (u, v, t, s), (u_s, v_s, t_s, s_s)
    borders = border_copies(north_rows, south_rows, strips, border_sem)
    for copy in strip_copies(0, fields, strips, load_sem):
        copy.start()
    for copy in borders:
        copy.start()
    for tile in range(1, TILES):
        for copy in strip_copies(tile, fields, strips, load_sem):
            copy.start()
    for copy in strip_copies(0, fields, strips, load_sem):
        copy.wait()
    for copy in borders:
        copy.wait()
    lane = lane_index()
    at_first, at_last = lane == 0, lane == LANES - 1
    even = (lane & 1) == 0
    half = (lane >> 1).astype(F32)
    rows_total = (LEV + 1) * PITCH * STRIPS
    uf, vf, tf, sf, ftf, fsf = [ref.reshape(rows_total, LANES) for ref in (u_s, v_s, t_s, s_s, ft_s, fs_s)]
    counts_flat = counts.reshape(STRIPS * 64, LANES)
    pivot, final = tables(DIFF_R)
    four = range(STRIPS)
    scale = 0.5 * TIME_STEP

    south_count = [jnp.minimum(counts_flat[pl.ds(c * 64, SUB), :], counts_flat[pl.ds(c * 64 + 1, SUB), :]) for c in four]
    for k in range(LEV):
        for c in four:
            here, up = level_rows(-1, c, k), level_rows(-1, c, k, 1)
            hv = jnp.where(south_count[c] > k, scale * vf[here, :], 0.0)
            ftf[here, :] = hv * (tf[here, :] + tf[up, :])
            fsf[here, :] = hv * (sf[here, :] + sf[up, :])

    def tile_step(tile, _):
        @pl.when(tile < TILES - 1)
        def _():
            for copy in strip_copies(tile + 1, fields, strips, load_sem):
                copy.wait()

        mid, nu, nv = face_counts(counts_flat, side_cols, tile, at_first)
        mid_rows = pl.ds(SUB * tile + SUB, SUB)
        own_rows = pl.ds(SUB * tile, SUB)
        side_u = side_cols[0, mid_rows, :]
        west_count = jnp.minimum(side_u[:, 2 * LEV:2 * LEV + 1], mid[0][:, 0:1])
        west_half = jnp.where(half < west_count, scale * side_u, 0.0)
        side_t, side_s = side_cols[2, mid_rows, :], side_cols[3, mid_rows, :]
        mix_t = jnp.where(even, west_half * (side_t + pltpu.roll(own_cols[2, own_rows, :], LANES - 1, 1)), side_t)
        mix_s = jnp.where(even, west_half * (side_s + pltpu.roll(own_cols[3, own_rows, :], LANES - 1, 1)), side_s)
        zero = jnp.zeros((SUB, LANES), F32)
        xt, xs = [zero] * STRIPS, [zero] * STRIPS
        for k in range(LEV):
            turn = LANES - 1 - 2 * k
            here = [level_rows(tile, c, k) for c in four]
            up = [level_rows(tile, c, k, 1) for c in four]
            below = [level_rows(tile, c, k, -1) for c in four]
            hu = [jnp.where(nu[c] > k, scale * uf[here[c], :], 0.0) for c in four]
            hv = [jnp.where(nv[c] > k, scale * vf[here[c], :], 0.0) for c in four]
            if k < LEV - 1:
                inverse = [jnp.where(mid[c] > k + 1, 1.0 / pivot[k], 1.0 / final[k]) for c in four]
            else:
                inverse = [1.0 / final[k]] * STRIPS

            def advance(flat, flux, mix, x, w):
                q = [flat[here[c], :] for c in four]
                edge = pltpu.roll(mix, turn, 1)
                q_east = east_of(q, edge, at_first)
                flux_e = [hu[c] * (q[c] + q_east[c]) for c in four]
                flux_w = west_of(flux_e, edge, at_last)
                for c in four:
                    flux_n = hv[c] * (q[c] + flat[up[c], :])
                    flux[here[c], :] = flux_n
                    new = q[c] - ((flux_e[c] - flux_w[c]) + (flux_n - flux[below[c], :]))
                    x[c] = (new + DIFF_R * x[c]) * inverse[c]
                    w[k, c] = x[c]

            advance(tf, ftf, mix_t, xt, wt)
            advance(sf, fsf, mix_s, xs, ws)
        bt, bs = [zero] * STRIPS, [zero] * STRIPS
        out_rows = pl.ds(pl.multiple_of(SUB * tile, SUB), SUB)
        for k in range(LEV - 1, -1, -1):
            for c in four:
                here = level_rows(tile, c, k)
                lanes = pl.ds(LANES * c, LANES)
                on = mid[c] > k
                yt = wt[k, c] + (DIFF_R / pivot[k]) * bt[c]
                ys = ws[k, c] + (DIFF_R / pivot[k]) * bs[c]
                t_new[k, out_rows, lanes] = jnp.where(on, yt, tf[here, :])
                s_new[k, out_rows, lanes] = jnp.where(on, ys, sf[here, :])
                bt[c] = jnp.where(on, yt, 0.0)
                bs[c] = jnp.where(on, ys, 0.0)
        pltpu.make_async_copy(t_new.at[:, out_rows, :], t_out.at[:, out_rows, :], store_sem.at[0, tile]).start()
        pltpu.make_async_copy(s_new.at[:, out_rows, :], s_out.at[:, out_rows, :], store_sem.at[1, tile]).start()
        return 0

    lax.fori_loop(0, TILES, tile_step, 0)
    for tile in range(TILES):
        rows = pl.ds(SUB * tile, SUB)
        pltpu.make_async_copy(t_new.at[:, rows, :], t_out.at[:, rows, :], store_sem.at[0, tile]).wait()
        pltpu.make_async_copy(s_new.at[:, rows, :], s_out.at[:, rows, :], store_sem.at[1, tile]).wait()


def fast_kernel(n_row, n_sub, weights, wu_in, wv_in, eta, tu, tv, depth, wide_north, wide_south, wide_side,
                force, force_north, force_south, force_side, level_mean, counts, side_cols,
                eta_out, tu_out, tv_out, u_out, v_out,
                e_s, u_s, v_s, b_s, d_s, cu_s, cv_s, bu_s, bv_s, fu_s, fv_s, bar_u, bar_v, wu, wv, u_new, v_new, load_sem, store_sem):
    row = lax.axis_index('row')
    for tile in range(TILES):
        pltpu.make_async_copy(wu_in.at[tile], wu.at[tile], load_sem.at[0, tile]).start()
        pltpu.make_async_copy(wv_in.at[tile], wv.at[tile], load_sem.at[1, tile]).start()
    lane = lane_index()
    at_first, at_last = lane == 0, lane == LANES - 1
    five = range(STRIPS + 1)
    dt_fast = TIME_STEP / n_sub
    total = ROWS * n_row
    zero = jnp.zeros((SUB, LANES), F32)

    def page(tile, c, offset=0):
        return pl.ds(c * PAGE + SUB + SUB * tile + offset, SUB)

    def gather(f, own, north, south, side, tile, c):
        if c == STRIPS:
            return side[f, SUB * tile:SUB * tile + SUB, :]
        lanes = slice(c * LANES, (c + 1) * LANES)
        if tile < REACH // SUB:
            return south[f, SUB * tile:SUB * tile + SUB, lanes]
        if tile < (REACH + ROWS) // SUB:
            return own[SUB * tile - REACH:SUB * tile - REACH + SUB, lanes]
        start = SUB * tile - REACH - ROWS
        return north[f, start:start + SUB, lanes]

    for ref in (e_s, u_s, v_s, b_s, d_s):
        for c in five:
            ref[page(-1, c), :] = zero
            ref[page(EXT_TILES, c), :] = zero
    for tile in range(EXT_TILES):
        for c in five:
            at = page(tile, c)
            e_s[at, :] = gather(0, eta, wide_north, wide_south, wide_side, tile, c)
            u_s[at, :] = gather(1, tu, wide_north, wide_south, wide_side, tile, c)
            v_s[at, :] = gather(2, tv, wide_north, wide_south, wide_side, tile, c)
            d_s[at, :] = gather(3, depth, wide_north, wide_south, wide_side, tile, c)
            bu_s[at, :] = gather(0, force.at[0], force_north, force_south, force_side, tile, c)
            bv_s[at, :] = gather(1, force.at[1], force_north, force_south, force_side, tile, c)
    for tile in range(EXT_TILES):
        place = row * ROWS + (SUB * tile - REACH) + lax.broadcasted_iota(jnp.int32, (SUB, LANES), 0)
        inside = jnp.logical_and(place >= 0, place < total)
        inside_v = jnp.logical_and(place >= 0, place < total - 1)
        row_pos = place.astype(F32)
        fu = (0.25 * dt_fast) * (CORIO_F0 + CORIO_BETA * ((row_pos + 0.5) / total - 0.5))
        fv = (0.25 * dt_fast) * (CORIO_F0 + CORIO_BETA * ((row_pos + 1.0) / total - 0.5))
        fu_s[SUB * tile:SUB * tile + SUB, :] = jnp.where(inside, fu, 0.0)
        fv_s[SUB * tile:SUB * tile + SUB, :] = jnp.where(inside_v, fv, 0.0)
        deep = [d_s[page(tile, c), :] for c in five]
        deep_e = east_of(deep, deep[0], at_first)
        for c in five:
            at = page(tile, c)
            hu = jnp.where(inside, 0.5 * (deep[c] + deep_e[c]), 0.0)
            hv = jnp.where(inside_v, 0.5 * (deep[c] + d_s[page(tile, c, 1), :]), 0.0)
            cu_s[at, :] = (dt_fast * GRAVITY) * hu
            cv_s[at, :] = (dt_fast * GRAVITY) * hv
            bu_s[at, :] = (dt_fast / TIME_STEP) * hu * bu_s[at, :]
            bv_s[at, :] = (dt_fast / TIME_STEP) * hv * bv_s[at, :]
    bar_u[...] = jnp.zeros_like(bar_u)
    bar_v[...] = jnp.zeros_like(bar_v)

    def subcycle(n, low, high):
        weight = weights[n]
        for tile in range(high - 1, low - 1, -1):
            uu = [u_s[page(tile, c), :] for c in five]
            vv = [v_s[page(tile, c), :] for c in five]
            v_south = [v_s[page(tile, c, -1), :] for c in five]
            u_west = west_of(uu, uu[-1], at_last)
            ee = []
            for c in five:
                at = page(tile, c)
                new = e_s[at, :] - dt_fast * ((uu[c] - u_west[c]) + (vv[c] - v_south[c]))
                e_s[at, :] = new
                ee.append(new)
                b_s[at, :] = uu[c] + u_west[c]
            pair_v = [vv[c] + v_south[c] for c in five]
            pair_ve = east_of(pair_v, pair_v[0], at_first)
            e_east = east_of(ee, ee[0], at_first)
            fu = fu_s[SUB * tile:SUB * tile + SUB, :]
            fv = fv_s[SUB * tile:SUB * tile + SUB, :]
            for c in five:
                at, up = page(tile, c), page(tile, c, 1)
                u_next = uu[c] + ((fu * (pair_v[c] + pair_ve[c]) + bu_s[at, :]) - cu_s[at, :] * (e_east[c] - ee[c]))
                v_next = vv[c] + ((bv_s[at, :] - fv * ((uu[c] + u_west[c]) + b_s[up, :])) - cv_s[at, :] * (e_s[up, :] - ee[c]))
                u_s[at, :] = u_next
                v_s[at, :] = v_next
                if c < STRIPS and REACH // SUB <= tile < (REACH + ROWS) // SUB:
                    own = tile - REACH // SUB
                    bar_u[own, c] += weight * u_next
                    bar_v[own, c] += weight * v_next

    def wall_row():
        for tile in range(EXT_TILES):
            place = row * ROWS + (SUB * tile - REACH) + lax.broadcasted_iota(jnp.int32, (SUB, LANES), 0)
            wet = jnp.logical_and(place >= 0, place < total - 1)
            for c in five:
                at = page(tile, c)
                v_s[at, :] = jnp.where(wet, v_s[at, :], 0.0)
                if c < STRIPS and REACH // SUB <= tile < (REACH + ROWS) // SUB:
                    own = tile - REACH // SUB
                    bar_v[own, c] = jnp.where(wet, bar_v[own, c], 0.0)

    n = 0
    while n < n_sub:
        spread = -(-(n_sub - n) // SUB)
        stop = n_sub - SUB * (spread - 1)
        low, high = REACH // SUB - spread, (REACH + ROWS) // SUB + spread

        def some(i, _, low=low, high=high, first=(n == 0)):
            subcycle(i, low, high)
            if first:
                pl.when(i == 0)(wall_row)
            return 0

        lax.fori_loop(n, stop, some, 0)
        n = stop

    counts_flat = counts.reshape(STRIPS * 64, LANES)
    pivot, final = tables(VISC_R)
    four = range(STRIPS)
    for tile in range(TILES):
        for c in four:
            at = page(tile + REACH // SUB, c)
            rows, lanes = pl.ds(SUB * tile, SUB), pl.ds(LANES * c, LANES)
            eta_out[rows, lanes] = e_s[at, :]
            tu_out[rows, lanes] = u_s[at, :]
            tv_out[rows, lanes] = v_s[at, :]

    def tile_step(tile, _):
        pltpu.make_async_copy(wu_in.at[tile], wu.at[tile], load_sem.at[0, tile]).wait()
        pltpu.make_async_copy(wv_in.at[tile], wv.at[tile], load_sem.at[1, tile]).wait()
        mid, nu, nv = face_counts(counts_flat, side_cols, tile, at_first)
        out_rows = pl.ds(pl.multiple_of(SUB * tile, SUB), SUB)
        add_u, add_v = [], []
        for c in four:
            at = pl.ds(c * PAGE + SUB + REACH + SUB * tile, SUB)
            lanes = pl.ds(LANES * c, LANES)
            deep_u = cu_s[at, :] * (1.0 / (dt_fast * GRAVITY))
            deep_v = cv_s[at, :] * (1.0 / (dt_fast * GRAVITY))
            deep_v = jnp.where(nv[c] > 0, deep_v, 1.0)
            add_u.append(bar_u[tile, c] / deep_u - level_mean[0, out_rows, lanes])
            add_v.append(bar_v[tile, c] / deep_v - level_mean[1, out_rows, lanes])
        xu, xv = [zero] * STRIPS, [zero] * STRIPS
        for k in range(LEV - 1, -1, -1):
            ratio, bottom = VISC_R / pivot[k], pivot[k] / final[k]
            for c in four:
                lanes = pl.ds(LANES * c, LANES)

                def solve(w, x, n, add, out):
                    value = w[tile, k, c]
                    last = value * bottom
                    if k < LEV - 1:
                        x[c] = jnp.where(n[c] > k + 1, value + ratio * x[c], last)
                    else:
                        x[c] = last
                    out[k, out_rows, lanes] = jnp.where(n[c] > k, x[c] + add[c], 0.0)

                solve(wu, xu, nu, add_u, u_new)
                solve(wv, xv, nv, add_v, v_new)
        pltpu.make_async_copy(u_new.at[:, out_rows, :], u_out.at[:, out_rows, :], store_sem.at[0, tile]).start()
        pltpu.make_async_copy(v_new.at[:, out_rows, :], v_out.at[:, out_rows, :], store_sem.at[1, tile]).start()
        return 0

    lax.fori_loop(0, TILES, tile_step, 0)
    for tile in range(TILES):
        rows = pl.ds(SUB * tile, SUB)
        pltpu.make_async_copy(u_new.at[:, rows, :], u_out.at[:, rows, :], store_sem.at[0, tile]).wait()
        pltpu.make_async_copy(v_new.at[:, rows, :], v_out.at[:, rows, :], store_sem.at[1, tile]).wait()


def solution(mesh):
    n_row = mesh.shape['row']
    hbm = pl.BlockSpec(memory_space=pltpu.HBM)
    vmem = pl.BlockSpec(memory_space=pltpu.VMEM)
    smem = pl.BlockSpec(memory_space=pltpu.SMEM)
    dma = pltpu.SemaphoreType.DMA
    strip = pltpu.VMEM((STRIPS, LEV + 1, PITCH, LANES), F32)
    whole = pltpu.VMEM((LEV, ROWS, COLS), F32)
    column = pltpu.VMEM((TILES, LEV, STRIPS, SUB, LANES), F32)
    one = pltpu.VMEM((LEV, STRIPS, SUB, LANES), F32)
    extended = pltpu.VMEM(((STRIPS + 1) * PAGE, LANES), F32)

    def shape(*dims):
        return jax.ShapeDtypeStruct(dims, F32)

    def call(body, ins, outs, shapes, scratch, **params):
        return pl.pallas_call(body, out_shape=shapes, in_specs=ins, out_specs=outs, scratch_shapes=scratch,
                              compiler_params=pltpu.CompilerParams(vmem_limit_bytes=VMEM_LIMIT, **params))

    def step(vel_u, vel_v, temp, salt, eta, tu, tv, depth, count, weights):
        n_sub = weights.shape[0]
        north_rows, south_rows, side_cols, own_cols, counts, wide_north, wide_south, wide_side = call(
            functools.partial(halo_kernel, n_row), [hbm] * 4 + [vmem] * 5, [hbm] * 2 + [vmem] * 6,
            [shape(4, LEV, 1, COLS)] * 2 + [shape(4, ROWS + 16, LANES), shape(4, ROWS, LANES), shape(STRIPS, ROWS + 16, LANES),
                                            shape(4, REACH, COLS), shape(4, REACH, COLS), shape(4, EXT, LANES)],
            [pltpu.VMEM((4, 2, LEV, ROWS, LANES), F32), pltpu.VMEM((4, ROWS, LANES), F32), pltpu.VMEM((LEV, 1, COLS), F32),
             dma((4, 2)), dma((4,)), dma((32,)), dma((32,))],
            collective_id=0, has_side_effects=True)(vel_u, vel_v, temp, salt, eta, tu, tv, depth, count)
        wu, wv, force, level_mean = call(
            functools.partial(momentum_kernel, n_row), [hbm] * 6 + [vmem] * 2, [hbm] * 2 + [vmem] * 2,
            [shape(TILES, LEV, STRIPS, SUB, LANES)] * 2 + [shape(2, ROWS, COLS)] * 2,
            [strip] * 6 + [column] * 2 + [dma((TILES, 4, STRIPS)), dma((2, 4, STRIPS)), dma((2, TILES))],
        )(vel_u, vel_v, temp, salt, north_rows, south_rows, side_cols, counts)
        force_north, force_south, force_side = call(
            functools.partial(force_kernel, n_row), [vmem], [vmem] * 3,
            [shape(2, REACH, COLS), shape(2, REACH, COLS), shape(2, EXT, LANES)],
            [pltpu.VMEM((2, ROWS, LANES), F32), dma((5,)), dma((5,))],
            collective_id=1, has_side_effects=True)(force)
        temp_new, salt_new = call(
            tracer_kernel, [hbm] * 6 + [vmem] * 3, [hbm] * 2,
            [shape(LEV, ROWS, COLS)] * 2,
            [strip] * 6 + [one] * 2 + [whole] * 2 + [dma((TILES, 4, STRIPS)), dma((2, 4, STRIPS)), dma((2, TILES))],
        )(vel_u, vel_v, temp, salt, north_rows, south_rows, side_cols, own_cols, counts)
        eta_new, tu_new, tv_new, u_new, v_new = call(
            functools.partial(fast_kernel, n_row, n_sub), [smem] + [hbm] * 2 + [vmem] * 14, [vmem] * 3 + [hbm] * 2,
            [shape(ROWS, COLS)] * 3 + [shape(LEV, ROWS, COLS)] * 2,
            [extended] * 9 + [pltpu.VMEM((EXT, LANES), F32)] * 2 + [pltpu.VMEM((TILES, STRIPS, SUB, LANES), F32)] * 2
            + [column] * 2 + [whole] * 2 + [dma((2, TILES)), dma((2, TILES))],
        )(weights, wu, wv, eta, tu, tv, depth, wide_north, wide_south, wide_side,
          force, force_north, force_south, force_side, level_mean, counts, side_cols)
        return eta_new, tu_new, tv_new, u_new, v_new, temp_new, salt_new

    cube = P(None, 'row', 'col')
    flat = P('row', 'col')
    return jax.shard_map(step, mesh=mesh, in_specs=(cube, cube, cube, cube, flat, flat, flat, flat, flat, P()),
                         out_specs=(flat, flat, flat, cube, cube, cube, cube), check_vma=False)
```

time: 1320 us -> 127 us (0.10); the launches traced: 1290 us -> 126 us
  other arithmetic: 812 us -> 0 us
  starting transfers between devices: 281 us -> 0 us
  Pallas kernels: 0 us -> 125 us
  waiting for transfers between devices: 109 us -> 0 us
  local copies, waits for them, and re-layouts: 87.7 us -> 0 us
    dynamic_update_slice x328 -> x0, other arithmetic: 559 us -> none  [tri_solve(): lax.scan(down, start, (low_links, up_links, right_side))]
    ppermute x143 -> x0, starting transfers between devices: 281 us -> none  [the longest x35 159 us: exchange(): from_south = lax.ppermute(wide[..., -1:, :], 'row', north_moves)]
    pallas_call x0 -> x5, Pallas kernels: none -> 125 us  [the longest x1 44.7 us: step(): call(functools.partial(momentum_kernel, n_row), [hbm] * 6 + [vmem] * 2, [...]
    ppermute x143 -> x0, waiting for transfers between devices: 109 us -> none  [the longest x36 69.8 us: exchange(): from_east = lax.ppermute(field[..., :1], 'col', west_moves)]
    add x62 -> x0, other arithmetic: 83.5 us -> none  [the longest x30 26.5 us: subcycle(): acc_u + weight * trans_u_new]
    another operation x1 -> x0, other arithmetic: 72.7 us -> none  [ocean_columns(): jnp.cumsum(density, axis=0) - 0.5 * density]
    sub x32 -> x0, other arithmetic: 38.3 us -> none  [the longest x2 31.6 us: advect(): tracer_mid - 0.5 * TIME_STEP * (flux_east - flux_west + flux_north - flux...]
    another operation x12 -> x0, local copies, waits for them, and re-layouts: 29.6 us -> none
  transfers between devices with their start and end apart: 143 -> 0, of which waited for: 91 -> 0; matrix products, arithmetic and copies ran while one was open for 63% -> 0% of each run, Pallas kernels for 0% -> 0%
where the time goes in v1:
time: 127 us; the launch traced here: 126 us
  Pallas kernels  125 us (98%)
    pallas_call x1, Pallas kernels, step(): call(functools.partial(momentum_kernel, n_row), [hbm] * 6 + [vmem] * 2, [...  44.7 us
    pallas_call x1, Pallas kernels, step(): call(tracer_kernel, [hbm] * 6 + [vmem] * 3, [hbm] * 2, [shape(LEV, ROWS,...  36.8 us
    pallas_call x1, Pallas kernels, step(): call(functools.partial(fast_kernel, n_row, n_sub), [smem] + [hbm] * 2 + [...  21.2 us
    pallas_call x1, Pallas kernels, step(): call(functools.partial(halo_kernel, n_row), [hbm] * 4 + [vmem] * 5, [hbm]...  13.5 us
    pallas_call x1, Pallas kernels, step(): call(functools.partial(force_kernel, n_row), [vmem], [vmem] * 3, [shape(2...  9.16 us

profile of v1, /device:TPU:0, one launch (start us, length us, event | category | flops | bytes accessed | tf_op | source)
XLA Modules:
  0.0 126.1 jit_solution(222173335125278832)
XLA Ops:
  0.6 13.5 %shard_map.153 = (f32[4,41,1,512]{3,2,1,0:T(1,128)}, f32[4,41,1,512]{3,2,1,0:T(1,128)}, f32[4,64,128]{2,1,0:T(8,128)}, f32[4,48,128]{2,1,0:T(8,128)}, f32[4,64,1...) custom-call(f32[41,48,512]{2,1,0:T(8,128)} %u.5, f32[41,48,512]{2,1,0:T(8,128)} %v.5, ...), custom_call_target="tpu_custom_call" | custom-call | tf_op jit(solution)/shard_map/pallas_call | solution.py:745
  14.1 44.7 %shard_map.154 = (f32[6,41,4,8,128]{4,3,2,1,0:T(8,128)}, f32[6,41,4,8,128]{4,3,2,1,0:T(8,128)}, f32[2,48,512]{2,1,0:T(8,128)}, f32[2,48,512]{2,1,0:T(8,128)}) custom-call(f32[41,48,512]{2,1,0:T(8,128)} %u.5, f32[41,48,512]{2,1,0:T(8,128)} %v.5, f32[41,48,512]{2,1,0:T(8,128)} %t.5, f32[41,48,512]{2,1,0:T(8,128)} %s.5, ...), custom_call_target="tpu_custom_call" | custom-call | tf_op jit(solution)/shard_map/pallas_call | solution.py:752
  58.9 9.2 %shard_map.155 = (f32[2,32,512]{2,1,0:T(8,128)}, f32[2,32,512]{2,1,0:T(8,128)}, f32[2,112,128]{2,1,0:T(8,128)}) custom-call(f32[2,48,512]{2,1,0:T(8,128)} %get-tuple-element.38.force), custom_call_target="tpu_custom_call" | custom-call | tf_op jit(solution)/shard_map/pallas_call | solution.py:757
  68.0 21.2 %shard_map.156 = (f32[48,512]{1,0:T(8,128)}, f32[48,512]{1,0:T(8,128)}, f32[48,512]{1,0:T(8,128)}, f32[41,48,512]{2,1,0:T(8,128)}, f32[41,48,512]{2,1,0:T(8,128)}) custom-call(f32[30]{0:T(128)} %weights.1, f32[6,41,4,8,128]{4,3,2,1,0:T(8,128)} %get-tuple-element.33.wu_in, f32[6,41,4,8,128]{4,3,2,1,0:T(8,128)} %get-tuple-element.34.wv_in, f32[48,512]{1,0:T(8,128)} %eta.3, ...), custom_call_target="tpu_custom_call" | custom-call | tf_op jit(solution)/shard_map/pallas_call | solution.py:767
  89.3 36.8 %shard_map.157 = (f32[41,48,512]{2,1,0:T(8,128)}, f32[41,48,512]{2,1,0:T(8,128)}) custom-call(f32[41,48,512]{2,1,0:T(8,128)} %u.5, f32[41,48,512]{2,1,0:T(8,128)} %v.5, f32[41,48,512]{2,1,0:T(8,128)} %t.5, f32[41,48,512]{2,1,0:T(8,128)} %s.5, f32[4,41,1,512]{3,2,1,0:T(1,128)} %get-tuple-element.29.north_rows, ...), custom_call_target="tpu_custom_call" | custom-call | tf_op jit(solution)/shard_map/pallas_call | solution.py:762

commit v2 on v1

--- a/solution.py
+++ b/solution.py
@@ -319,9 +319,15 @@
     return mid, [jnp.minimum(a, b) for a, b in zip(mid, east)], [jnp.minimum(a, b) for a, b in zip(mid, north)]
 
 
+def unpack(packed, edges, rows):
+    for k in range(LEV):
+        for f, side in enumerate(packed):
+            edges[f, k, rows, :] = pltpu.roll(side, LANES - 1 - 2 * k, 1)
+
+
 def momentum_kernel(n_row, u, v, t, s, north_rows, south_rows, side_cols, counts,
                     wu_out, wv_out, force, level_mean,
-                    u_s, v_s, t_s, s_s, p_s, b_s, wu, wv, load_sem, border_sem, store_sem):
+                    u_s, v_s, t_s, s_s, p_s, b_s, edges, wu, wv, load_sem, border_sem, store_sem):
     row = lax.axis_index('row')
     fields, strips = (u, v, t, s), (u_s, v_s, t_s, s_s)
     borders = border_copies(north_rows, south_rows, strips, border_sem)
@@ -332,12 +338,6 @@
     for tile in range(TILES - 2, -1, -1):
         for copy in strip_copies(tile, fields, strips, load_sem):
             copy.start()
-    for copy in strip_copies(TILES - 1, fields, strips, load_sem):
-        copy.wait()
-    for copy in borders:
-        copy.wait()
-    lane = lane_index()
-    at_first, at_last = lane == 0, lane == LANES - 1
     rows_total = (LEV + 1) * PITCH * STRIPS
     uf, vf, tf, sf, pf, bf = [ref.reshape(rows_total, LANES) for ref in (u_s, v_s, t_s, s_s, p_s, b_s)]
     counts_flat = counts.reshape(STRIPS * 64, LANES)
@@ -348,10 +348,25 @@
     def density(sal, tem):
         return (half_scale * CONTRACT_S) * sal - (half_scale * EXPAND_T) * tem
 
+    def spread(tile, _):
+        rows = pl.ds(pl.multiple_of(SUB * tile, SUB), SUB)
+        mid_rows = pl.ds(SUB * tile + SUB, SUB)
+        side_v = side_cols[1, mid_rows, :]
+        packed = (side_cols[0, mid_rows, :], side_v, side_v + side_cols[1, pl.ds(SUB * tile + SUB - 1, SUB), :],
+                  density(side_cols[3, mid_rows, :], side_cols[2, mid_rows, :]))
+        unpack(packed, edges, rows)
+        return 0
+
+    lax.fori_loop(0, TILES + 1, spread, 0)
+    lane = lane_index()
+    at_first, at_last = lane == 0, lane == LANES - 1
+    for copy in strip_copies(TILES - 1, fields, strips, load_sem):
+        copy.wait()
+    for copy in borders:
+        copy.wait()
     acc = [jnp.zeros((SUB, LANES), F32)] * STRIPS
-    side_u = side_cols[0, pl.ds(SUB + ROWS, SUB), :]
     for k in range(LEV):
-        edge = pltpu.roll(side_u, LANES - 1 - 2 * k, 1)
+        edge = edges[0, k, pl.ds(ROWS, SUB), :]
         uu = [uf[level_rows(TILES, c, k), :] for c in four]
         uw = west_of(uu, edge, at_last)
         for c in four:
@@ -373,33 +388,28 @@
         row_pos = (row * ROWS + SUB * tile + lax.broadcasted_iota(jnp.int32, (SUB, LANES), 0)).astype(F32)
         fu = 0.25 * (CORIO_F0 + CORIO_BETA * ((row_pos + 0.5) / (ROWS * n_row) - 0.5))
         fv = 0.25 * (CORIO_F0 + CORIO_BETA * ((row_pos + 1.0) / (ROWS * n_row) - 0.5))
-        mid_rows = pl.ds(SUB * tile + SUB, SUB)
-        side_u = side_cols[0, mid_rows, :]
-        side_v = side_cols[1, mid_rows, :]
-        side_a = side_v + side_cols[1, pl.ds(SUB * tile + 7, SUB), :]
-        side_r = density(side_cols[3, mid_rows, :], side_cols[2, mid_rows, :])
+        out_rows = pl.ds(pl.multiple_of(SUB * tile, SUB), SUB)
         zero = jnp.zeros((SUB, LANES), F32)
         acc = [zero] * STRIPS
         acc_e = zero
         xu, xv = [zero] * STRIPS, [zero] * STRIPS
         sum_du, sum_dv, sum_su, sum_sv = [zero] * STRIPS, [zero] * STRIPS, [zero] * STRIPS, [zero] * STRIPS
         for k in range(LEV):
-            turn = LANES - 1 - 2 * k
             here = [level_rows(tile, c, k) for c in four]
             up = [level_rows(tile, c, k, 1) for c in four]
             below = [level_rows(tile, c, k, -1) for c in four]
             uu = [uf[here[c], :] for c in four]
             vv = [vf[here[c], :] for c in four]
             v_south = [vf[below[c], :] for c in four]
-            edge_u = pltpu.roll(side_u, turn, 1)
-            edge_v = pltpu.roll(side_v, turn, 1)
+            edge_u = edges[0, k, out_rows, :]
+            edge_v = edges[1, k, out_rows, :]
             u_west = west_of(uu, edge_u, at_last)
             u_east = east_of(uu, edge_u, at_first)
             v_west = west_of(vv, edge_v, at_last)
             v_east = east_of(vv, edge_v, at_first)
             pair_v = [vv[c] + v_south[c] for c in four]
-            pair_ve = east_of(pair_v, pltpu.roll(side_a, turn, 1), at_first)
-            rho_e = pltpu.roll(side_r, turn, 1)
+            pair_ve = east_of(pair_v, edges[2, k, out_rows, :], at_first)
+            rho_e = edges[3, k, out_rows, :]
             p_edge = acc_e + rho_e
             acc_e = p_edge + rho_e
             pp = []
@@ -426,7 +436,6 @@
                 xv[c] = vs * (1.0 / pivot[k]) + xv[c] * (VISC_R / pivot[k])
                 wu[tile, k, c] = xu[c]
                 wv[tile, k, c] = xv[c]
-        out_rows = pl.ds(pl.multiple_of(SUB * tile, SUB), SUB)
         for c in four:
             lanes = pl.ds(LANES * c, LANES)
             inv_u = 1.0 / jnp.maximum(nu[c], 1.0)
@@ -445,9 +454,9 @@
         pltpu.make_async_copy(wv.at[tile], wv_out.at[tile], store_sem.at[1, tile]).wait()
 
 
-def tracer_kernel(u, v, t, s, north_rows, south_rows, side_cols, own_cols, counts,
+def tracer_kernel(u, v, t, s, north_rows, south_rows, side_cols, counts,
                   t_out, s_out,
-                  u_s, v_s, t_s, s_s, ft_s, fs_s, wt, ws, t_new, s_new, load_sem, border_sem, store_sem):
+                  u_s, v_s, t_s, s_s, ft_s, fs_s, edges, wt, ws, t_new, s_new, load_sem, border_sem, store_sem):
     fields, strips = (u, v, t, s), (u_s, v_s, t_s, s_s)
     borders = border_copies(north_rows, south_rows, strips, border_sem)
     for copy in strip_copies(0, fields, strips, load_sem):
@@ -457,13 +466,8 @@
     for tile in range(1, TILES):
         for copy in strip_copies(tile, fields, strips, load_sem):
             copy.start()
-    for copy in strip_copies(0, fields, strips, load_sem):
-        copy.wait()
-    for copy in borders:
-        copy.wait()
     lane = lane_index()
     at_first, at_last = lane == 0, lane == LANES - 1
-    even = (lane & 1) == 0
     half = (lane >> 1).astype(F32)
     rows_total = (LEV + 1) * PITCH * STRIPS
     uf, vf, tf, sf, ftf, fsf = [ref.reshape(rows_total, LANES) for ref in (u_s, v_s, t_s, s_s, ft_s, fs_s)]
@@ -472,6 +476,21 @@
     four = range(STRIPS)
     scale = 0.5 * TIME_STEP
 
+    def spread(tile, _):
+        rows = pl.ds(pl.multiple_of(SUB * tile, SUB), SUB)
+        mid_rows = pl.ds(SUB * tile + SUB, SUB)
+        side_u = side_cols[0, mid_rows, :]
+        west_count = jnp.minimum(side_u[:, 2 * LEV:2 * LEV + 1], counts[0, mid_rows, :][:, 0:1])
+        west_half = jnp.where(half < west_count, scale * side_u, 0.0)
+        packed = (side_cols[2, mid_rows, :], side_cols[3, mid_rows, :], west_half)
+        unpack(packed, edges, rows)
+        return 0
+
+    lax.fori_loop(0, TILES, spread, 0)
+    for copy in strip_copies(0, fields, strips, load_sem):
+        copy.wait()
+    for copy in borders:
+        copy.wait()
     south_count = [jnp.minimum(counts_flat[pl.ds(c * 64, SUB), :], counts_flat[pl.ds(c * 64 + 1, SUB), :]) for c in four]
     for k in range(LEV):
         for c in four:
@@ -487,34 +506,28 @@
                 copy.wait()
 
         mid, nu, nv = face_counts(counts_flat, side_cols, tile, at_first)
-        mid_rows = pl.ds(SUB * tile + SUB, SUB)
-        own_rows = pl.ds(SUB * tile, SUB)
-        side_u = side_cols[0, mid_rows, :]
-        west_count = jnp.minimum(side_u[:, 2 * LEV:2 * LEV + 1], mid[0][:, 0:1])
-        west_half = jnp.where(half < west_count, scale * side_u, 0.0)
-        side_t, side_s = side_cols[2, mid_rows, :], side_cols[3, mid_rows, :]
-        mix_t = jnp.where(even, west_half * (side_t + pltpu.roll(own_cols[2, own_rows, :], LANES - 1, 1)), side_t)
-        mix_s = jnp.where(even, west_half * (side_s + pltpu.roll(own_cols[3, own_rows, :], LANES - 1, 1)), side_s)
+        out_rows = pl.ds(pl.multiple_of(SUB * tile, SUB), SUB)
         zero = jnp.zeros((SUB, LANES), F32)
         xt, xs = [zero] * STRIPS, [zero] * STRIPS
         for k in range(LEV):
-            turn = LANES - 1 - 2 * k
             here = [level_rows(tile, c, k) for c in four]
             up = [level_rows(tile, c, k, 1) for c in four]
             below = [level_rows(tile, c, k, -1) for c in four]
             hu = [jnp.where(nu[c] > k, scale * uf[here[c], :], 0.0) for c in four]
             hv = [jnp.where(nv[c] > k, scale * vf[here[c], :], 0.0) for c in four]
+            hw = west_of(hu, edges[2, k, out_rows, :], at_last)
             if k < LEV - 1:
                 inverse = [jnp.where(mid[c] > k + 1, 1.0 / pivot[k], 1.0 / final[k]) for c in four]
             else:
                 inverse = [1.0 / final[k]] * STRIPS
 
-            def advance(flat, flux, mix, x, w):
+            def advance(flat, flux, which, x, w):
                 q = [flat[here[c], :] for c in four]
-                edge = pltpu.roll(mix, turn, 1)
+                edge = edges[which, k, out_rows, :]
                 q_east = east_of(q, edge, at_first)
+                q_west = west_of(q, edge, at_last)
                 flux_e = [hu[c] * (q[c] + q_east[c]) for c in four]
-                flux_w = west_of(flux_e, edge, at_last)
+                flux_w = [hw[c] * (q[c] + q_west[c]) for c in four]
                 for c in four:
                     flux_n = hv[c] * (q[c] + flat[up[c], :])
                     flux[here[c], :] = flux_n
@@ -522,10 +535,9 @@
                     x[c] = (new + DIFF_R * x[c]) * inverse[c]
                     w[k, c] = x[c]
 
-            advance(tf, ftf, mix_t, xt, wt)
-            advance(sf, fsf, mix_s, xs, ws)
+            advance(tf, ftf, 0, xt, wt)
+            advance(sf, fsf, 1, xs, ws)
         bt, bs = [zero] * STRIPS, [zero] * STRIPS
-        out_rows = pl.ds(pl.multiple_of(SUB * tile, SUB), SUB)
         for k in range(LEV - 1, -1, -1):
             for c in four:
                 here = level_rows(tile, c, k)
@@ -752,7 +764,7 @@
         wu, wv, force, level_mean = call(
             functools.partial(momentum_kernel, n_row), [hbm] * 6 + [vmem] * 2, [hbm] * 2 + [vmem] * 2,
             [shape(TILES, LEV, STRIPS, SUB, LANES)] * 2 + [shape(2, ROWS, COLS)] * 2,
-            [strip] * 6 + [column] * 2 + [dma((TILES, 4, STRIPS)), dma((2, 4, STRIPS)), dma((2, TILES))],
+            [strip] * 6 + [pltpu.VMEM((4, LEV, ROWS + SUB, LANES), F32)] + [column] * 2 + [dma((TILES, 4, STRIPS)), dma((2, 4, STRIPS)), dma((2, TILES))],
         )(vel_u, vel_v, temp, salt, north_rows, south_rows, side_cols, counts)
         force_north, force_south, force_side = call(
             functools.partial(force_kernel, n_row), [vmem], [vmem] * 3,
@@ -760,10 +772,10 @@
             [pltpu.VMEM((2, ROWS, LANES), F32), dma((5,)), dma((5,))],
             collective_id=1, has_side_effects=True)(force)
         temp_new, salt_new = call(
-            tracer_kernel, [hbm] * 6 + [vmem] * 3, [hbm] * 2,
+            tracer_kernel, [hbm] * 6 + [vmem] * 2, [hbm] * 2,
             [shape(LEV, ROWS, COLS)] * 2,
-            [strip] * 6 + [one] * 2 + [whole] * 2 + [dma((TILES, 4, STRIPS)), dma((2, 4, STRIPS)), dma((2, TILES))],
-        )(vel_u, vel_v, temp, salt, north_rows, south_rows, side_cols, own_cols, counts)
+            [strip] * 6 + [pltpu.VMEM((3, LEV, ROWS, LANES), F32)] + [one] * 2 + [whole] * 2 + [dma((TILES, 4, STRIPS)), dma((2, 4, STRIPS)), dma((2, TILES))],
+        )(vel_u, vel_v, temp, salt, north_rows, south_rows, side_cols, counts)
         eta_new, tu_new, tv_new, u_new, v_new = call(
             functools.partial(fast_kernel, n_row, n_sub), [smem] + [hbm] * 2 + [vmem] * 14, [vmem] * 3 + [hbm] * 2,
             [shape(ROWS, COLS)] * 3 + [shape(LEV, ROWS, COLS)] * 2,

time: 127 us -> 77.6 us (0.61)
  Pallas kernels: 125 us -> 76.5 us
    pallas_call x1, Pallas kernels: 44.7 us -> 16.4 us  [step(): call(functools.partial(momentum_kernel, n_row), [hbm] * 6 + [vmem] * 2, [...]
    pallas_call x1, Pallas kernels: 36.8 us -> 16.2 us  [step(): call(tracer_kernel, [hbm] * 6 + [vmem] * 2, [hbm] * 2, [shape(LEV, ROWS,...]
where the time goes in v2:
time: 77.6 us; the launch traced here: 77.1 us
  Pallas kernels  76.5 us (99%)
    pallas_call x1, Pallas kernels, step(): call(functools.partial(fast_kernel, n_row, n_sub), [smem] + [hbm] * 2 + [...  21.2 us
    pallas_call x1, Pallas kernels, step(): call(functools.partial(momentum_kernel, n_row), [hbm] * 6 + [vmem] * 2, [...  16.4 us
    pallas_call x1, Pallas kernels, step(): call(tracer_kernel, [hbm] * 6 + [vmem] * 2, [hbm] * 2, [shape(LEV, ROWS,...  16.2 us
    pallas_call x1, Pallas kernels, step(): call(functools.partial(halo_kernel, n_row), [hbm] * 4 + [vmem] * 5, [hbm]...  13.5 us
    pallas_call x1, Pallas kernels, step(): call(functools.partial(force_kernel, n_row), [vmem], [vmem] * 3, [shape(2...  9.16 us

profile of v2, /device:TPU:0, one launch (start us, length us, event | category | flops | bytes accessed | tf_op | source)
XLA Modules:
  0.0 77.1 jit_solution(9969364412280299715)
XLA Ops:
  0.6 13.5 %shard_map.153 = (f32[4,41,1,512]{3,2,1,0:T(1,128)}, f32[4,41,1,512]{3,2,1,0:T(1,128)}, f32[4,64,128]{2,1,0:T(8,128)}, f32[4,48,128]{2,1,0:T(8,128)}, f32[4,64,1...) custom-call(f32[41,48,512]{2,1,0:T(8,128)} %u.5, f32[41,48,512]{2,1,0:T(8,128)} %v.5, ...), custom_call_target="tpu_custom_call" | custom-call | tf_op jit(solution)/shard_map/pallas_call | solution.py:757
  14.1 16.4 %shard_map.154 = (f32[6,41,4,8,128]{4,3,2,1,0:T(8,128)}, f32[6,41,4,8,128]{4,3,2,1,0:T(8,128)}, f32[2,48,512]{2,1,0:T(8,128)}, f32[2,48,512]{2,1,0:T(8,128)}) custom-call(f32[41,48,512]{2,1,0:T(8,128)} %u.5, f32[41,48,512]{2,1,0:T(8,128)} %v.5, f32[41,48,512]{2,1,0:T(8,128)} %t.5, f32[41,48,512]{2,1,0:T(8,128)} %s.5, ...), custom_call_target="tpu_custom_call" | custom-call | tf_op jit(solution)/shard_map/pallas_call | solution.py:764
  30.5 9.2 %shard_map.155 = (f32[2,32,512]{2,1,0:T(8,128)}, f32[2,32,512]{2,1,0:T(8,128)}, f32[2,112,128]{2,1,0:T(8,128)}) custom-call(f32[2,48,512]{2,1,0:T(8,128)} %get-tuple-element.37.force), custom_call_target="tpu_custom_call" | custom-call | tf_op jit(solution)/shard_map/pallas_call | solution.py:769
  39.7 21.2 %shard_map.156 = (f32[48,512]{1,0:T(8,128)}, f32[48,512]{1,0:T(8,128)}, f32[48,512]{1,0:T(8,128)}, f32[41,48,512]{2,1,0:T(8,128)}, f32[41,48,512]{2,1,0:T(8,128)}) custom-call(f32[30]{0:T(128)} %weights.1, f32[6,41,4,8,128]{4,3,2,1,0:T(8,128)} %get-tuple-element.32.wu_in, f32[6,41,4,8,128]{4,3,2,1,0:T(8,128)} %get-tuple-element.33.wv_in, f32[48,512]{1,0:T(8,128)} %eta.3, ...), custom_call_target="tpu_custom_call" | custom-call | tf_op jit(solution)/shard_map/pallas_call | solution.py:779
  60.9 16.2 %shard_map.157 = (f32[41,48,512]{2,1,0:T(8,128)}, f32[41,48,512]{2,1,0:T(8,128)}) custom-call(f32[41,48,512]{2,1,0:T(8,128)} %u.5, f32[41,48,512]{2,1,0:T(8,128)} %v.5, f32[41,48,512]{2,1,0:T(8,128)} %t.5, f32[41,48,512]{2,1,0:T(8,128)} %s.5, f32[4,41,1,512]{3,2,1,0:T(1,128)} %get-tuple-element.28.north_rows, ...), custom_call_target="tpu_custom_call" | custom-call | tf_op jit(solution)/shard_map/pallas_call | solution.py:774

commit v3 on v0

v3 whole, which is shorter than its diff:
```python
import functools

import jax
import jax.numpy as jnp
from jax import lax
from jax.experimental import pallas as pl
from jax.experimental.pallas import tpu as pltpu
from jax.sharding import PartitionSpec as P

TIME_STEP = 1.0
GRAVITY = 16.0
BC_GRAVITY = 4.0
EXPAND_T = 0.2
CONTRACT_S = 0.6
CORIO_F0 = 0.4
CORIO_BETA = 0.4
VISC_R = 2.0
DIFF_R = 0.5

LEV = 41
ROWS = 48
SUB = 8
COLS = 512
LANES = 128
STRIPS = COLS // LANES
TILES = ROWS // SUB
PITCH = 56
REACH = 32
EXT = ROWS + 2 * REACH
EXT_TILES = EXT // SUB
PAGE = EXT + 16
MESH = pl.DeviceIdType.MESH
F32 = jnp.float32
VMEM_LIMIT = 62 * 1024 * 1024


def tables(strength):
    inner, last, ratio = [], [], 0.0
    for level in range(LEV):
        low = strength if level else 0.0
        pivot = 1.0 + low + strength - low * ratio
        inner.append(pivot)
        last.append(1.0 + low - low * ratio)
        ratio = strength / pivot
    return inner, last


def lane_index():
    return lax.broadcasted_iota(jnp.int32, (SUB, LANES), 1)


def west_of(strips, edge, at_last):
    mixed = [jnp.where(at_last, edge if c == 0 else strips[c - 1], strips[c]) for c in range(len(strips))]
    return [pltpu.roll(x, 1, 1) for x in mixed]


def east_of(strips, edge, at_first):
    n = len(strips)
    mixed = [jnp.where(at_first, edge if c == n - 1 else strips[c + 1], strips[c]) for c in range(n)]
    return [pltpu.roll(x, LANES - 1, 1) for x in mixed]


def places(n_row):
    row = lax.axis_index('row')
    col = lax.axis_index('col')
    other = 1 - col
    has_north = row < n_row - 1
    has_south = row > 0
    return dict(
        row=row, has_north=has_north, has_south=has_south,
        side={'col': other, 'row': row},
        north={'col': col, 'row': row + 1}, south={'col': col, 'row': row - 1},
        north_side={'col': other, 'row': row + 1}, south_side={'col': other, 'row': row - 1})


def meet(at):
    barrier = pltpu.get_barrier_semaphore()
    pl.semaphore_signal(barrier, inc=1, device_id=at['side'], device_id_type=MESH)

    @pl.when(at['has_north'])
    def _():
        pl.semaphore_signal(barrier, inc=1, device_id=at['north'], device_id_type=MESH)
        pl.semaphore_signal(barrier, inc=1, device_id=at['north_side'], device_id_type=MESH)

    @pl.when(at['has_south'])
    def _():
        pl.semaphore_signal(barrier, inc=1, device_id=at['south'], device_id_type=MESH)
        pl.semaphore_signal(barrier, inc=1, device_id=at['south_side'], device_id_type=MESH)

    return barrier


def await_meet(barrier, at):
    pl.semaphore_wait(barrier, 1 + 2 * at['has_north'].astype(jnp.int32) + 2 * at['has_south'].astype(jnp.int32))


def remote(src, dst, send, recv, where):
    return pltpu.make_async_remote_copy(src_ref=src, dst_ref=dst, send_sem=send, recv_sem=recv, device_id=where, device_id_type=MESH)


def level_rows(tile, k, offset=0):
    return pl.ds(SUB * tile + (PITCH * (k + 1) + offset), SUB)


def west_stack(strips, edge, at_last):
    return pltpu.roll(jnp.where(at_last, jnp.concatenate([edge[None], strips[:-1]], axis=0), strips), 1, 2)


def east_stack(strips, edge, at_first):
    return pltpu.roll(jnp.where(at_first, jnp.concatenate([strips[1:], edge[None]], axis=0), strips), LANES - 1, 2)


def face_counts(counts, side_cols, tile):
    rows = SUB * tile + SUB
    mid = counts[:, pl.ds(rows, SUB), :]
    north = counts[:, pl.ds(rows + 1, SUB), :]
    edge = pltpu.roll(side_cols[0, pl.ds(rows, SUB), :], LANES - 1 - 2 * LEV, 1)
    at_first = lax.broadcasted_iota(jnp.int32, mid.shape, 2) == 0
    return mid, jnp.minimum(mid, east_stack(mid, edge, at_first)), jnp.minimum(mid, north)


def unpack(packed, edges, rows):
    for k in range(LEV):
        for f, side in enumerate(packed):
            edges[f, k, rows, :] = pltpu.roll(side, LANES - 1 - 2 * k, 1)


def step_kernel(n_row, u, v, t, s, eta, tu, tv, depth, count,
                wu_out, wv_out, wt_out, ws_out, force, level_mean, side_cols, counts,
                wide_north, wide_south, wide_side, force_north, force_south, force_side,
                u_s, v_s, t_s, s_s, one_s, two_s, edges, wu, wv, wt, ws, own_cols, fold, force_fold,
                load_sem, send_sem, recv_sem, store_sem):
    at = places(n_row)
    fields, strips = (u, v, t, s), (u_s, v_s, t_s, s_s)
    four = range(STRIPS)
    loads = [[pltpu.make_async_copy(fields[f].at[:, :, pl.ds(LANES * c, LANES)], strips[f].at[c, pl.ds(1, LEV), pl.ds(0, ROWS), :], load_sem.at[f, c])
              for c in four] for f in four]
    for c in (0, STRIPS - 1):
        for f in four:
            loads[f][c].start()
    for c in range(1, STRIPS - 1):
        for f in four:
            loads[f][c].start()
    lane = lane_index()
    at_first, at_last = lane == 0, lane == LANES - 1
    zero = jnp.zeros((SUB, LANES), F32)

    def clear_rows():
        def body(k, _):
            for strip in strips:
                for c in four:
                    strip[c, k, pl.ds(ROWS, SUB), :] = zero
            return 0

        lax.fori_loop(0, LEV + 1, body, 0)

    @pl.when(jnp.logical_not(at['has_north']))
    def _():
        clear_rows()
        counts[:, SUB + ROWS:, :] = jnp.zeros((STRIPS, SUB, LANES), F32)
        side_cols[:, SUB + ROWS:, :] = jnp.zeros((STRIPS, SUB, LANES), F32)
        wide_north[...] = jnp.zeros_like(wide_north)
        force_north[...] = jnp.zeros_like(force_north)
        wide_side[:, REACH + ROWS:, :] = jnp.zeros((STRIPS, REACH, LANES), F32)
        force_side[:, REACH + ROWS:, :] = jnp.zeros((2, REACH, LANES), F32)

    @pl.when(jnp.logical_not(at['has_south']))
    def _():
        clear_rows()
        counts[:, :SUB, :] = jnp.zeros((STRIPS, SUB, LANES), F32)
        side_cols[:, :SUB, :] = jnp.zeros((STRIPS, SUB, LANES), F32)
        wide_south[...] = jnp.zeros_like(wide_south)
        force_south[...] = jnp.zeros_like(force_south)
        wide_side[:, :REACH, :] = jnp.zeros((STRIPS, REACH, LANES), F32)
        force_side[:, :REACH, :] = jnp.zeros((2, REACH, LANES), F32)

    for c in four:
        counts[c, SUB:SUB + ROWS, :] = count[:, c * LANES:(c + 1) * LANES].astype(F32)
    barrier = meet(at)
    await_meet(barrier, at)
    slot = iter(range(LANES))

    def plan(bucket, src, dst, where):
        i = next(slot)
        bucket.append(remote(src, dst, send_sem.at[i], recv_sem.at[i], at[where]))

    def start(north, south, side=()):
        @pl.when(at['has_north'])
        def _():
            for copy in north:
                copy.start()

        @pl.when(at['has_south'])
        def _():
            for copy in south:
                copy.start()

        for copy in side:
            copy.start()

    def arrive(north, south, side=()):
        for copy in side:
            copy.wait_recv()

        @pl.when(at['has_north'])
        def _():
            for copy in south:
                copy.wait_recv()

        @pl.when(at['has_south'])
        def _():
            for copy in north:
                copy.wait_recv()

    def leave(north, south, side=()):
        for copy in side:
            copy.wait_send()

        @pl.when(at['has_north'])
        def _():
            for copy in north:
                copy.wait_send()

        @pl.when(at['has_south'])
        def _():
            for copy in south:
                copy.wait_send()

    rows_north, rows_south = [], []
    for f in four:
        for c in four:
            lanes = pl.ds(LANES * c, LANES)
            plan(rows_north, fields[f].at[:, pl.ds(ROWS - 1, 1), lanes], strips[f].at[c, pl.ds(0, LEV), pl.ds(PITCH - 1, 1), :], 'north')
            plan(rows_south, fields[f].at[:, pl.ds(0, 1), lanes], strips[f].at[c, pl.ds(1, LEV), pl.ds(ROWS, 1), :], 'south')
    count_north, count_south = [], []
    plan(count_north, counts.at[:, pl.ds(ROWS, SUB), :], counts.at[:, pl.ds(0, SUB), :], 'north')
    plan(count_south, counts.at[:, pl.ds(SUB, SUB), :], counts.at[:, pl.ds(SUB + ROWS, SUB), :], 'south')
    start(count_north + rows_north, count_south + rows_south)

    half_lane = lane >> 1
    sides, corner_north, corner_south = [], [], []
    for f in four:
        loads[f][0].wait()
        loads[f][STRIPS - 1].wait()

        def pack(tile, _):
            rows = pl.ds(pl.multiple_of(SUB * tile, SUB), SUB)
            packed = zero
            for k in range(LEV + 1 if f == 0 else LEV):
                if k < LEV:
                    first, last = strips[f][0, k + 1, rows, :], strips[f][STRIPS - 1, k + 1, rows, :]
                else:
                    lower = pl.ds(pl.multiple_of(SUB * tile + SUB, SUB), SUB)
                    first, last = counts[0, lower, :], counts[STRIPS - 1, lower, :]
                both = pltpu.roll(jnp.where(at_first, first, last), 2 * k + 1, 1)
                packed = jnp.where(half_lane == k, both, packed)
            own_cols[f, rows, :] = packed
            return 0

        lax.fori_loop(0, TILES, pack, 0)
        plan(sides, own_cols.at[f], side_cols.at[f, pl.ds(SUB, ROWS), :], 'side')
        sides[-1].start()
        if f == 0:
            plan(corner_south, own_cols.at[f, pl.ds(0, SUB), :], side_cols.at[f, pl.ds(SUB + ROWS, SUB), :], 'south_side')
        if f == 1:
            plan(corner_north, own_cols.at[f, pl.ds(ROWS - SUB, SUB), :], side_cols.at[f, pl.ds(0, SUB), :], 'north_side')
    start(corner_north, corner_south)

    fast = (eta, tu, tv, depth)
    low_half = lax.broadcasted_iota(jnp.int32, (ROWS, LANES), 1) < LANES // 2
    for f in four:
        fold[f] = jnp.where(low_half, fast[f][:, :LANES], fast[f][:, COLS - LANES:])
    wide_up, wide_down, wide_across = [], [], []
    for f in four:
        plan(wide_up, fast[f].at[pl.ds(ROWS - REACH, REACH), :], wide_south.at[f], 'north')
        plan(wide_down, fast[f].at[pl.ds(0, REACH), :], wide_north.at[f], 'south')
    plan(wide_up, fold.at[:, pl.ds(ROWS - REACH, REACH), :], wide_side.at[:, pl.ds(0, REACH), :], 'north_side')
    plan(wide_down, fold.at[:, pl.ds(0, REACH), :], wide_side.at[:, pl.ds(REACH + ROWS, REACH), :], 'south_side')
    plan(wide_across, fold, wide_side.at[:, pl.ds(REACH, ROWS), :], 'side')

    half_scale = 0.5 * BC_GRAVITY / LEV
    scale = 0.5 * TIME_STEP
    half = half_lane.astype(F32)

    def density(sal, tem):
        return (half_scale * CONTRACT_S) * sal - (half_scale * EXPAND_T) * tem

    arrive(count_north + corner_north, count_south + corner_south, sides)

    def spread(tile, _):
        rows = pl.ds(pl.multiple_of(SUB * tile, SUB), SUB)
        mid_rows = pl.ds(SUB * tile + SUB, SUB)
        side = [side_cols[f, mid_rows, :] for f in four]
        west_count = jnp.minimum(side[0][:, 2 * LEV:2 * LEV + 1], counts[0, mid_rows, :][:, 0:1])
        unpack((side[0], side[1], side[1] + side_cols[1, pl.ds(SUB * tile + SUB - 1, SUB), :], density(side[3], side[2]),
                side[2], side[3], jnp.where(half < west_count, scale * side[0], 0.0)), edges, rows)
        return 0

    lax.fori_loop(0, TILES + 1, spread, 0)
    for c in range(1, STRIPS - 1):
        for f in four:
            loads[f][c].wait()
    arrive(rows_north, rows_south)
    leave(rows_north, rows_south)
    start(wide_up, wide_down, wide_across)
    flats = [ref.reshape(STRIPS, (LEV + 1) * PITCH, LANES) for ref in (u_s, v_s, t_s, s_s, one_s, two_s)]
    uf, vf, tf, sf, pf, bf = flats
    stack = lax.broadcasted_iota(jnp.int32, (STRIPS, SUB, LANES), 2)
    first_lanes, last_lanes = stack == 0, stack == LANES - 1
    none = jnp.zeros((STRIPS, SUB, LANES), F32)
    pivot, _ = tables(VISC_R)
    acc = none
    for k in range(LEV):
        spot = level_rows(TILES, k)
        uu = uf[:, spot, :]
        bf[:, spot, :] = uu + west_stack(uu, edges[0, k, pl.ds(ROWS, SUB), :], last_lanes)
        rho = density(sf[:, spot, :], tf[:, spot, :])
        pf[:, spot, :] = acc + rho
        acc = (acc + rho) + rho

    def momentum(step, _):
        tile = TILES - 1 - step
        _, nu, nv = face_counts(counts, side_cols, tile)
        row_pos = (at['row'] * ROWS + SUB * tile + lax.broadcasted_iota(jnp.int32, (STRIPS, SUB, LANES), 1)).astype(F32)
        fu = 0.25 * (CORIO_F0 + CORIO_BETA * ((row_pos + 0.5) / (ROWS * n_row) - 0.5))
        fv = 0.25 * (CORIO_F0 + CORIO_BETA * ((row_pos + 1.0) / (ROWS * n_row) - 0.5))
        out_rows = pl.ds(pl.multiple_of(SUB * tile, SUB), SUB)
        acc, acc_e = none, zero
        xu, xv, sum_du, sum_dv, sum_su, sum_sv = (none,) * 6
        for k in range(LEV):
            here, up, below = [level_rows(tile, k, step) for step in (0, 1, -1)]
            uu, vv = uf[:, here, :], vf[:, here, :]
            v_south = vf[:, below, :]
            edge_u, edge_v = edges[0, k, out_rows, :], edges[1, k, out_rows, :]
            u_west = west_stack(uu, edge_u, last_lanes)
            u_east = east_stack(uu, edge_u, first_lanes)
            v_west = west_stack(vv, edge_v, last_lanes)
            v_east = east_stack(vv, edge_v, first_lanes)
            pair_v = vv + v_south
            pair_ve = east_stack(pair_v, edges[2, k, out_rows, :], first_lanes)
            rho_e = edges[3, k, out_rows, :]
            p_edge = acc_e + rho_e
            acc_e = p_edge + rho_e
            rho = density(sf[:, here, :], tf[:, here, :])
            pp = acc + rho
            acc = pp + rho
            pf[:, here, :] = pp
            p_east = east_stack(pp, p_edge, first_lanes)
            pair_u = uu + u_west
            bf[:, here, :] = pair_u
            v4 = pair_v + pair_ve
            u4 = pair_u + bf[:, up, :]
            du = v4 * (fu - 0.125 * (uf[:, up, :] - uf[:, below, :])) - 0.5 * uu * (u_east - u_west) + (pp - p_east)
            dv = (pp - pf[:, up, :]) - u4 * (fv + 0.125 * (v_east - v_west)) - 0.5 * vv * (vf[:, up, :] - v_south)
            us, vs = uu + du, vv + dv
            on_u, on_v = nu > k, nv > k
            sum_du += jnp.where(on_u, du, 0.0)
            sum_dv += jnp.where(on_v, dv, 0.0)
            sum_su += jnp.where(on_u, us, 0.0)
            sum_sv += jnp.where(on_v, vs, 0.0)
            xu = us * (1.0 / pivot[k]) + xu * (VISC_R / pivot[k])
            xv = vs * (1.0 / pivot[k]) + xv * (VISC_R / pivot[k])
            wu[tile, k] = xu
            wv[tile, k] = xv
        inv_u = 1.0 / jnp.maximum(nu, 1.0)
        inv_v = 1.0 / jnp.maximum(nv, 1.0)
        for c in four:
            lanes = pl.ds(LANES * c, LANES)
            force[0, out_rows, lanes] = (sum_du * inv_u)[c]
            force[1, out_rows, lanes] = (sum_dv * inv_v)[c]
            level_mean[0, out_rows, lanes] = (sum_su * inv_u)[c]
            level_mean[1, out_rows, lanes] = (sum_sv * inv_v)[c]
        pltpu.make_async_copy(wu.at[tile], wu_out.at[tile], store_sem.at[0, tile]).start()
        pltpu.make_async_copy(wv.at[tile], wv_out.at[tile], store_sem.at[1, tile]).start()
        return 0

    lax.fori_loop(0, TILES, momentum, 0)

    low_half = lax.broadcasted_iota(jnp.int32, (ROWS, LANES), 1) < LANES // 2
    for f in range(2):
        force_fold[f] = jnp.where(low_half, force[f, :, :LANES], force[f, :, COLS - LANES:])
    force_up, force_down, force_across = [], [], []
    plan(force_up, force.at[:, pl.ds(ROWS - REACH, REACH), :], force_south, 'north')
    plan(force_up, force_fold.at[:, pl.ds(ROWS - REACH, REACH), :], force_side.at[:, pl.ds(0, REACH), :], 'north_side')
    plan(force_down, force.at[:, pl.ds(0, REACH), :], force_north, 'south')
    plan(force_down, force_fold.at[:, pl.ds(0, REACH), :], force_side.at[:, pl.ds(REACH + ROWS, REACH), :], 'south_side')
    plan(force_across, force_fold, force_side.at[:, pl.ds(REACH, ROWS), :], 'side')
    start(force_up, force_down, force_across)

    ftf, fsf = pf, bf
    pivot, final = tables(DIFF_R)

    south_count = jnp.minimum(counts[:, pl.ds(0, SUB), :], counts[:, pl.ds(1, SUB), :])
    for k in range(LEV):
        here, up = level_rows(-1, k), level_rows(-1, k, 1)
        hv = jnp.where(south_count > k, scale * vf[:, here, :], 0.0)
        ftf[:, here, :] = hv * (tf[:, here, :] + tf[:, up, :])
        fsf[:, here, :] = hv * (sf[:, here, :] + sf[:, up, :])

    def tracers(tile, _):
        mid, nu, nv = face_counts(counts, side_cols, tile)
        out_rows = pl.ds(pl.multiple_of(SUB * tile, SUB), SUB)
        xt, xs = none, none
        for k in range(LEV):
            here, up, below = [level_rows(tile, k, step) for step in (0, 1, -1)]
            hu = jnp.where(nu > k, scale * uf[:, here, :], 0.0)
            hv = jnp.where(nv > k, scale * vf[:, here, :], 0.0)
            hw = west_stack(hu, edges[6, k, out_rows, :], last_lanes)
            inverse = jnp.where(mid > k + 1, 1.0 / pivot[k], 1.0 / final[k]) if k < LEV - 1 else 1.0 / final[k]

            def advance(flat, flux, which, x, w):
                q = flat[:, here, :]
                edge = edges[which, k, out_rows, :]
                flux_e = hu * (q + east_stack(q, edge, first_lanes))
                flux_w = hw * (q + west_stack(q, edge, last_lanes))
                flux_n = hv * (q + flat[:, up, :])
                flux[:, here, :] = flux_n
                new = q - ((flux_e - flux_w) + (flux_n - flux[:, below, :]))
                x = (new + DIFF_R * x) * inverse
                w[tile, k] = jnp.where(mid > k, x, new)
                return x

            xt = advance(tf, ftf, 4, xt, wt)
            xs = advance(sf, fsf, 5, xs, ws)
        pltpu.make_async_copy(wt.at[tile], wt_out.at[tile], store_sem.at[2, tile]).start()
        pltpu.make_async_copy(ws.at[tile], ws_out.at[tile], store_sem.at[3, tile]).start()
        return 0

    lax.fori_loop(0, TILES, tracers, 0)
    for tile in range(TILES):
        for i, (src, dst) in enumerate(((wu, wu_out), (wv, wv_out), (wt, wt_out), (ws, ws_out))):
            pltpu.make_async_copy(src.at[tile], dst.at[tile], store_sem.at[i, tile]).wait()
    leave(count_north + corner_north, count_south + corner_south, sides)
    for group in ((wide_up, wide_down, wide_across), (force_up, force_down, force_across)):
        arrive(*group)
        leave(*group)


def fast_kernel(n_row, n_sub, weights, wu_in, wv_in, wt_in, ws_in, eta, tu, tv, depth, wide_north, wide_south, wide_side,
                force, force_north, force_south, force_side, level_mean, counts, side_cols,
                eta_out, tu_out, tv_out, u_out, v_out, t_out, s_out,
                e_s, u_s, v_s, b_s, d_s, cu_s, cv_s, bu_s, bv_s, fu_s, fv_s, bar_u, bar_v, wu, wv, wt, ws, u_new, v_new, t_new, s_new, load_sem, store_sem):
    row = lax.axis_index('row')
    def fetch(tile):
        return [pltpu.make_async_copy(src.at[tile], dst.at[tile], load_sem.at[i, tile])
                for i, (src, dst) in enumerate(((wt_in, wt), (ws_in, ws), (wu_in, wu), (wv_in, wv)))]

    def put(tile, i, src, dst):
        rows = pl.ds(pl.multiple_of(SUB * tile, SUB), SUB)
        return pltpu.make_async_copy(src.at[:, rows, :], dst.at[:, rows, :], store_sem.at[i, tile])

    for part in (slice(0, 2), slice(2, 4)):
        for tile in range(TILES):
            for copy in fetch(tile)[part]:
                copy.start()
    lane = lane_index()
    at_first, at_last = lane == 0, lane == LANES - 1
    five = range(STRIPS + 1)
    dt_fast = TIME_STEP / n_sub
    total = ROWS * n_row
    zero = jnp.zeros((SUB, LANES), F32)

    def page(tile, c, offset=0):
        return pl.ds(c * PAGE + SUB + SUB * tile + offset, SUB)

    def gather(f, own, north, south, side, tile, c):
        if c == STRIPS:
            return side[f, SUB * tile:SUB * tile + SUB, :]
        lanes = slice(c * LANES, (c + 1) * LANES)
        if tile < REACH // SUB:
            return south[f, SUB * tile:SUB * tile + SUB, lanes]
        if tile < (REACH + ROWS) // SUB:
            return own[SUB * tile - REACH:SUB * tile - REACH + SUB, lanes]
        start = SUB * tile - REACH - ROWS
        return north[f, start:start + SUB, lanes]

    for ref in (e_s, u_s, v_s, b_s, d_s):
        for c in five:
            ref[page(-1, c), :] = zero
            ref[page(EXT_TILES, c), :] = zero
    for tile in range(EXT_TILES):
        for c in five:
            at = page(tile, c)
            e_s[at, :] = gather(0, eta, wide_north, wide_south, wide_side, tile, c)
            u_s[at, :] = dt_fast * gather(1, tu, wide_north, wide_south, wide_side, tile, c)
            v_s[at, :] = dt_fast * gather(2, tv, wide_north, wide_south, wide_side, tile, c)
            d_s[at, :] = gather(3, depth, wide_north, wide_south, wide_side, tile, c)
            bu_s[at, :] = gather(0, force.at[0], force_north, force_south, force_side, tile, c)
            bv_s[at, :] = gather(1, force.at[1], force_north, force_south, force_side, tile, c)
    for tile in range(EXT_TILES):
        place = row * ROWS + (SUB * tile - REACH) + lax.broadcasted_iota(jnp.int32, (SUB, LANES), 0)
        inside = jnp.logical_and(place >= 0, place < total)
        inside_v = jnp.logical_and(place >= 0, place < total - 1)
        row_pos = place.astype(F32)
        fu = (0.25 * dt_fast) * (CORIO_F0 + CORIO_BETA * ((row_pos + 0.5) / total - 0.5))
        fv = (0.25 * dt_fast) * (CORIO_F0 + CORIO_BETA * ((row_pos + 1.0) / total - 0.5))
        fu_s[SUB * tile:SUB * tile + SUB, :] = jnp.where(inside, fu, 0.0)
        fv_s[SUB * tile:SUB * tile + SUB, :] = jnp.where(inside_v, fv, 0.0)
        deep = [d_s[page(tile, c), :] for c in five]
        deep_e = east_of(deep, deep[0], at_first)
        for c in five:
            at = page(tile, c)
            hu = jnp.where(inside, 0.5 * (deep[c] + deep_e[c]), 0.0)
            hv = jnp.where(inside_v, 0.5 * (deep[c] + d_s[page(tile, c, 1), :]), 0.0)
            cu_s[at, :] = (dt_fast * dt_fast * GRAVITY) * hu
            cv_s[at, :] = (dt_fast * dt_fast * GRAVITY) * hv
            bu_s[at, :] = (dt_fast * dt_fast / TIME_STEP) * hu * bu_s[at, :]
            bv_s[at, :] = (dt_fast * dt_fast / TIME_STEP) * hv * bv_s[at, :]
    bar_u[...] = jnp.zeros_like(bar_u)
    bar_v[...] = jnp.zeros_like(bar_v)

    def subcycle(n, low, high):
        weight = weights[n]
        for tile in range(high - 1, low - 1, -1):
            uu = [u_s[page(tile, c), :] for c in five]
            vv = [v_s[page(tile, c), :] for c in five]
            v_south = [v_s[page(tile, c, -1), :] for c in five]
            part = [e_s[page(tile, c), :] - (uu[c] + (vv[c] - v_south[c])) for c in five]
            pair_v = [vv[c] + v_south[c] for c in five]
            u_west = west_of(uu, uu[-1], at_last)
            part_e = east_of(part, part[0], at_first)
            pair_ve = east_of(pair_v, pair_v[0], at_first)
            fu = fu_s[SUB * tile:SUB * tile + SUB, :]
            fv = fv_s[SUB * tile:SUB * tile + SUB, :]
            for c in five:
                at, up = page(tile, c), page(tile, c, 1)
                new = part[c] + u_west[c]
                pair_u = uu[c] + u_west[c]
                e_s[at, :] = new
                b_s[at, :] = pair_u
                u_next = uu[c] + ((fu * (pair_v[c] + pair_ve[c]) + bu_s[at, :]) - cu_s[at, :] * ((part_e[c] + uu[c]) - new))
                v_next = vv[c] + ((bv_s[at, :] - fv * (pair_u + b_s[up, :])) - cv_s[at, :] * (e_s[up, :] - new))
                u_s[at, :] = u_next
                v_s[at, :] = v_next
                if c < STRIPS and REACH // SUB <= tile < (REACH + ROWS) // SUB:
                    own = tile - REACH // SUB
                    bar_u[own, c] += weight * u_next
                    bar_v[own, c] += weight * v_next

    def wall_row():
        for tile in range(EXT_TILES):
            place = row * ROWS + (SUB * tile - REACH) + lax.broadcasted_iota(jnp.int32, (SUB, LANES), 0)
            wet = jnp.logical_and(place >= 0, place < total - 1)
            for c in five:
                at = page(tile, c)
                v_s[at, :] = jnp.where(wet, v_s[at, :], 0.0)
                if c < STRIPS and REACH // SUB <= tile < (REACH + ROWS) // SUB:
                    own = tile - REACH // SUB
                    bar_v[own, c] = jnp.where(wet, bar_v[own, c], 0.0)

    four = range(STRIPS)
    inner, _ = tables(DIFF_R)

    def tracers(tile, _):
        for copy in fetch(tile)[:2]:
            copy.wait()
        mid = [counts[c, pl.ds(pl.multiple_of(SUB * tile + SUB, SUB), SUB), :] for c in four]
        out_rows = pl.ds(pl.multiple_of(SUB * tile, SUB), SUB)
        xt, xs = [zero] * STRIPS, [zero] * STRIPS
        for k in range(LEV - 1, -1, -1):
            for c in four:
                on = mid[c] > k
                lanes = pl.ds(LANES * c, LANES)

                def solve(w, x, out):
                    value = w[tile, k, c]
                    full = value + (DIFF_R / inner[k]) * x[c]
                    out[k, out_rows, lanes] = jnp.where(on, full, value)
                    x[c] = jnp.where(on, full, 0.0)

                solve(wt, xt, t_new)
                solve(ws, xs, s_new)
        put(tile, 2, t_new, t_out).start()
        put(tile, 3, s_new, s_out).start()
        return 0

    n = 0
    while n < n_sub:
        spread = -(-(n_sub - n) // SUB)
        stop = n_sub - SUB * (spread - 1)
        low, high = REACH // SUB - spread, (REACH + ROWS) // SUB + spread

        def some(i, _, low=low, high=high, first=(n == 0)):
            subcycle(i, low, high)
            if first:
                pl.when(i == 0)(wall_row)
            return 0

        lax.fori_loop(n, stop, some, 0)
        if n == 0:
            lax.fori_loop(0, TILES, tracers, 0)
        n = stop

    pivot, final = tables(VISC_R)
    for tile in range(TILES):
        for c in four:
            at = page(tile + REACH // SUB, c)
            rows, lanes = pl.ds(SUB * tile, SUB), pl.ds(LANES * c, LANES)
            eta_out[rows, lanes] = e_s[at, :]
            tu_out[rows, lanes] = u_s[at, :] * (1.0 / dt_fast)
            tv_out[rows, lanes] = v_s[at, :] * (1.0 / dt_fast)

    def tile_step(tile, _):
        for copy in fetch(tile)[2:]:
            copy.wait()
        _, nu, nv = face_counts(counts, side_cols, tile)
        out_rows = pl.ds(pl.multiple_of(SUB * tile, SUB), SUB)
        add_u, add_v = [], []
        for c in four:
            at = pl.ds(c * PAGE + SUB + REACH + SUB * tile, SUB)
            lanes = pl.ds(LANES * c, LANES)
            deep_u = cu_s[at, :] * (1.0 / (dt_fast * GRAVITY))
            deep_v = cv_s[at, :] * (1.0 / (dt_fast * GRAVITY))
            deep_v = jnp.where(nv[c] > 0, deep_v, 1.0)
            add_u.append(bar_u[tile, c] / deep_u - level_mean[0, out_rows, lanes])
            add_v.append(bar_v[tile, c] / deep_v - level_mean[1, out_rows, lanes])
        xu, xv = [zero] * STRIPS, [zero] * STRIPS
        for k in range(LEV - 1, -1, -1):
            ratio, bottom = VISC_R / pivot[k], pivot[k] / final[k]
            for c in four:
                lanes = pl.ds(LANES * c, LANES)

                def solve(w, x, n, add, out):
                    value = w[tile, k, c]
                    last = value * bottom
                    if k < LEV - 1:
                        x[c] = jnp.where(n[c] > k + 1, value + ratio * x[c], last)
                    else:
                        x[c] = last
                    out[k, out_rows, lanes] = jnp.where(n[c] > k, x[c] + add[c], 0.0)

                solve(wu, xu, nu, add_u, u_new)
                solve(wv, xv, nv, add_v, v_new)
        put(tile, 0, u_new, u_out).start()
        put(tile, 1, v_new, v_out).start()
        return 0

    lax.fori_loop(0, TILES, tile_step, 0)
    for tile in range(TILES):
        for i, (src, dst) in enumerate(((u_new, u_out), (v_new, v_out), (t_new, t_out), (s_new, s_out))):
            put(tile, i, src, dst).wait()


def solution(mesh):
    n_row = mesh.shape['row']
    hbm = pl.BlockSpec(memory_space=pltpu.HBM)
    vmem = pl.BlockSpec(memory_space=pltpu.VMEM)
    smem = pl.BlockSpec(memory_space=pltpu.SMEM)
    dma = pltpu.SemaphoreType.DMA
    strip = pltpu.VMEM((STRIPS, LEV + 1, PITCH, LANES), F32)
    whole = pltpu.VMEM((LEV, ROWS, COLS), F32)
    column = pltpu.VMEM((TILES, LEV, STRIPS, SUB, LANES), F32)
    extended = pltpu.VMEM(((STRIPS + 1) * PAGE, LANES), F32)

    def shape(*dims):
        return jax.ShapeDtypeStruct(dims, F32)

    def call(body, ins, outs, shapes, scratch, **params):
        return pl.pallas_call(body, out_shape=shapes, in_specs=ins, out_specs=outs, scratch_shapes=scratch,
                              compiler_params=pltpu.CompilerParams(vmem_limit_bytes=VMEM_LIMIT, **params))

    def step(vel_u, vel_v, temp, salt, eta, tu, tv, depth, count, weights):
        n_sub = weights.shape[0]
        (wu, wv, wt, ws, force, level_mean, side_cols, counts, wide_north, wide_south, wide_side,
         force_north, force_south, force_side) = call(
            functools.partial(step_kernel, n_row), [hbm] * 4 + [vmem] * 5, [hbm] * 4 + [vmem] * 10,
            [shape(TILES, LEV, STRIPS, SUB, LANES)] * 4 + [shape(2, ROWS, COLS)] * 2
            + [shape(4, ROWS + 2 * SUB, LANES), shape(STRIPS, ROWS + 2 * SUB, LANES)]
            + [shape(4, REACH, COLS), shape(4, REACH, COLS), shape(4, EXT, LANES)]
            + [shape(2, REACH, COLS), shape(2, REACH, COLS), shape(2, EXT, LANES)],
            [strip] * 6 + [pltpu.VMEM((7, LEV, ROWS + SUB, LANES), F32)] + [column] * 4
            + [pltpu.VMEM((4, ROWS, LANES), F32)] * 2 + [pltpu.VMEM((2, ROWS, LANES), F32)]
            + [dma((4, STRIPS)), dma((64,)), dma((64,)), dma((4, TILES))],
            collective_id=0, has_side_effects=True)(vel_u, vel_v, temp, salt, eta, tu, tv, depth, count)
        return call(
            functools.partial(fast_kernel, n_row, n_sub), [smem] + [hbm] * 4 + [vmem] * 14, [vmem] * 3 + [hbm] * 4,
            [shape(ROWS, COLS)] * 3 + [shape(LEV, ROWS, COLS)] * 4,
            [extended] * 9 + [pltpu.VMEM((EXT, LANES), F32)] * 2 + [pltpu.VMEM((TILES, STRIPS, SUB, LANES), F32)] * 2
            + [column] * 4 + [whole] * 4 + [dma((4, TILES)), dma((4, TILES))],
        )(weights, wu, wv, wt, ws, eta, tu, tv, depth, wide_north, wide_south, wide_side,
          force, force_north, force_south, force_side, level_mean, counts, side_cols)

    cube = P(None, 'row', 'col')
    flat = P('row', 'col')
    return jax.shard_map(step, mesh=mesh, in_specs=(cube, cube, cube, cube, flat, flat, flat, flat, flat, P()),
                         out_specs=(flat, flat, flat, cube, cube, cube, cube), check_vma=False)
```

time: 1320 us -> 56 us (0.04); the launches traced: 1290 us -> 55.9 us
  other arithmetic: 812 us -> 0 us
  starting transfers between devices: 281 us -> 0 us
  waiting for transfers between devices: 109 us -> 0 us
  local copies, waits for them, and re-layouts: 87.7 us -> 0 us
  Pallas kernels: 0 us -> 55.2 us
    dynamic_update_slice x328 -> x0, other arithmetic: 559 us -> none  [tri_solve(): lax.scan(down, start, (low_links, up_links, right_side))]
    ppermute x143 -> x0, starting transfers between devices: 281 us -> none  [the longest x35 159 us: exchange(): from_south = lax.ppermute(wide[..., -1:, :], 'row', north_moves)]
    ppermute x143 -> x0, waiting for transfers between devices: 109 us -> none  [the longest x36 69.8 us: exchange(): from_east = lax.ppermute(field[..., :1], 'col', west_moves)]
    add x62 -> x0, other arithmetic: 83.5 us -> none  [the longest x30 26.5 us: subcycle(): acc_u + weight * trans_u_new]
    another operation x1 -> x0, other arithmetic: 72.7 us -> none  [ocean_columns(): jnp.cumsum(density, axis=0) - 0.5 * density]
    pallas_call x0 -> x2, Pallas kernels: none -> 55.2 us  [the longest x1 35.7 us: step(): call(functools.partial(step_kernel, n_row), [hbm] * 4 + [vmem] * 5, [hbm]...]
    sub x32 -> x0, other arithmetic: 38.3 us -> none  [the longest x2 31.6 us: advect(): tracer_mid - 0.5 * TIME_STEP * (flux_east - flux_west + flux_north - flux...]
    another operation x12 -> x0, local copies, waits for them, and re-layouts: 29.6 us -> none
  transfers between devices with their start and end apart: 143 -> 0, of which waited for: 91 -> 0; matrix products, arithmetic and copies ran while one was open for 63% -> 0% of each run, Pallas kernels for 0% -> 0%
where the time goes in v3:
time: 56 us; the launch traced here: 55.9 us
  Pallas kernels  55.2 us (99%)
  between operations  0.64 us (1%)
    pallas_call x1, Pallas kernels, step(): call(functools.partial(step_kernel, n_row), [hbm] * 4 + [vmem] * 5, [hbm]...  35.7 us
    pallas_call x1, Pallas kernels, step(): call(functools.partial(fast_kernel, n_row, n_sub), [smem] + [hbm] * 4 + [...  19.6 us

profile of v3, /device:TPU:0, one launch (start us, length us, event | category | flops | bytes accessed | tf_op | source)
XLA Modules:
  0.0 55.9 jit_solution(708611488228382367)
XLA Ops:
  0.6 35.7 %shard_map.153 = (f32[6,41,4,8,128]{4,3,2,1,0:T(8,128)}, f32[6,41,4,8,128]{4,3,2,1,0:T(8,128)}, f32[6,41,4,8,128]{4,3,2,1,0:T(8,128)}, f32[6,41,4,8,128]{4,3,2,1...) custom-call(f32[41,48,512]{2,1,0:T(8,128)} %u.1, ...), custom_call_target="tpu_custom_call" | custom-call | tf_op jit(solution)/shard_map/pallas_call | solution.py:665
  36.3 19.6 %shard_map.154 = (f32[48,512]{1,0:T(8,128)}, f32[48,512]{1,0:T(8,128)}, f32[48,512]{1,0:T(8,128)}, f32[41,48,512]{2,1,0:T(8,128)}, f32[41,48,512]{2,1,0:T(8,128)...) custom-call(f32[30]{0:T(128)} %weights.1, f32[6,41,4,8,128]{4,3,2,1,0:T(8,128)} %get-tuple-element.21.wu_in, ...), custom_call_target="tpu_custom_call" | custom-call | tf_op jit(solution)/shard_map/pallas_call | solution.py:675

commit v4 on v3

--- a/solution.py
+++ b/solution.py
@@ -119,136 +119,104 @@
     return mid, jnp.minimum(mid, east_stack(mid, edge, at_first)), jnp.minimum(mid, north)
 
 
-def unpack(packed, edges, rows):
+def unpack(packed, edges, f, rows):
     for k in range(LEV):
-        for f, side in enumerate(packed):
-            edges[f, k, rows, :] = pltpu.roll(side, LANES - 1 - 2 * k, 1)
+        edges[f, k, rows, :] = pltpu.roll(packed[f, rows, :], LANES - 1 - 2 * k, 1)
 
 
 def step_kernel(n_row, u, v, t, s, eta, tu, tv, depth, count,
                 wu_out, wv_out, wt_out, ws_out, force, level_mean, side_cols, counts,
                 wide_north, wide_south, wide_side, force_north, force_south, force_side,
-                u_s, v_s, t_s, s_s, one_s, two_s, edges, wu, wv, wt, ws, own_cols, fold, force_fold,
+                cube, one_s, two_s, edges, wu, wv, wt, ws, own_cols, fold, force_fold,
                 load_sem, send_sem, recv_sem, store_sem):
     at = places(n_row)
-    fields, strips = (u, v, t, s), (u_s, v_s, t_s, s_s)
+    fields = (u, v, t, s)
     four = range(STRIPS)
-    loads = [[pltpu.make_async_copy(fields[f].at[:, :, pl.ds(LANES * c, LANES)], strips[f].at[c, pl.ds(1, LEV), pl.ds(0, ROWS), :], load_sem.at[f, c])
-              for c in four] for f in four]
-    for c in (0, STRIPS - 1):
-        for f in four:
-            loads[f][c].start()
-    for c in range(1, STRIPS - 1):
-        for f in four:
-            loads[f][c].start()
+
+    def load(f, c, sem):
+        return pltpu.make_async_copy(fields[f].at[:, :, pl.ds(LANES * c, LANES)], cube.at[f, c, pl.ds(1, LEV), pl.ds(0, ROWS), :], sem)
+
+    outer = [[load(f, c, load_sem.at[2 * f + e]) for e, c in enumerate((0, STRIPS - 1))] for f in four]
+    inner_sem = load_sem.at[2 * STRIPS]
+    for pair in outer:
+        for copy in pair:
+            copy.start()
+    for f in four:
+        for c in range(1, STRIPS - 1):
+            load(f, c, inner_sem).start()
+    barrier = meet(at)
     lane = lane_index()
-    at_first, at_last = lane == 0, lane == LANES - 1
+    at_first = lane == 0
     zero = jnp.zeros((SUB, LANES), F32)
-
-    def clear_rows():
-        def body(k, _):
-            for strip in strips:
-                for c in four:
-                    strip[c, k, pl.ds(ROWS, SUB), :] = zero
-            return 0
-
-        lax.fori_loop(0, LEV + 1, body, 0)
-
-    @pl.when(jnp.logical_not(at['has_north']))
-    def _():
-        clear_rows()
-        counts[:, SUB + ROWS:, :] = jnp.zeros((STRIPS, SUB, LANES), F32)
-        side_cols[:, SUB + ROWS:, :] = jnp.zeros((STRIPS, SUB, LANES), F32)
-        wide_north[...] = jnp.zeros_like(wide_north)
-        force_north[...] = jnp.zeros_like(force_north)
-        wide_side[:, REACH + ROWS:, :] = jnp.zeros((STRIPS, REACH, LANES), F32)
-        force_side[:, REACH + ROWS:, :] = jnp.zeros((2, REACH, LANES), F32)
-
-    @pl.when(jnp.logical_not(at['has_south']))
-    def _():
-        clear_rows()
-        counts[:, :SUB, :] = jnp.zeros((STRIPS, SUB, LANES), F32)
-        side_cols[:, :SUB, :] = jnp.zeros((STRIPS, SUB, LANES), F32)
-        wide_south[...] = jnp.zeros_like(wide_south)
-        force_south[...] = jnp.zeros_like(force_south)
-        wide_side[:, :REACH, :] = jnp.zeros((STRIPS, REACH, LANES), F32)
-        force_side[:, :REACH, :] = jnp.zeros((2, REACH, LANES), F32)
-
+    line = jnp.zeros((1, LANES), F32)
     for c in four:
         counts[c, SUB:SUB + ROWS, :] = count[:, c * LANES:(c + 1) * LANES].astype(F32)
-    barrier = meet(at)
+    fast = (eta, tu, tv, depth)
+    low_half = lax.broadcasted_iota(jnp.int32, (ROWS, LANES), 1) < LANES // 2
+    for f in four:
+        fold[f] = jnp.where(low_half, fast[f][:, :LANES], fast[f][:, COLS - LANES:])
     await_meet(barrier, at)
     slot = iter(range(LANES))
 
-    def plan(bucket, src, dst, where):
+    def plan(where, region, *pairs):
         i = next(slot)
-        bucket.append(remote(src, dst, send_sem.at[i], recv_sem.at[i], at[where]))
+        copies = [remote(src, dst, send_sem.at[i], recv_sem.at[i], at[where]) for src, dst in pairs]
+        return copies, remote(region, region, send_sem.at[i], recv_sem.at[i], at[where])
+
+    def begin(plans):
+        for copies, _ in plans:
+            for copy in copies:
+                copy.start()
 
     def start(north, south, side=()):
-        @pl.when(at['has_north'])
-        def _():
-            for copy in north:
-                copy.start()
-
-        @pl.when(at['has_south'])
-        def _():
-            for copy in south:
-                copy.start()
-
-        for copy in side:
-            copy.start()
+        pl.when(at['has_north'])(lambda: begin(north))
+        pl.when(at['has_south'])(lambda: begin(south))
+        begin(side)
+
+    def received(plans):
+        for _, waiter in plans:
+            waiter.wait_recv()
+
+    def sent(plans):
+        for _, waiter in plans:
+            waiter.wait_send()
 
     def arrive(north, south, side=()):
-        for copy in side:
-            copy.wait_recv()
-
-        @pl.when(at['has_north'])
-        def _():
-            for copy in south:
-                copy.wait_recv()
-
-        @pl.when(at['has_south'])
-        def _():
-            for copy in north:
-                copy.wait_recv()
+        received(side)
+        pl.when(at['has_north'])(lambda: received(south))
+        pl.when(at['has_south'])(lambda: received(north))
 
     def leave(north, south, side=()):
-        for copy in side:
-            copy.wait_send()
-
-        @pl.when(at['has_north'])
-        def _():
-            for copy in north:
-                copy.wait_send()
-
-        @pl.when(at['has_south'])
-        def _():
-            for copy in south:
-                copy.wait_send()
-
-    rows_north, rows_south = [], []
+        sent(side)
+        pl.when(at['has_north'])(lambda: sent(north))
+        pl.when(at['has_south'])(lambda: sent(south))
+
+    def row_region(level, row):
+        return cube.at[:, :, pl.ds(level, LEV), pl.ds(row, 1), :]
+
+    def row_pairs(source, level, row):
+        return [(fields[f].at[:, pl.ds(source, 1), pl.ds(LANES * c, LANES)], cube.at[f, c, pl.ds(level, LEV), pl.ds(row, 1), :])
+                for f in four for c in four]
+
+    rows_north = [plan('north', row_region(0, PITCH - 1), *row_pairs(ROWS - 1, 0, PITCH - 1))]
+    rows_south = [plan('south', row_region(1, ROWS), *row_pairs(0, 1, ROWS))]
+    low_tile, high_tile = counts.at[:, pl.ds(0, SUB), :], counts.at[:, pl.ds(SUB + ROWS, SUB), :]
+    count_north = [plan('north', low_tile, (counts.at[:, pl.ds(ROWS, SUB), :], low_tile))]
+    count_south = [plan('south', high_tile, (counts.at[:, pl.ds(SUB, SUB), :], high_tile))]
+    start(count_north + rows_north, count_south + rows_south)
+
+    half_lane = lane >> 1
+    sides = []
     for f in four:
-        for c in four:
-            lanes = pl.ds(LANES * c, LANES)
-            plan(rows_north, fields[f].at[:, pl.ds(ROWS - 1, 1), lanes], strips[f].at[c, pl.ds(0, LEV), pl.ds(PITCH - 1, 1), :], 'north')
-            plan(rows_south, fields[f].at[:, pl.ds(0, 1), lanes], strips[f].at[c, pl.ds(1, LEV), pl.ds(ROWS, 1), :], 'south')
-    count_north, count_south = [], []
-    plan(count_north, counts.at[:, pl.ds(ROWS, SUB), :], counts.at[:, pl.ds(0, SUB), :], 'north')
-    plan(count_south, counts.at[:, pl.ds(SUB, SUB), :], counts.at[:, pl.ds(SUB + ROWS, SUB), :], 'south')
-    start(count_north + rows_north, count_south + rows_south)
-
-    half_lane = lane >> 1
-    sides, corner_north, corner_south = [], [], []
-    for f in four:
-        loads[f][0].wait()
-        loads[f][STRIPS - 1].wait()
+        for copy in outer[f]:
+            copy.wait()
 
         def pack(tile, _):
             rows = pl.ds(pl.multiple_of(SUB * tile, SUB), SUB)
             packed = zero
             for k in range(LEV + 1 if f == 0 else LEV):
                 if k < LEV:
-                    first, last = strips[f][0, k + 1, rows, :], strips[f][STRIPS - 1, k + 1, rows, :]
+                    first, last = cube[f, 0, k + 1, rows, :], cube[f, STRIPS - 1, k + 1, rows, :]
                 else:
                     lower = pl.ds(pl.multiple_of(SUB * tile + SUB, SUB), SUB)
                     first, last = counts[0, lower, :], counts[STRIPS - 1, lower, :]
@@ -258,53 +226,76 @@
             return 0
 
         lax.fori_loop(0, TILES, pack, 0)
-        plan(sides, own_cols.at[f], side_cols.at[f, pl.ds(SUB, ROWS), :], 'side')
-        sides[-1].start()
-        if f == 0:
-            plan(corner_south, own_cols.at[f, pl.ds(0, SUB), :], side_cols.at[f, pl.ds(SUB + ROWS, SUB), :], 'south_side')
-        if f == 1:
-            plan(corner_north, own_cols.at[f, pl.ds(ROWS - SUB, SUB), :], side_cols.at[f, pl.ds(0, SUB), :], 'north_side')
+        target = side_cols.at[f, pl.ds(SUB, ROWS), :]
+        sides.append(plan('side', target, (own_cols.at[f], target)))
+        begin(sides[-1:])
+    high_u, low_v = side_cols.at[0, pl.ds(SUB + ROWS, SUB), :], side_cols.at[1, pl.ds(0, SUB), :]
+    corner_south = [plan('south_side', high_u, (own_cols.at[0, pl.ds(0, SUB), :], high_u))]
+    corner_north = [plan('north_side', low_v, (own_cols.at[1, pl.ds(ROWS - SUB, SUB), :], low_v))]
     start(corner_north, corner_south)
 
-    fast = (eta, tu, tv, depth)
-    low_half = lax.broadcasted_iota(jnp.int32, (ROWS, LANES), 1) < LANES // 2
-    for f in four:
-        fold[f] = jnp.where(low_half, fast[f][:, :LANES], fast[f][:, COLS - LANES:])
-    wide_up, wide_down, wide_across = [], [], []
-    for f in four:
-        plan(wide_up, fast[f].at[pl.ds(ROWS - REACH, REACH), :], wide_south.at[f], 'north')
-        plan(wide_down, fast[f].at[pl.ds(0, REACH), :], wide_north.at[f], 'south')
-    plan(wide_up, fold.at[:, pl.ds(ROWS - REACH, REACH), :], wide_side.at[:, pl.ds(0, REACH), :], 'north_side')
-    plan(wide_down, fold.at[:, pl.ds(0, REACH), :], wide_side.at[:, pl.ds(REACH + ROWS, REACH), :], 'south_side')
-    plan(wide_across, fold, wide_side.at[:, pl.ds(REACH, ROWS), :], 'side')
+    def clear(level, row):
+        def body(k, _):
+            for f in four:
+                for c in four:
+                    cube[f, c, k + level, pl.ds(row, 1), :] = line
+            return 0
+
+        lax.fori_loop(0, LEV, body, 0)
+
+    @pl.when(jnp.logical_not(at['has_north']))
+    def _():
+        clear(1, ROWS)
+        counts[:, SUB + ROWS:, :] = jnp.zeros((STRIPS, SUB, LANES), F32)
+        side_cols[:, SUB + ROWS:, :] = jnp.zeros((STRIPS, SUB, LANES), F32)
+        wide_north[...] = jnp.zeros_like(wide_north)
+        force_north[...] = jnp.zeros_like(force_north)
+        wide_side[:, REACH + ROWS:, :] = jnp.zeros((STRIPS, REACH, LANES), F32)
+        force_side[:, REACH + ROWS:, :] = jnp.zeros((2, REACH, LANES), F32)
+
+    @pl.when(jnp.logical_not(at['has_south']))
+    def _():
+        clear(0, PITCH - 1)
+        counts[:, :SUB, :] = jnp.zeros((STRIPS, SUB, LANES), F32)
+        side_cols[:, :SUB, :] = jnp.zeros((STRIPS, SUB, LANES), F32)
+        wide_south[...] = jnp.zeros_like(wide_south)
+        force_south[...] = jnp.zeros_like(force_south)
+        wide_side[:, :REACH, :] = jnp.zeros((STRIPS, REACH, LANES), F32)
+        force_side[:, :REACH, :] = jnp.zeros((2, REACH, LANES), F32)
 
     half_scale = 0.5 * BC_GRAVITY / LEV
     scale = 0.5 * TIME_STEP
-    half = half_lane.astype(F32)
 
     def density(sal, tem):
         return (half_scale * CONTRACT_S) * sal - (half_scale * EXPAND_T) * tem
 
-    arrive(count_north + corner_north, count_south + corner_south, sides)
-
-    def spread(tile, _):
-        rows = pl.ds(pl.multiple_of(SUB * tile, SUB), SUB)
-        mid_rows = pl.ds(SUB * tile + SUB, SUB)
-        side = [side_cols[f, mid_rows, :] for f in four]
-        west_count = jnp.minimum(side[0][:, 2 * LEV:2 * LEV + 1], counts[0, mid_rows, :][:, 0:1])
-        unpack((side[0], side[1], side[1] + side_cols[1, pl.ds(SUB * tile + SUB - 1, SUB), :], density(side[3], side[2]),
-                side[2], side[3], jnp.where(half < west_count, scale * side[0], 0.0)), edges, rows)
-        return 0
-
-    lax.fori_loop(0, TILES + 1, spread, 0)
-    for c in range(1, STRIPS - 1):
-        for f in four:
-            loads[f][c].wait()
+    for f in four:
+        received(sides[f:f + 1])
+
+        def spread(tile, _):
+            unpack(side_cols, edges, f, pl.ds(pl.multiple_of(SUB * tile, SUB), SUB))
+            return 0
+
+        lax.fori_loop(1, TILES + 1, spread, 0)
+    arrive(count_north + corner_north, count_south + corner_south)
+    unpack(side_cols, edges, 0, pl.ds(SUB + ROWS, SUB))
+    unpack(side_cols, edges, 1, pl.ds(0, SUB))
+    pltpu.make_async_copy(cube.at[:, pl.ds(1, STRIPS - 2), pl.ds(1, LEV), pl.ds(0, ROWS), :],
+                          cube.at[:, pl.ds(1, STRIPS - 2), pl.ds(1, LEV), pl.ds(0, ROWS), :], inner_sem).wait()
     arrive(rows_north, rows_south)
     leave(rows_north, rows_south)
+    low_rows, high_rows = pl.ds(0, REACH), pl.ds(ROWS - REACH, REACH)
+    side_low, side_high = wide_side.at[:, low_rows, :], wide_side.at[:, pl.ds(REACH + ROWS, REACH), :]
+    side_mid = wide_side.at[:, pl.ds(REACH, ROWS), :]
+    wide_up = [plan('north', wide_south, *[(fast[f].at[high_rows, :], wide_south.at[f]) for f in four]),
+               plan('north_side', side_low, (fold.at[:, high_rows, :], side_low))]
+    wide_down = [plan('south', wide_north, *[(fast[f].at[low_rows, :], wide_north.at[f]) for f in four]),
+                 plan('south_side', side_high, (fold.at[:, low_rows, :], side_high))]
+    wide_across = [plan('side', side_mid, (fold, side_mid))]
     start(wide_up, wide_down, wide_across)
-    flats = [ref.reshape(STRIPS, (LEV + 1) * PITCH, LANES) for ref in (u_s, v_s, t_s, s_s, one_s, two_s)]
-    uf, vf, tf, sf, pf, bf = flats
+    rows_flat = (LEV + 1) * PITCH
+    uf, vf, tf, sf = [cube.at[f].reshape(STRIPS, rows_flat, LANES) for f in four]
+    pf, bf = [ref.reshape(STRIPS, rows_flat, LANES) for ref in (one_s, two_s)]
     stack = lax.broadcasted_iota(jnp.int32, (STRIPS, SUB, LANES), 2)
     first_lanes, last_lanes = stack == 0, stack == LANES - 1
     none = jnp.zeros((STRIPS, SUB, LANES), F32)
@@ -313,7 +304,7 @@
     for k in range(LEV):
         spot = level_rows(TILES, k)
         uu = uf[:, spot, :]
-        bf[:, spot, :] = uu + west_stack(uu, edges[0, k, pl.ds(ROWS, SUB), :], last_lanes)
+        bf[:, spot, :] = uu + west_stack(uu, edges[0, k, pl.ds(SUB + ROWS, SUB), :], last_lanes)
         rho = density(sf[:, spot, :], tf[:, spot, :])
         pf[:, spot, :] = acc + rho
         acc = (acc + rho) + rho
@@ -325,20 +316,21 @@
         fu = 0.25 * (CORIO_F0 + CORIO_BETA * ((row_pos + 0.5) / (ROWS * n_row) - 0.5))
         fv = 0.25 * (CORIO_F0 + CORIO_BETA * ((row_pos + 1.0) / (ROWS * n_row) - 0.5))
         out_rows = pl.ds(pl.multiple_of(SUB * tile, SUB), SUB)
+        mid_rows = pl.ds(pl.multiple_of(SUB * tile + SUB, SUB), SUB)
         acc, acc_e = none, zero
         xu, xv, sum_du, sum_dv, sum_su, sum_sv = (none,) * 6
         for k in range(LEV):
             here, up, below = [level_rows(tile, k, step) for step in (0, 1, -1)]
             uu, vv = uf[:, here, :], vf[:, here, :]
             v_south = vf[:, below, :]
-            edge_u, edge_v = edges[0, k, out_rows, :], edges[1, k, out_rows, :]
+            edge_u, edge_v = edges[0, k, mid_rows, :], edges[1, k, mid_rows, :]
             u_west = west_stack(uu, edge_u, last_lanes)
             u_east = east_stack(uu, edge_u, first_lanes)
             v_west = west_stack(vv, edge_v, last_lanes)
             v_east = east_stack(vv, edge_v, first_lanes)
             pair_v = vv + v_south
-            pair_ve = east_stack(pair_v, edges[2, k, out_rows, :], first_lanes)
-            rho_e = edges[3, k, out_rows, :]
+            pair_ve = east_stack(pair_v, edge_v + edges[1, k, pl.ds(SUB * tile + SUB - 1, SUB), :], first_lanes)
+            rho_e = density(edges[3, k, mid_rows, :], edges[2, k, mid_rows, :])
             p_edge = acc_e + rho_e
             acc_e = p_edge + rho_e
             rho = density(sf[:, here, :], tf[:, here, :])
@@ -370,21 +362,21 @@
             force[1, out_rows, lanes] = (sum_dv * inv_v)[c]
             level_mean[0, out_rows, lanes] = (sum_su * inv_u)[c]
             level_mean[1, out_rows, lanes] = (sum_sv * inv_v)[c]
-        pltpu.make_async_copy(wu.at[tile], wu_out.at[tile], store_sem.at[0, tile]).start()
-        pltpu.make_async_copy(wv.at[tile], wv_out.at[tile], store_sem.at[1, tile]).start()
+        pltpu.make_async_copy(wu.at[tile], wu_out.at[tile], store_sem.at[0]).start()
+        pltpu.make_async_copy(wv.at[tile], wv_out.at[tile], store_sem.at[1]).start()
         return 0
 
     lax.fori_loop(0, TILES, momentum, 0)
 
-    low_half = lax.broadcasted_iota(jnp.int32, (ROWS, LANES), 1) < LANES // 2
     for f in range(2):
         force_fold[f] = jnp.where(low_half, force[f, :, :LANES], force[f, :, COLS - LANES:])
-    force_up, force_down, force_across = [], [], []
-    plan(force_up, force.at[:, pl.ds(ROWS - REACH, REACH), :], force_south, 'north')
-    plan(force_up, force_fold.at[:, pl.ds(ROWS - REACH, REACH), :], force_side.at[:, pl.ds(0, REACH), :], 'north_side')
-    plan(force_down, force.at[:, pl.ds(0, REACH), :], force_north, 'south')
-    plan(force_down, force_fold.at[:, pl.ds(0, REACH), :], force_side.at[:, pl.ds(REACH + ROWS, REACH), :], 'south_side')
-    plan(force_across, force_fold, force_side.at[:, pl.ds(REACH, ROWS), :], 'side')
+    side_low, side_high = force_side.at[:, low_rows, :], force_side.at[:, pl.ds(REACH + ROWS, REACH), :]
+    side_mid = force_side.at[:, pl.ds(REACH, ROWS), :]
+    force_up = [plan('north', force_south, (force.at[:, high_rows, :], force_south)),
+                plan('north_side', side_low, (force_fold.at[:, high_rows, :], side_low))]
+    force_down = [plan('south', force_north, (force.at[:, low_rows, :], force_north)),
+                  plan('south_side', side_high, (force_fold.at[:, low_rows, :], side_high))]
+    force_across = [plan('side', side_mid, (force_fold, side_mid))]
     start(force_up, force_down, force_across)
 
     ftf, fsf = pf, bf
@@ -400,17 +392,19 @@
     def tracers(tile, _):
         mid, nu, nv = face_counts(counts, side_cols, tile)
         out_rows = pl.ds(pl.multiple_of(SUB * tile, SUB), SUB)
+        mid_rows = pl.ds(pl.multiple_of(SUB * tile + SUB, SUB), SUB)
+        west_count = jnp.minimum(pltpu.roll(side_cols[0, mid_rows, :], LANES - 1 - 2 * LEV, 1), pltpu.roll(counts[0, mid_rows, :], LANES - 1, 1))
         xt, xs = none, none
         for k in range(LEV):
             here, up, below = [level_rows(tile, k, step) for step in (0, 1, -1)]
             hu = jnp.where(nu > k, scale * uf[:, here, :], 0.0)
             hv = jnp.where(nv > k, scale * vf[:, here, :], 0.0)
-            hw = west_stack(hu, edges[6, k, out_rows, :], last_lanes)
+            hw = west_stack(hu, jnp.where(west_count > k, scale * edges[0, k, mid_rows, :], 0.0), last_lanes)
             inverse = jnp.where(mid > k + 1, 1.0 / pivot[k], 1.0 / final[k]) if k < LEV - 1 else 1.0 / final[k]
 
             def advance(flat, flux, which, x, w):
                 q = flat[:, here, :]
-                edge = edges[which, k, out_rows, :]
+                edge = edges[which, k, mid_rows, :]
                 flux_e = hu * (q + east_stack(q, edge, first_lanes))
                 flux_w = hw * (q + west_stack(q, edge, last_lanes))
                 flux_n = hv * (q + flat[:, up, :])
@@ -420,16 +414,15 @@
                 w[tile, k] = jnp.where(mid > k, x, new)
                 return x
 
-            xt = advance(tf, ftf, 4, xt, wt)
-            xs = advance(sf, fsf, 5, xs, ws)
-        pltpu.make_async_copy(wt.at[tile], wt_out.at[tile], store_sem.at[2, tile]).start()
-        pltpu.make_async_copy(ws.at[tile], ws_out.at[tile], store_sem.at[3, tile]).start()
+            xt = advance(tf, ftf, 2, xt, wt)
+            xs = advance(sf, fsf, 3, xs, ws)
+        pltpu.make_async_copy(wt.at[tile], wt_out.at[tile], store_sem.at[2]).start()
+        pltpu.make_async_copy(ws.at[tile], ws_out.at[tile], store_sem.at[3]).start()
         return 0
 
     lax.fori_loop(0, TILES, tracers, 0)
-    for tile in range(TILES):
-        for i, (src, dst) in enumerate(((wu, wu_out), (wv, wv_out), (wt, wt_out), (ws, ws_out))):
-            pltpu.make_async_copy(src.at[tile], dst.at[tile], store_sem.at[i, tile]).wait()
+    for i, (src, dst) in enumerate(((wu, wu_out), (wv, wv_out), (wt, wt_out), (ws, ws_out))):
+        pltpu.make_async_copy(src, dst, store_sem.at[i]).wait()
     leave(count_north + corner_north, count_south + corner_south, sides)
     for group in ((wide_up, wide_down, wide_across), (force_up, force_down, force_across)):
         arrive(*group)
@@ -668,9 +661,9 @@
             + [shape(4, ROWS + 2 * SUB, LANES), shape(STRIPS, ROWS + 2 * SUB, LANES)]
             + [shape(4, REACH, COLS), shape(4, REACH, COLS), shape(4, EXT, LANES)]
             + [shape(2, REACH, COLS), shape(2, REACH, COLS), shape(2, EXT, LANES)],
-            [strip] * 6 + [pltpu.VMEM((7, LEV, ROWS + SUB, LANES), F32)] + [column] * 4
+            [pltpu.VMEM((4, STRIPS, LEV + 1, PITCH, LANES), F32)] + [strip] * 2 + [pltpu.VMEM((4, LEV, ROWS + 2 * SUB, LANES), F32)] + [column] * 4
             + [pltpu.VMEM((4, ROWS, LANES), F32)] * 2 + [pltpu.VMEM((2, ROWS, LANES), F32)]
-            + [dma((4, STRIPS)), dma((64,)), dma((64,)), dma((4, TILES))],
+            + [dma((9,)), dma((20,)), dma((20,)), dma((4,))],
             collective_id=0, has_side_effects=True)(vel_u, vel_v, temp, salt, eta, tu, tv, depth, count)
         return call(
             functools.partial(fast_kernel, n_row, n_sub), [smem] + [hbm] * 4 + [vmem] * 14, [vmem] * 3 + [hbm] * 4,

time: 56 us -> 52.8 us (0.943)
  Pallas kernels: 55.2 us -> 51.9 us
    pallas_call x1, Pallas kernels: 35.7 us -> 32.4 us  [step(): call(functools.partial(step_kernel, n_row), [hbm] * 4 + [vmem] * 5, [hbm]...]
where the time goes in v4:
time: 52.8 us; the launch traced here: 52.6 us
  Pallas kernels  51.9 us (98%)
  between operations  0.64 us (1%)
    pallas_call x1, Pallas kernels, step(): call(functools.partial(step_kernel, n_row), [hbm] * 4 + [vmem] * 5, [hbm]...  32.4 us
    pallas_call x1, Pallas kernels, step(): call(functools.partial(fast_kernel, n_row, n_sub), [smem] + [hbm] * 4 + [...  19.6 us

profile of v4, /device:TPU:0, one launch (start us, length us, event | category | flops | bytes accessed | tf_op | source)
XLA Modules:
  0.0 52.6 jit_solution(331049153163469955)
XLA Ops:
  0.6 32.4 %shard_map.153 = (f32[6,41,4,8,128]{4,3,2,1,0:T(8,128)}, f32[6,41,4,8,128]{4,3,2,1,0:T(8,128)}, f32[6,41,4,8,128]{4,3,2,1,0:T(8,128)}, f32[6,41,4,8,128]{4,3,2,1...) custom-call(f32[41,48,512]{2,1,0:T(8,128)} %u.1, ...), custom_call_target="tpu_custom_call" | custom-call | tf_op jit(solution)/shard_map/pallas_call | solution.py:658
  33.0 19.6 %shard_map.154 = (f32[48,512]{1,0:T(8,128)}, f32[48,512]{1,0:T(8,128)}, f32[48,512]{1,0:T(8,128)}, f32[41,48,512]{2,1,0:T(8,128)}, f32[41,48,512]{2,1,0:T(8,128)...) custom-call(f32[30]{0:T(128)} %weights.1, f32[6,41,4,8,128]{4,3,2,1,0:T(8,128)} %get-tuple-element.21.wu_in, ...), custom_call_target="tpu_custom_call" | custom-call | tf_op jit(solution)/shard_map/pallas_call | solution.py:668

commit v5 on v4

--- a/solution.py
+++ b/solution.py
@@ -110,11 +110,11 @@
     return pltpu.roll(jnp.where(at_first, jnp.concatenate([strips[1:], edge[None]], axis=0), strips), LANES - 1, 2)
 
 
-def face_counts(counts, side_cols, tile):
+def face_counts(counts, side, tile):
     rows = SUB * tile + SUB
     mid = counts[:, pl.ds(rows, SUB), :]
     north = counts[:, pl.ds(rows + 1, SUB), :]
-    edge = pltpu.roll(side_cols[0, pl.ds(rows, SUB), :], LANES - 1 - 2 * LEV, 1)
+    edge = pltpu.roll(side[pl.ds(rows, SUB), :], LANES - 1 - 2 * LEV, 1)
     at_first = lax.broadcasted_iota(jnp.int32, mid.shape, 2) == 0
     return mid, jnp.minimum(mid, east_stack(mid, edge, at_first)), jnp.minimum(mid, north)
 
@@ -125,9 +125,10 @@
 
 
 def step_kernel(n_row, u, v, t, s, eta, tu, tv, depth, count,
-                wu_out, wv_out, wt_out, ws_out, force, level_mean, side_cols, counts,
+                wu_out, wv_out, wt_out, ws_out, force_out, mean_out, side_out, counts_out,
                 wide_north, wide_south, wide_side, force_north, force_south, force_side,
-                cube, one_s, two_s, edges, wu, wv, wt, ws, own_cols, fold, force_fold,
+                cube, one_s, two_s, slope, edges, wu, wv, wt, ws, own_cols, fold, force_fold,
+                flat_in, count_in, force, level_mean, side_cols, counts, blank,
                 load_sem, send_sem, recv_sem, store_sem):
     at = places(n_row)
     fields = (u, v, t, s)
@@ -137,24 +138,25 @@
         return pltpu.make_async_copy(fields[f].at[:, :, pl.ds(LANES * c, LANES)], cube.at[f, c, pl.ds(1, LEV), pl.ds(0, ROWS), :], sem)
 
     outer = [[load(f, c, load_sem.at[2 * f + e]) for e, c in enumerate((0, STRIPS - 1))] for f in four]
-    inner_sem = load_sem.at[2 * STRIPS]
+    inner_sem, flat_sem, count_sem = load_sem.at[9], load_sem.at[10], load_sem.at[11]
+    fetch_count = pltpu.make_async_copy(count, count_in, count_sem)
+    fetch_count.start()
     for pair in outer:
         for copy in pair:
             copy.start()
-    for f in four:
+    for f in (2, 3, 0, 1):
         for c in range(1, STRIPS - 1):
-            load(f, c, inner_sem).start()
+            load(f, c, load_sem.at[8 + (f < 2)]).start()
+    for f, src in enumerate((eta, tu, tv, depth)):
+        pltpu.make_async_copy(src, flat_in.at[f], flat_sem).start()
     barrier = meet(at)
     lane = lane_index()
-    at_first = lane == 0
+    at_first, at_last = lane == 0, lane == LANES - 1
     zero = jnp.zeros((SUB, LANES), F32)
     line = jnp.zeros((1, LANES), F32)
+    fetch_count.wait()
     for c in four:
-        counts[c, SUB:SUB + ROWS, :] = count[:, c * LANES:(c + 1) * LANES].astype(F32)
-    fast = (eta, tu, tv, depth)
-    low_half = lax.broadcasted_iota(jnp.int32, (ROWS, LANES), 1) < LANES // 2
-    for f in four:
-        fold[f] = jnp.where(low_half, fast[f][:, :LANES], fast[f][:, COLS - LANES:])
+        counts[c, SUB:SUB + ROWS, :] = count_in[:, c * LANES:(c + 1) * LANES].astype(F32)
     await_meet(barrier, at)
     slot = iter(range(LANES))
 
@@ -243,25 +245,32 @@
 
         lax.fori_loop(0, LEV, body, 0)
 
+    narrow = blank.at[:, :, pl.ds(0, LANES)]
+    pair = pl.ds(0, 2)
+    low_rows, high_rows = pl.ds(0, REACH), pl.ds(ROWS - REACH, REACH)
+    far_rows = pl.ds(REACH + ROWS, REACH)
+
+    def blanks(wide, forced, rows):
+        targets = ((blank, wide), (narrow, wide_side.at[:, rows, :]), (blank.at[pair], forced), (blank.at[pair, :, pl.ds(0, LANES)], force_side.at[:, rows, :]))
+        return [pltpu.make_async_copy(src, dst, load_sem.at[12 + i]) for i, (src, dst) in enumerate(targets)]
+
     @pl.when(jnp.logical_not(at['has_north']))
     def _():
         clear(1, ROWS)
         counts[:, SUB + ROWS:, :] = jnp.zeros((STRIPS, SUB, LANES), F32)
         side_cols[:, SUB + ROWS:, :] = jnp.zeros((STRIPS, SUB, LANES), F32)
-        wide_north[...] = jnp.zeros_like(wide_north)
-        force_north[...] = jnp.zeros_like(force_north)
-        wide_side[:, REACH + ROWS:, :] = jnp.zeros((STRIPS, REACH, LANES), F32)
-        force_side[:, REACH + ROWS:, :] = jnp.zeros((2, REACH, LANES), F32)
+        blank[...] = jnp.zeros_like(blank)
+        for copy in blanks(wide_north, force_north, far_rows):
+            copy.start()
 
     @pl.when(jnp.logical_not(at['has_south']))
     def _():
         clear(0, PITCH - 1)
         counts[:, :SUB, :] = jnp.zeros((STRIPS, SUB, LANES), F32)
         side_cols[:, :SUB, :] = jnp.zeros((STRIPS, SUB, LANES), F32)
-        wide_south[...] = jnp.zeros_like(wide_south)
-        force_south[...] = jnp.zeros_like(force_south)
-        wide_side[:, :REACH, :] = jnp.zeros((STRIPS, REACH, LANES), F32)
-        force_side[:, :REACH, :] = jnp.zeros((2, REACH, LANES), F32)
+        blank[...] = jnp.zeros_like(blank)
+        for copy in blanks(wide_south, force_south, low_rows):
+            copy.start()
 
     half_scale = 0.5 * BC_GRAVITY / LEV
     scale = 0.5 * TIME_STEP
@@ -269,36 +278,57 @@
     def density(sal, tem):
         return (half_scale * CONTRACT_S) * sal - (half_scale * EXPAND_T) * tem
 
-    for f in four:
-        received(sides[f:f + 1])
-
-        def spread(tile, _):
-            unpack(side_cols, edges, f, pl.ds(pl.multiple_of(SUB * tile, SUB), SUB))
-            return 0
-
-        lax.fori_loop(1, TILES + 1, spread, 0)
-    arrive(count_north + corner_north, count_south + corner_south)
-    unpack(side_cols, edges, 0, pl.ds(SUB + ROWS, SUB))
-    unpack(side_cols, edges, 1, pl.ds(0, SUB))
-    pltpu.make_async_copy(cube.at[:, pl.ds(1, STRIPS - 2), pl.ds(1, LEV), pl.ds(0, ROWS), :],
-                          cube.at[:, pl.ds(1, STRIPS - 2), pl.ds(1, LEV), pl.ds(0, ROWS), :], inner_sem).wait()
-    arrive(rows_north, rows_south)
-    leave(rows_north, rows_south)
-    low_rows, high_rows = pl.ds(0, REACH), pl.ds(ROWS - REACH, REACH)
-    side_low, side_high = wide_side.at[:, low_rows, :], wide_side.at[:, pl.ds(REACH + ROWS, REACH), :]
-    side_mid = wide_side.at[:, pl.ds(REACH, ROWS), :]
-    wide_up = [plan('north', wide_south, *[(fast[f].at[high_rows, :], wide_south.at[f]) for f in four]),
-               plan('north_side', side_low, (fold.at[:, high_rows, :], side_low))]
-    wide_down = [plan('south', wide_north, *[(fast[f].at[low_rows, :], wide_north.at[f]) for f in four]),
-                 plan('south_side', side_high, (fold.at[:, low_rows, :], side_high))]
-    wide_across = [plan('side', side_mid, (fold, side_mid))]
-    start(wide_up, wide_down, wide_across)
+    def interior(f, sem):
+        region = cube.at[pl.ds(f, 2), pl.ds(1, STRIPS - 2), pl.ds(1, LEV), pl.ds(0, ROWS), :]
+        return pltpu.make_async_copy(region, region, sem)
+
     rows_flat = (LEV + 1) * PITCH
     uf, vf, tf, sf = [cube.at[f].reshape(STRIPS, rows_flat, LANES) for f in four]
     pf, bf = [ref.reshape(STRIPS, rows_flat, LANES) for ref in (one_s, two_s)]
     stack = lax.broadcasted_iota(jnp.int32, (STRIPS, SUB, LANES), 2)
     first_lanes, last_lanes = stack == 0, stack == LANES - 1
     none = jnp.zeros((STRIPS, SUB, LANES), F32)
+    interior(2, load_sem.at[8]).wait()
+
+    def pressure(tile, _):
+        acc = none
+        for k in range(LEV):
+            here = level_rows(tile, k)
+            rho = density(sf[:, here, :], tf[:, here, :])
+            pp = acc + rho
+            acc = pp + rho
+            pf[:, here, :] = pp
+            slope[tile, k] = pp - east_stack(pp, zero, first_lanes)
+        return 0
+
+    lax.fori_loop(0, TILES, pressure, 0)
+
+    for f in four:
+        received(sides[f:f + 1])
+
+        def spread(tile, _):
+            unpack(side_cols, edges, f, pl.ds(pl.multiple_of(SUB * tile, SUB), SUB))
+            return 0
+
+        lax.fori_loop(1, TILES + 1, spread, 0)
+    arrive(count_north + corner_north, count_south + corner_south)
+    unpack(side_cols, edges, 0, pl.ds(SUB + ROWS, SUB))
+    unpack(side_cols, edges, 1, pl.ds(0, SUB))
+    interior(0, inner_sem).wait()
+    low_half = lax.broadcasted_iota(jnp.int32, (ROWS, LANES), 1) < LANES // 2
+    pltpu.make_async_copy(flat_in, flat_in, flat_sem).wait()
+    for f in four:
+        fold[f] = jnp.where(low_half, flat_in[f, :, :LANES], flat_in[f, :, COLS - LANES:])
+    arrive(rows_north, rows_south)
+    leave(rows_north, rows_south)
+    side_low, side_high = wide_side.at[:, low_rows, :], wide_side.at[:, far_rows, :]
+    side_mid = wide_side.at[:, pl.ds(REACH, ROWS), :]
+    wide_up = [plan('north', wide_south, (flat_in.at[:, high_rows, :], wide_south)),
+               plan('north_side', side_low, (fold.at[:, high_rows, :], side_low))]
+    wide_down = [plan('south', wide_north, (flat_in.at[:, low_rows, :], wide_north)),
+                 plan('south_side', side_high, (fold.at[:, low_rows, :], side_high))]
+    wide_across = [plan('side', side_mid, (fold, side_mid))]
+    start(wide_up, wide_down, wide_across)
     pivot, _ = tables(VISC_R)
     acc = none
     for k in range(LEV):
@@ -311,13 +341,13 @@
 
     def momentum(step, _):
         tile = TILES - 1 - step
-        _, nu, nv = face_counts(counts, side_cols, tile)
+        _, nu, nv = face_counts(counts, side_cols.at[0], tile)
         row_pos = (at['row'] * ROWS + SUB * tile + lax.broadcasted_iota(jnp.int32, (STRIPS, SUB, LANES), 1)).astype(F32)
         fu = 0.25 * (CORIO_F0 + CORIO_BETA * ((row_pos + 0.5) / (ROWS * n_row) - 0.5))
         fv = 0.25 * (CORIO_F0 + CORIO_BETA * ((row_pos + 1.0) / (ROWS * n_row) - 0.5))
         out_rows = pl.ds(pl.multiple_of(SUB * tile, SUB), SUB)
         mid_rows = pl.ds(pl.multiple_of(SUB * tile + SUB, SUB), SUB)
-        acc, acc_e = none, zero
+        acc_e = zero
         xu, xv, sum_du, sum_dv, sum_su, sum_sv = (none,) * 6
         for k in range(LEV):
             here, up, below = [level_rows(tile, k, step) for step in (0, 1, -1)]
@@ -330,19 +360,17 @@
             v_east = east_stack(vv, edge_v, first_lanes)
             pair_v = vv + v_south
             pair_ve = east_stack(pair_v, edge_v + edges[1, k, pl.ds(SUB * tile + SUB - 1, SUB), :], first_lanes)
-            rho_e = density(edges[3, k, mid_rows, :], edges[2, k, mid_rows, :])
+            rho_e = pltpu.roll(density(edges[3, k, mid_rows, :], edges[2, k, mid_rows, :]), LANES - 1, 1)
             p_edge = acc_e + rho_e
             acc_e = p_edge + rho_e
-            rho = density(sf[:, here, :], tf[:, here, :])
-            pp = acc + rho
-            acc = pp + rho
-            pf[:, here, :] = pp
-            p_east = east_stack(pp, p_edge, first_lanes)
+            pp = pf[:, here, :]
+            fall = slope[tile, k]
+            fall = jnp.concatenate([fall[:-1], jnp.where(at_last, pp[-1] - p_edge, fall[-1])[None]], axis=0)
             pair_u = uu + u_west
             bf[:, here, :] = pair_u
             v4 = pair_v + pair_ve
             u4 = pair_u + bf[:, up, :]
-            du = v4 * (fu - 0.125 * (uf[:, up, :] - uf[:, below, :])) - 0.5 * uu * (u_east - u_west) + (pp - p_east)
+            du = v4 * (fu - 0.125 * (uf[:, up, :] - uf[:, below, :])) - 0.5 * uu * (u_east - u_west) + fall
             dv = (pp - pf[:, up, :]) - u4 * (fv + 0.125 * (v_east - v_west)) - 0.5 * vv * (vf[:, up, :] - v_south)
             us, vs = uu + du, vv + dv
             on_u, on_v = nu > k, nv > k
@@ -370,7 +398,7 @@
 
     for f in range(2):
         force_fold[f] = jnp.where(low_half, force[f, :, :LANES], force[f, :, COLS - LANES:])
-    side_low, side_high = force_side.at[:, low_rows, :], force_side.at[:, pl.ds(REACH + ROWS, REACH), :]
+    side_low, side_high = force_side.at[:, low_rows, :], force_side.at[:, far_rows, :]
     side_mid = force_side.at[:, pl.ds(REACH, ROWS), :]
     force_up = [plan('north', force_south, (force.at[:, high_rows, :], force_south)),
                 plan('north_side', side_low, (force_fold.at[:, high_rows, :], side_low))]
@@ -378,6 +406,10 @@
                   plan('south_side', side_high, (force_fold.at[:, low_rows, :], side_high))]
     force_across = [plan('side', side_mid, (force_fold, side_mid))]
     start(force_up, force_down, force_across)
+    extras = [pltpu.make_async_copy(src, dst, store_sem.at[4 + i])
+              for i, (src, dst) in enumerate(((force, force_out), (level_mean, mean_out), (side_cols.at[0], side_out), (counts, counts_out)))]
+    for copy in extras:
+        copy.start()
 
     ftf, fsf = pf, bf
     pivot, final = tables(DIFF_R)
@@ -390,7 +422,7 @@
         fsf[:, here, :] = hv * (sf[:, here, :] + sf[:, up, :])
 
     def tracers(tile, _):
-        mid, nu, nv = face_counts(counts, side_cols, tile)
+        mid, nu, nv = face_counts(counts, side_cols.at[0], tile)
         out_rows = pl.ds(pl.multiple_of(SUB * tile, SUB), SUB)
         mid_rows = pl.ds(pl.multiple_of(SUB * tile + SUB, SUB), SUB)
         west_count = jnp.minimum(pltpu.roll(side_cols[0, mid_rows, :], LANES - 1 - 2 * LEV, 1), pltpu.roll(counts[0, mid_rows, :], LANES - 1, 1))
@@ -423,10 +455,22 @@
     lax.fori_loop(0, TILES, tracers, 0)
     for i, (src, dst) in enumerate(((wu, wu_out), (wv, wv_out), (wt, wt_out), (ws, ws_out))):
         pltpu.make_async_copy(src, dst, store_sem.at[i]).wait()
+    for copy in extras:
+        copy.wait()
     leave(count_north + corner_north, count_south + corner_south, sides)
     for group in ((wide_up, wide_down, wide_across), (force_up, force_down, force_across)):
         arrive(*group)
         leave(*group)
+
+    @pl.when(jnp.logical_not(at['has_north']))
+    def _():
+        for copy in blanks(wide_north, force_north, far_rows):
+            copy.wait()
+
+    @pl.when(jnp.logical_not(at['has_south']))
+    def _():
+        for copy in blanks(wide_south, force_south, low_rows):
+            copy.wait()
 
 
 def fast_kernel(n_row, n_sub, weights, wu_in, wv_in, wt_in, ws_in, eta, tu, tv, depth, wide_north, wide_south, wide_side,
@@ -656,14 +700,16 @@
         n_sub = weights.shape[0]
         (wu, wv, wt, ws, force, level_mean, side_cols, counts, wide_north, wide_south, wide_side,
          force_north, force_south, force_side) = call(
-            functools.partial(step_kernel, n_row), [hbm] * 4 + [vmem] * 5, [hbm] * 4 + [vmem] * 10,
+            functools.partial(step_kernel, n_row), [hbm] * 9, [hbm] * 14,
             [shape(TILES, LEV, STRIPS, SUB, LANES)] * 4 + [shape(2, ROWS, COLS)] * 2
-            + [shape(4, ROWS + 2 * SUB, LANES), shape(STRIPS, ROWS + 2 * SUB, LANES)]
+            + [shape(ROWS + 2 * SUB, LANES), shape(STRIPS, ROWS + 2 * SUB, LANES)]
             + [shape(4, REACH, COLS), shape(4, REACH, COLS), shape(4, EXT, LANES)]
             + [shape(2, REACH, COLS), shape(2, REACH, COLS), shape(2, EXT, LANES)],
-            [pltpu.VMEM((4, STRIPS, LEV + 1, PITCH, LANES), F32)] + [strip] * 2 + [pltpu.VMEM((4, LEV, ROWS + 2 * SUB, LANES), F32)] + [column] * 4
+            [pltpu.VMEM((4, STRIPS, LEV + 1, PITCH, LANES), F32)] + [strip] * 2 + [column] + [pltpu.VMEM((4, LEV, ROWS + 2 * SUB, LANES), F32)] + [column] * 4
             + [pltpu.VMEM((4, ROWS, LANES), F32)] * 2 + [pltpu.VMEM((2, ROWS, LANES), F32)]
-            + [dma((9,)), dma((20,)), dma((20,)), dma((4,))],
+            + [pltpu.VMEM((4, ROWS, COLS), F32), pltpu.VMEM((ROWS, COLS), jnp.int32)] + [pltpu.VMEM((2, ROWS, COLS), F32)] * 2
+            + [pltpu.VMEM((4, ROWS + 2 * SUB, LANES), F32), pltpu.VMEM((STRIPS, ROWS + 2 * SUB, LANES), F32), pltpu.VMEM((4, REACH, COLS), F32)]
+            + [dma((16,)), dma((20,)), dma((20,)), dma((8,))],
             collective_id=0, has_side_effects=True)(vel_u, vel_v, temp, salt, eta, tu, tv, depth, count)
         return call(
             functools.partial(fast_kernel, n_row, n_sub), [smem] + [hbm] * 4 + [vmem] * 14, [vmem] * 3 + [hbm] * 4,

time: 52.8 us -> 49.7 us (0.941)
  Pallas kernels: 51.9 us -> 49 us
    pallas_call x1, Pallas kernels: 32.4 us -> 29.4 us  [step(): call(functools.partial(step_kernel, n_row), [hbm] * 9, [hbm] * 14, [shape...]
where the time goes in v5:
time: 49.7 us; the launch traced here: 49.6 us
  Pallas kernels  49 us (99%)
  between operations  0.64 us (1%)
    pallas_call x1, Pallas kernels, step(): call(functools.partial(step_kernel, n_row), [hbm] * 9, [hbm] * 14, [shape...  29.4 us
    pallas_call x1, Pallas kernels, step(): call(functools.partial(fast_kernel, n_row, n_sub), [smem] + [hbm] * 4 + [...  19.5 us

profile of v5, /device:TPU:0, one launch (start us, length us, event | category | flops | bytes accessed | tf_op | source)
XLA Modules:
  0.0 49.6 jit_solution(14649473128468799758)
XLA Ops:
  0.6 29.4 %shard_map.153 = (f32[6,41,4,8,128]{4,3,2,1,0:T(8,128)}, f32[6,41,4,8,128]{4,3,2,1,0:T(8,128)}, f32[6,41,4,8,128]{4,3,2,1,0:T(8,128)}, f32[6,41,4,8,128]{4,3,2,1...) custom-call(f32[41,48,512]{2,1,0:T(8,128)} %u.1, ...), custom_call_target="tpu_custom_call" | custom-call | tf_op jit(solution)/shard_map/pallas_call | solution.py:702
  30.1 19.5 %shard_map.154 = (f32[48,512]{1,0:T(8,128)}, f32[48,512]{1,0:T(8,128)}, f32[48,512]{1,0:T(8,128)}, f32[41,48,512]{2,1,0:T(8,128)}, f32[41,48,512]{2,1,0:T(8,128)...) custom-call(f32[30]{0:T(128)} %weights.1, f32[6,41,4,8,128]{4,3,2,1,0:T(8,128)} %get-tuple-element.21.wu_in, ...), custom_call_target="tpu_custom_call" | custom-call | tf_op jit(solution)/shard_map/pallas_call | solution.py:714

commit v6 on v5

--- a/solution.py
+++ b/solution.py
@@ -31,7 +31,7 @@
 PAGE = EXT + 16
 MESH = pl.DeviceIdType.MESH
 F32 = jnp.float32
-VMEM_LIMIT = 62 * 1024 * 1024
+STEP_MIB, FAST_MIB = 35, 36
 
 
 def tables(strength):
@@ -124,12 +124,11 @@
         edges[f, k, rows, :] = pltpu.roll(packed[f, rows, :], LANES - 1 - 2 * k, 1)
 
 
-def step_kernel(n_row, u, v, t, s, eta, tu, tv, depth, count,
-                wu_out, wv_out, wt_out, ws_out, force_out, mean_out, side_out, counts_out,
+def step_kernel(n_row, u, v, t, s, flat_in,
+                wu, wv, wt, ws, force, level_mean, side_cols, counts,
                 wide_north, wide_south, wide_side, force_north, force_south, force_side,
-                cube, one_s, two_s, slope, edges, wu, wv, wt, ws, own_cols, fold, force_fold,
-                flat_in, count_in, force, level_mean, side_cols, counts, blank,
-                load_sem, send_sem, recv_sem, store_sem):
+                cube, one_s, two_s, edges, own_cols, fold, force_fold,
+                load_sem, send_sem, recv_sem):
     at = places(n_row)
     fields = (u, v, t, s)
     four = range(STRIPS)
@@ -138,25 +137,17 @@
         return pltpu.make_async_copy(fields[f].at[:, :, pl.ds(LANES * c, LANES)], cube.at[f, c, pl.ds(1, LEV), pl.ds(0, ROWS), :], sem)
 
     outer = [[load(f, c, load_sem.at[2 * f + e]) for e, c in enumerate((0, STRIPS - 1))] for f in four]
-    inner_sem, flat_sem, count_sem = load_sem.at[9], load_sem.at[10], load_sem.at[11]
-    fetch_count = pltpu.make_async_copy(count, count_in, count_sem)
-    fetch_count.start()
+    inner_sem = load_sem.at[9]
     for pair in outer:
         for copy in pair:
             copy.start()
-    for f in (2, 3, 0, 1):
-        for c in range(1, STRIPS - 1):
-            load(f, c, load_sem.at[8 + (f < 2)]).start()
-    for f, src in enumerate((eta, tu, tv, depth)):
-        pltpu.make_async_copy(src, flat_in.at[f], flat_sem).start()
     barrier = meet(at)
     lane = lane_index()
     at_first, at_last = lane == 0, lane == LANES - 1
     zero = jnp.zeros((SUB, LANES), F32)
     line = jnp.zeros((1, LANES), F32)
-    fetch_count.wait()
     for c in four:
-        counts[c, SUB:SUB + ROWS, :] = count_in[:, c * LANES:(c + 1) * LANES].astype(F32)
+        counts[c, SUB:SUB + ROWS, :] = flat_in[4, :, c * LANES:(c + 1) * LANES]
     await_meet(barrier, at)
     slot = iter(range(LANES))
 
@@ -212,6 +203,9 @@
     for f in four:
         for copy in outer[f]:
             copy.wait()
+        later = (f + 2) % 4
+        for c in range(1, STRIPS - 1):
+            load(later, c, load_sem.at[8 + (later < 2)]).start()
 
         def pack(tile, _):
             rows = pl.ds(pl.multiple_of(SUB * tile, SUB), SUB)
@@ -245,33 +239,20 @@
 
         lax.fori_loop(0, LEV, body, 0)
 
-    narrow = blank.at[:, :, pl.ds(0, LANES)]
-    pair = pl.ds(0, 2)
     low_rows, high_rows = pl.ds(0, REACH), pl.ds(ROWS - REACH, REACH)
     far_rows = pl.ds(REACH + ROWS, REACH)
 
-    def blanks(wide, forced, rows):
-        targets = ((blank, wide), (narrow, wide_side.at[:, rows, :]), (blank.at[pair], forced), (blank.at[pair, :, pl.ds(0, LANES)], force_side.at[:, rows, :]))
-        return [pltpu.make_async_copy(src, dst, load_sem.at[12 + i]) for i, (src, dst) in enumerate(targets)]
-
-    @pl.when(jnp.logical_not(at['has_north']))
-    def _():
-        clear(1, ROWS)
-        counts[:, SUB + ROWS:, :] = jnp.zeros((STRIPS, SUB, LANES), F32)
-        side_cols[:, SUB + ROWS:, :] = jnp.zeros((STRIPS, SUB, LANES), F32)
-        blank[...] = jnp.zeros_like(blank)
-        for copy in blanks(wide_north, force_north, far_rows):
-            copy.start()
-
-    @pl.when(jnp.logical_not(at['has_south']))
-    def _():
-        clear(0, PITCH - 1)
-        counts[:, :SUB, :] = jnp.zeros((STRIPS, SUB, LANES), F32)
-        side_cols[:, :SUB, :] = jnp.zeros((STRIPS, SUB, LANES), F32)
-        blank[...] = jnp.zeros_like(blank)
-        for copy in blanks(wide_south, force_south, low_rows):
-            copy.start()
-
+    def walled(level, row, tile, wide, forced, rows):
+        clear(level, row)
+        counts[:, pl.ds(tile, SUB), :] = jnp.zeros((STRIPS, SUB, LANES), F32)
+        side_cols[:, pl.ds(tile, SUB), :] = jnp.zeros((STRIPS, SUB, LANES), F32)
+        wide[...] = jnp.zeros_like(wide)
+        forced[...] = jnp.zeros_like(forced)
+        wide_side[:, rows, :] = jnp.zeros((STRIPS, REACH, LANES), F32)
+        force_side[:, rows, :] = jnp.zeros((2, REACH, LANES), F32)
+
+    pl.when(jnp.logical_not(at['has_north']))(lambda: walled(1, ROWS, SUB + ROWS, wide_north, force_north, far_rows))
+    pl.when(jnp.logical_not(at['has_south']))(lambda: walled(0, PITCH - 1, 0, wide_south, force_south, low_rows))
     half_scale = 0.5 * BC_GRAVITY / LEV
     scale = 0.5 * TIME_STEP
 
@@ -289,6 +270,8 @@
     first_lanes, last_lanes = stack == 0, stack == LANES - 1
     none = jnp.zeros((STRIPS, SUB, LANES), F32)
     interior(2, load_sem.at[8]).wait()
+
+    slope = wt
 
     def pressure(tile, _):
         acc = none
@@ -316,31 +299,36 @@
     unpack(side_cols, edges, 1, pl.ds(0, SUB))
     interior(0, inner_sem).wait()
     low_half = lax.broadcasted_iota(jnp.int32, (ROWS, LANES), 1) < LANES // 2
-    pltpu.make_async_copy(flat_in, flat_in, flat_sem).wait()
     for f in four:
         fold[f] = jnp.where(low_half, flat_in[f, :, :LANES], flat_in[f, :, COLS - LANES:])
-    arrive(rows_north, rows_south)
-    leave(rows_north, rows_south)
     side_low, side_high = wide_side.at[:, low_rows, :], wide_side.at[:, far_rows, :]
     side_mid = wide_side.at[:, pl.ds(REACH, ROWS), :]
-    wide_up = [plan('north', wide_south, (flat_in.at[:, high_rows, :], wide_south)),
+    wide_up = [plan('north', wide_south, (flat_in.at[pl.ds(0, 4), high_rows, :], wide_south)),
                plan('north_side', side_low, (fold.at[:, high_rows, :], side_low))]
-    wide_down = [plan('south', wide_north, (flat_in.at[:, low_rows, :], wide_north)),
+    wide_down = [plan('south', wide_north, (flat_in.at[pl.ds(0, 4), low_rows, :], wide_north)),
                  plan('south_side', side_high, (fold.at[:, low_rows, :], side_high))]
     wide_across = [plan('side', side_mid, (fold, side_mid))]
     start(wide_up, wide_down, wide_across)
     pivot, _ = tables(VISC_R)
-    acc = none
     for k in range(LEV):
-        spot = level_rows(TILES, k)
+        spot = level_rows(TILES - 1, k)
         uu = uf[:, spot, :]
-        bf[:, spot, :] = uu + west_stack(uu, edges[0, k, pl.ds(SUB + ROWS, SUB), :], last_lanes)
-        rho = density(sf[:, spot, :], tf[:, spot, :])
-        pf[:, spot, :] = acc + rho
-        acc = (acc + rho) + rho
+        bf[:, spot, :] = uu + west_stack(uu, edges[0, k, pl.ds(ROWS, SUB), :], last_lanes)
+
+    def border_rows():
+        arrive(rows_north, rows_south)
+        acc = none
+        for k in range(LEV):
+            spot = level_rows(TILES, k)
+            uu = uf[:, spot, :]
+            bf[:, spot, :] = uu + west_stack(uu, edges[0, k, pl.ds(SUB + ROWS, SUB), :], last_lanes)
+            rho = density(sf[:, spot, :], tf[:, spot, :])
+            pf[:, spot, :] = acc + rho
+            acc = (acc + rho) + rho
 
     def momentum(step, _):
-        tile = TILES - 1 - step
+        tile = (2 * TILES - 2 - step) % TILES
+        pl.when(step == TILES - 2)(border_rows)
         _, nu, nv = face_counts(counts, side_cols.at[0], tile)
         row_pos = (at['row'] * ROWS + SUB * tile + lax.broadcasted_iota(jnp.int32, (STRIPS, SUB, LANES), 1)).astype(F32)
         fu = 0.25 * (CORIO_F0 + CORIO_BETA * ((row_pos + 0.5) / (ROWS * n_row) - 0.5))
@@ -390,8 +378,6 @@
             force[1, out_rows, lanes] = (sum_dv * inv_v)[c]
             level_mean[0, out_rows, lanes] = (sum_su * inv_u)[c]
             level_mean[1, out_rows, lanes] = (sum_sv * inv_v)[c]
-        pltpu.make_async_copy(wu.at[tile], wu_out.at[tile], store_sem.at[0]).start()
-        pltpu.make_async_copy(wv.at[tile], wv_out.at[tile], store_sem.at[1]).start()
         return 0
 
     lax.fori_loop(0, TILES, momentum, 0)
@@ -406,11 +392,6 @@
                   plan('south_side', side_high, (force_fold.at[:, low_rows, :], side_high))]
     force_across = [plan('side', side_mid, (force_fold, side_mid))]
     start(force_up, force_down, force_across)
-    extras = [pltpu.make_async_copy(src, dst, store_sem.at[4 + i])
-              for i, (src, dst) in enumerate(((force, force_out), (level_mean, mean_out), (side_cols.at[0], side_out), (counts, counts_out)))]
-    for copy in extras:
-        copy.start()
-
     ftf, fsf = pf, bf
     pivot, final = tables(DIFF_R)
 
@@ -448,48 +429,25 @@
 
             xt = advance(tf, ftf, 2, xt, wt)
             xs = advance(sf, fsf, 3, xs, ws)
-        pltpu.make_async_copy(wt.at[tile], wt_out.at[tile], store_sem.at[2]).start()
-        pltpu.make_async_copy(ws.at[tile], ws_out.at[tile], store_sem.at[3]).start()
         return 0
 
     lax.fori_loop(0, TILES, tracers, 0)
-    for i, (src, dst) in enumerate(((wu, wu_out), (wv, wv_out), (wt, wt_out), (ws, ws_out))):
-        pltpu.make_async_copy(src, dst, store_sem.at[i]).wait()
-    for copy in extras:
-        copy.wait()
-    leave(count_north + corner_north, count_south + corner_south, sides)
+    leave(count_north + corner_north + rows_north, count_south + corner_south + rows_south, sides)
     for group in ((wide_up, wide_down, wide_across), (force_up, force_down, force_across)):
         arrive(*group)
         leave(*group)
 
-    @pl.when(jnp.logical_not(at['has_north']))
-    def _():
-        for copy in blanks(wide_north, force_north, far_rows):
-            copy.wait()
-
-    @pl.when(jnp.logical_not(at['has_south']))
-    def _():
-        for copy in blanks(wide_south, force_south, low_rows):
-            copy.wait()
-
-
-def fast_kernel(n_row, n_sub, weights, wu_in, wv_in, wt_in, ws_in, eta, tu, tv, depth, wide_north, wide_south, wide_side,
-                force, force_north, force_south, force_side, level_mean, counts, side_cols,
+
+def fast_kernel(n_row, n_sub, weights, flat_in, wu, wv, wt, ws, force, level_mean, side_cols, counts,
+                wide_north, wide_south, wide_side, force_north, force_south, force_side,
                 eta_out, tu_out, tv_out, u_out, v_out, t_out, s_out,
-                e_s, u_s, v_s, b_s, d_s, cu_s, cv_s, bu_s, bv_s, fu_s, fv_s, bar_u, bar_v, wu, wv, wt, ws, u_new, v_new, t_new, s_new, load_sem, store_sem):
+                flat_out, small_sem, e_s, u_s, v_s, b_s, d_s, cu_s, cv_s, bu_s, bv_s, fu_s, fv_s, bar_u, bar_v,
+                u_new, v_new, t_new, s_new, store_sem):
     row = lax.axis_index('row')
-    def fetch(tile):
-        return [pltpu.make_async_copy(src.at[tile], dst.at[tile], load_sem.at[i, tile])
-                for i, (src, dst) in enumerate(((wt_in, wt), (ws_in, ws), (wu_in, wu), (wv_in, wv)))]
-
     def put(tile, i, src, dst):
         rows = pl.ds(pl.multiple_of(SUB * tile, SUB), SUB)
         return pltpu.make_async_copy(src.at[:, rows, :], dst.at[:, rows, :], store_sem.at[i, tile])
 
-    for part in (slice(0, 2), slice(2, 4)):
-        for tile in range(TILES):
-            for copy in fetch(tile)[part]:
-                copy.start()
     lane = lane_index()
     at_first, at_last = lane == 0, lane == LANES - 1
     five = range(STRIPS + 1)
@@ -518,10 +476,10 @@
     for tile in range(EXT_TILES):
         for c in five:
             at = page(tile, c)
-            e_s[at, :] = gather(0, eta, wide_north, wide_south, wide_side, tile, c)
-            u_s[at, :] = dt_fast * gather(1, tu, wide_north, wide_south, wide_side, tile, c)
-            v_s[at, :] = dt_fast * gather(2, tv, wide_north, wide_south, wide_side, tile, c)
-            d_s[at, :] = gather(3, depth, wide_north, wide_south, wide_side, tile, c)
+            e_s[at, :] = gather(0, flat_in.at[0], wide_north, wide_south, wide_side, tile, c)
+            u_s[at, :] = dt_fast * gather(1, flat_in.at[1], wide_north, wide_south, wide_side, tile, c)
+            v_s[at, :] = dt_fast * gather(2, flat_in.at[2], wide_north, wide_south, wide_side, tile, c)
+            d_s[at, :] = gather(3, flat_in.at[3], wide_north, wide_south, wide_side, tile, c)
             bu_s[at, :] = gather(0, force.at[0], force_north, force_south, force_side, tile, c)
             bv_s[at, :] = gather(1, force.at[1], force_north, force_south, force_side, tile, c)
     for tile in range(EXT_TILES):
@@ -589,8 +547,6 @@
     inner, _ = tables(DIFF_R)
 
     def tracers(tile, _):
-        for copy in fetch(tile)[:2]:
-            copy.wait()
         mid = [counts[c, pl.ds(pl.multiple_of(SUB * tile + SUB, SUB), SUB), :] for c in four]
         out_rows = pl.ds(pl.multiple_of(SUB * tile, SUB), SUB)
         xt, xs = [zero] * STRIPS, [zero] * STRIPS
@@ -633,14 +589,16 @@
         for c in four:
             at = page(tile + REACH // SUB, c)
             rows, lanes = pl.ds(SUB * tile, SUB), pl.ds(LANES * c, LANES)
-            eta_out[rows, lanes] = e_s[at, :]
-            tu_out[rows, lanes] = u_s[at, :] * (1.0 / dt_fast)
-            tv_out[rows, lanes] = v_s[at, :] * (1.0 / dt_fast)
+            flat_out[0, rows, lanes] = e_s[at, :]
+            flat_out[1, rows, lanes] = u_s[at, :] * (1.0 / dt_fast)
+            flat_out[2, rows, lanes] = v_s[at, :] * (1.0 / dt_fast)
+
+    results = [pltpu.make_async_copy(flat_out.at[i], dst, small_sem.at[i]) for i, dst in enumerate((eta_out, tu_out, tv_out))]
+    for copy in results:
+        copy.start()
 
     def tile_step(tile, _):
-        for copy in fetch(tile)[2:]:
-            copy.wait()
-        _, nu, nv = face_counts(counts, side_cols, tile)
+        _, nu, nv = face_counts(counts, side_cols.at[0], tile)
         out_rows = pl.ds(pl.multiple_of(SUB * tile, SUB), SUB)
         add_u, add_v = [], []
         for c in four:
@@ -676,6 +634,8 @@
     for tile in range(TILES):
         for i, (src, dst) in enumerate(((u_new, u_out), (v_new, v_out), (t_new, t_out), (s_new, s_out))):
             put(tile, i, src, dst).wait()
+    for copy in results:
+        copy.wait()
 
 
 def solution(mesh):
@@ -686,38 +646,39 @@
     dma = pltpu.SemaphoreType.DMA
     strip = pltpu.VMEM((STRIPS, LEV + 1, PITCH, LANES), F32)
     whole = pltpu.VMEM((LEV, ROWS, COLS), F32)
-    column = pltpu.VMEM((TILES, LEV, STRIPS, SUB, LANES), F32)
     extended = pltpu.VMEM(((STRIPS + 1) * PAGE, LANES), F32)
 
     def shape(*dims):
         return jax.ShapeDtypeStruct(dims, F32)
 
-    def call(body, ins, outs, shapes, scratch, **params):
+    def call(limit, body, ins, outs, shapes, scratch, **params):
         return pl.pallas_call(body, out_shape=shapes, in_specs=ins, out_specs=outs, scratch_shapes=scratch,
-                              compiler_params=pltpu.CompilerParams(vmem_limit_bytes=VMEM_LIMIT, **params))
+                              compiler_params=pltpu.CompilerParams(vmem_limit_bytes=limit * 1024 * 1024, **params))
 
     def step(vel_u, vel_v, temp, salt, eta, tu, tv, depth, count, weights):
         n_sub = weights.shape[0]
-        (wu, wv, wt, ws, force, level_mean, side_cols, counts, wide_north, wide_south, wide_side,
-         force_north, force_south, force_side) = call(
-            functools.partial(step_kernel, n_row), [hbm] * 9, [hbm] * 14,
+        part = lax.broadcasted_iota(jnp.int32, (5, ROWS, COLS), 0)
+        flat_in = jnp.where(part == 4, count, part).astype(F32)
+        for f, field in enumerate((eta, tu, tv, depth)):
+            flat_in = jnp.where(part == f, field, flat_in)
+        kept = call(
+            STEP_MIB, functools.partial(step_kernel, n_row), [hbm] * 4 + [vmem], [vmem] * 14,
             [shape(TILES, LEV, STRIPS, SUB, LANES)] * 4 + [shape(2, ROWS, COLS)] * 2
-            + [shape(ROWS + 2 * SUB, LANES), shape(STRIPS, ROWS + 2 * SUB, LANES)]
+            + [shape(4, ROWS + 2 * SUB, LANES), shape(STRIPS, ROWS + 2 * SUB, LANES)]
             + [shape(4, REACH, COLS), shape(4, REACH, COLS), shape(4, EXT, LANES)]
             + [shape(2, REACH, COLS), shape(2, REACH, COLS), shape(2, EXT, LANES)],
-            [pltpu.VMEM((4, STRIPS, LEV + 1, PITCH, LANES), F32)] + [strip] * 2 + [column] + [pltpu.VMEM((4, LEV, ROWS + 2 * SUB, LANES), F32)] + [column] * 4
-            + [pltpu.VMEM((4, ROWS, LANES), F32)] * 2 + [pltpu.VMEM((2, ROWS, LANES), F32)]
-            + [pltpu.VMEM((4, ROWS, COLS), F32), pltpu.VMEM((ROWS, COLS), jnp.int32)] + [pltpu.VMEM((2, ROWS, COLS), F32)] * 2
-            + [pltpu.VMEM((4, ROWS + 2 * SUB, LANES), F32), pltpu.VMEM((STRIPS, ROWS + 2 * SUB, LANES), F32), pltpu.VMEM((4, REACH, COLS), F32)]
-            + [dma((16,)), dma((20,)), dma((20,)), dma((8,))],
-            collective_id=0, has_side_effects=True)(vel_u, vel_v, temp, salt, eta, tu, tv, depth, count)
+            [pltpu.VMEM((4, STRIPS, LEV + 1, PITCH, LANES), F32)] + [strip] * 2
+            + [pltpu.VMEM((4, LEV, ROWS + 2 * SUB, LANES), F32)] + [pltpu.VMEM((4, ROWS, LANES), F32)] * 2
+            + [pltpu.VMEM((2, ROWS, LANES), F32)]
+            + [dma((10,)), dma((20,)), dma((20,))],
+            collective_id=0, has_side_effects=True)(vel_u, vel_v, temp, salt, flat_in)
         return call(
-            functools.partial(fast_kernel, n_row, n_sub), [smem] + [hbm] * 4 + [vmem] * 14, [vmem] * 3 + [hbm] * 4,
+            FAST_MIB, functools.partial(fast_kernel, n_row, n_sub), [smem] + [vmem] * 15, [hbm] * 7,
             [shape(ROWS, COLS)] * 3 + [shape(LEV, ROWS, COLS)] * 4,
-            [extended] * 9 + [pltpu.VMEM((EXT, LANES), F32)] * 2 + [pltpu.VMEM((TILES, STRIPS, SUB, LANES), F32)] * 2
-            + [column] * 4 + [whole] * 4 + [dma((4, TILES)), dma((4, TILES))],
-        )(weights, wu, wv, wt, ws, eta, tu, tv, depth, wide_north, wide_south, wide_side,
-          force, force_north, force_south, force_side, level_mean, counts, side_cols)
+            [pltpu.VMEM((3, ROWS, COLS), F32), dma((3,))]
+            + [extended] * 9 + [pltpu.VMEM((EXT, LANES), F32)] * 2 + [pltpu.VMEM((TILES, STRIPS, SUB, LANES), F32)] * 2
+            + [whole] * 4 + [dma((4, TILES))],
+        )(weights, flat_in, *kept)
 
     cube = P(None, 'row', 'col')
     flat = P('row', 'col')

time: 49.7 us -> 48.2 us (0.970)
  Pallas kernels: 49 us -> 46 us
  other arithmetic: 0 us -> 1.31 us
    pallas_call x2, Pallas kernels: 49 us -> 46 us  [the longest x1 28.6 us: step(): call(STEP_MIB, functools.partial(step_kernel, n_row), [hbm] * 4 + [vmem],...]
    select_n x0 -> x1, other arithmetic: none -> 1.29 us  [step(): flat_in = jnp.where(part == f, field, flat_in)]
where the time goes in v6:
time: 48.2 us; the launch traced here: 48 us
  Pallas kernels  46 us (95%)
  other arithmetic  1.31 us (3%)
  between operations  0.68 us (1%)
    pallas_call x1, Pallas kernels, step(): call(STEP_MIB, functools.partial(step_kernel, n_row), [hbm] * 4 + [vmem],...  28.6 us
    pallas_call x1, Pallas kernels, step(): call(FAST_MIB, functools.partial(fast_kernel, n_row, n_sub), [smem] + [vm...  17.5 us
    select_n x1, other arithmetic, step(): flat_in = jnp.where(part == f, field, flat_in)  1.29 us

profile of v6, /device:TPU:0, one launch (start us, length us, event | category | flops | bytes accessed | tf_op | source)
XLA Modules:
  0.0 48.0 jit_solution(7950013040615552049)
XLA Ops:
  0.7 1.3 %select_select_fusion.flat_in = f32[5,48,512]{2,1,0:T(8,128)S(1)} fusion(s32[48,512]{1,0:T(8,128)} %param.18, f32[48,512]{1,0:T(8,128)} %param.14, f32[48,512]{1,0:T(8,128)} %param.15, f32[48,512]{1,0:T(8,128)} %param.16, f32[48,512]{1,0:T(8,128)} %param.17, pred[5]{0:T(512)(128)(4,1)S(1)} %get-tuple-element.35, pred[5]{0:T(512)(128)(4,1)S(1)} %get-tuple-element.36, ...), kind=kLoop, calls=%fused_computation | loop fusion | flops 737280 | bytes 983065 | tf_op jit(solution)/shard_map/jit(_where)/select_n | solution.py:663
  2.0 0.0 copy-start
  2.0 28.6 %shard_map.153 = (f32[6,41,4,8,128]{4,3,2,1,0:T(8,128)S(1)}, f32[6,41,4,8,128]{4,3,2,1,0:T(8,128)S(1)}, f32[6,41,4,8,128]{4,3,2,1,0:T(8,128)S(1)}, f32[6,41,4,8,...) custom-call(f32[41,48,512]{2,1,0:T(8,128)} %u.1, ...), custom_call_target="tpu_custom_call" | custom-call | tf_op jit(solution)/shard_map/pallas_call | solution.py:664
  30.6 0.0 copy-done
  30.6 17.5 %shard_map.154 = (f32[48,512]{1,0:T(8,128)}, f32[48,512]{1,0:T(8,128)}, f32[48,512]{1,0:T(8,128)}, f32[41,48,512]{2,1,0:T(8,128)}, f32[41,48,512]{2,1,0:T(8,128)...) custom-call(f32[30]{0:T(128)S(1)} %copy-done, f32[5,48,512]{2,1,0:T(8,128)S(1)} %select_select_fusion.flat_in, ...), custom_call_target="tpu_custom_call" | custom-call | tf_op jit(solution)/shard_map/pallas_call | solution.py:675
  (3 shorter events, 0.0 us)
Async XLA Ops:
  2.0 28.6 %copy-start = (f32[30]{0:T(128)S(1)}, f32[30]{0:T(128)}, u32[]{:S(2)}) copy-start(f32[30]{0:T(128)} %weights.1) | copy-start | bytes 364

commit v7 on v6

--- a/solution.py
+++ b/solution.py
@@ -207,7 +207,7 @@
         for c in range(1, STRIPS - 1):
             load(later, c, load_sem.at[8 + (later < 2)]).start()
 
-        def pack(tile, _):
+        def pack(tile):
             rows = pl.ds(pl.multiple_of(SUB * tile, SUB), SUB)
             packed = zero
             for k in range(LEV + 1 if f == 0 else LEV):
@@ -219,9 +219,13 @@
                 both = pltpu.roll(jnp.where(at_first, first, last), 2 * k + 1, 1)
                 packed = jnp.where(half_lane == k, both, packed)
             own_cols[f, rows, :] = packed
+
+        def pack_two(pair, _):
+            pack(2 * pair)
+            pack(2 * pair + 1)
             return 0
 
-        lax.fori_loop(0, TILES, pack, 0)
+        lax.fori_loop(0, TILES // 2, pack_two, 0)
         target = side_cols.at[f, pl.ds(SUB, ROWS), :]
         sides.append(plan('side', target, (own_cols.at[f], target)))
         begin(sides[-1:])
@@ -289,11 +293,12 @@
     for f in four:
         received(sides[f:f + 1])
 
-        def spread(tile, _):
-            unpack(side_cols, edges, f, pl.ds(pl.multiple_of(SUB * tile, SUB), SUB))
+        def spread(group, _):
+            for part in range(3):
+                unpack(side_cols, edges, f, pl.ds(pl.multiple_of(SUB * (3 * group + part + 1), SUB), SUB))
             return 0
 
-        lax.fori_loop(1, TILES + 1, spread, 0)
+        lax.fori_loop(0, TILES // 3, spread, 0)
     arrive(count_north + corner_north, count_south + corner_south)
     unpack(side_cols, edges, 0, pl.ds(SUB + ROWS, SUB))
     unpack(side_cols, edges, 1, pl.ds(0, SUB))

time: 48.2 us -> 47.2 us (0.979)
  Pallas kernels: 46 us -> 45.1 us
    pallas_call x1, Pallas kernels: 28.6 us -> 27.6 us  [step(): call(STEP_MIB, functools.partial(step_kernel, n_row), [hbm] * 4 + [vmem],...]
where the time goes in v7:
time: 47.2 us; the launch traced here: 47.1 us
  Pallas kernels  45.1 us (96%)
  other arithmetic  1.31 us (3%)
  between operations  0.68 us (1%)
    pallas_call x1, Pallas kernels, step(): call(STEP_MIB, functools.partial(step_kernel, n_row), [hbm] * 4 + [vmem],...  27.6 us
    pallas_call x1, Pallas kernels, step(): call(FAST_MIB, functools.partial(fast_kernel, n_row, n_sub), [smem] + [vm...  17.5 us
    select_n x1, other arithmetic, step(): flat_in = jnp.where(part == f, field, flat_in)  1.29 us

profile of v7, /device:TPU:0, one launch (start us, length us, event | category | flops | bytes accessed | tf_op | source)
XLA Modules:
  0.0 47.1 jit_solution(7765925154036162124)
XLA Ops:
  0.7 1.3 %select_select_fusion.flat_in = f32[5,48,512]{2,1,0:T(8,128)S(1)} fusion(s32[48,512]{1,0:T(8,128)} %param.18, f32[48,512]{1,0:T(8,128)} %param.14, f32[48,512]{1,0:T(8,128)} %param.15, f32[48,512]{1,0:T(8,128)} %param.16, f32[48,512]{1,0:T(8,128)} %param.17, pred[5]{0:T(512)(128)(4,1)S(1)} %get-tuple-element.35, pred[5]{0:T(512)(128)(4,1)S(1)} %get-tuple-element.36, ...), kind=kLoop, calls=%fused_computation | loop fusion | flops 737280 | bytes 983065 | tf_op jit(solution)/shard_map/jit(_where)/select_n | solution.py:668
  2.0 0.0 copy-start
  2.0 27.6 %shard_map.153 = (f32[6,41,4,8,128]{4,3,2,1,0:T(8,128)S(1)}, f32[6,41,4,8,128]{4,3,2,1,0:T(8,128)S(1)}, f32[6,41,4,8,128]{4,3,2,1,0:T(8,128)S(1)}, f32[6,41,4,8,...) custom-call(f32[41,48,512]{2,1,0:T(8,128)} %u.1, ...), custom_call_target="tpu_custom_call" | custom-call | tf_op jit(solution)/shard_map/pallas_call | solution.py:669
  29.6 0.0 copy-done
  29.6 17.5 %shard_map.154 = (f32[48,512]{1,0:T(8,128)}, f32[48,512]{1,0:T(8,128)}, f32[48,512]{1,0:T(8,128)}, f32[41,48,512]{2,1,0:T(8,128)}, f32[41,48,512]{2,1,0:T(8,128)...) custom-call(f32[30]{0:T(128)S(1)} %copy-done, f32[5,48,512]{2,1,0:T(8,128)S(1)} %select_select_fusion.flat_in, ...), custom_call_target="tpu_custom_call" | custom-call | tf_op jit(solution)/shard_map/pallas_call | solution.py:680
  (3 shorter events, 0.0 us)
Async XLA Ops:
  2.0 27.6 %copy-start = (f32[30]{0:T(128)S(1)}, f32[30]{0:T(128)}, u32[]{:S(2)}) copy-start(f32[30]{0:T(128)} %weights.1) | copy-start | bytes 364
